TPU v7x, 32 devices: a whole 2x2x4 slice. The times are simulated.
32 devices in a mesh: dp: 2 (over x), tp: 4 (over z), cp: 4 (over y, core).
Axes of the slice: x: 2, y: 2, z: 4, core: 2. Of those that a mesh axis runs over, the one named last changes fastest.
Arguments:
- x_suffix: bfloat16 [8192, 4096], P(('dp', 'cp')), parts along dimension 0
- k_prefix: bfloat16 [16384, 8, 128], P(('dp', 'cp'), 'tp'), parts along dimension 0
- v_prefix: bfloat16 [16384, 8, 128], P(('dp', 'cp'), 'tp'), parts along dimension 0
- norm_attn: bfloat16 [4096], replicated
- w_query: bfloat16 [4096, 4096], P(None, 'tp')
- w_key: bfloat16 [4096, 1024], P(None, 'tp')
- w_value: bfloat16 [4096, 1024], P(None, 'tp')
- w_out: bfloat16 [4096, 4096], P('tp')
- norm_mlp: bfloat16 [4096], replicated
- w_gate: bfloat16 [4096, 14336], P(None, 'tp')
- w_up: bfloat16 [4096, 14336], P(None, 'tp')
- w_down: bfloat16 [14336, 4096], P('tp')
Outputs:
- output 1: bfloat16 [8192, 4096], P(('dp', 'cp')), parts along dimension 0
- output 2: bfloat16 [8192, 8, 128], P(('dp', 'cp'), 'tp'), parts along dimension 0
- output 3: bfloat16 [8192, 8, 128], P(('dp', 'cp'), 'tp'), parts along dimension 0
There are 2 independent parts. A program takes and returns all parts, laid end to end along the dimension named above; an argument that names none is the same for every part.
All inputs are finite; a program needn't handle non-finite values.
Results may differ from a plain program's by a relative error of at most 0.0109479.
Values are sent between devices in bfloat16 or wider.
A program may use at most 1 GiB of HBM per device.

v0:
```python
import jax
import jax.numpy as jnp
from jax import lax
from jax.sharding import PartitionSpec as P

ROPE_THETA = 500000.0
NORM_EPS = 1e-5


def block_positions(owner, groups, blk_len, prefix_len):
    local_row = jnp.arange(2 * blk_len, dtype=jnp.int32)
    blk_idx = jnp.where(local_row < blk_len, owner, 2 * groups - 1 - owner)
    return prefix_len + blk_idx * blk_len + local_row % blk_len


def rope_tables(positions, head_dim):
    inv_freq = ROPE_THETA ** (-jnp.arange(0, head_dim, 2, dtype=jnp.float32) / head_dim)
    angles = positions.astype(jnp.float32)[:, None] * inv_freq[None, :]
    return jnp.cos(angles), jnp.sin(angles)


def apply_rope(values, cos_tab, sin_tab):
    half_dim = values.shape[-1] // 2
    first_half = values[..., :half_dim]
    second_half = values[..., half_dim:]
    cos_rows = cos_tab[:, None, :]
    sin_rows = sin_tab[:, None, :]
    return jnp.concatenate([first_half * cos_rows - second_half * sin_rows, second_half * cos_rows + first_half * sin_rows], axis=-1)


def rms_norm(values, gain_vec):
    vals32 = values.astype(jnp.float32)
    inv_rms = lax.rsqrt(jnp.mean(vals32 * vals32, axis=-1, keepdims=True) + NORM_EPS)
    return (vals32 * inv_rms * gain_vec.astype(jnp.float32)).astype(jnp.bfloat16)


def attend_step(acc_state, q_rot, k_blk, v_blk, q_pos, k_pos, score_scale):
    row_max, denom_sum, numer_sum = acc_state
    scores = jnp.einsum('sgrd,kgd->sgrk', q_rot, k_blk, preferred_element_type=jnp.float32) * score_scale
    visible = (k_pos[None, :] <= q_pos[:, None])[:, None, None, :]
    scores = jnp.where(visible, scores, -jnp.inf)
    new_max = jnp.maximum(row_max, jnp.max(scores, axis=-1))
    correction = jnp.exp(row_max - new_max)
    weights = jnp.exp(scores - new_max[..., None])
    denom_sum = denom_sum * correction + jnp.sum(weights, axis=-1)
    numer_sum = numer_sum * correction[..., None] + jnp.einsum('sgrk,kgd->sgrd', weights.astype(jnp.bfloat16), v_blk, preferred_element_type=jnp.float32)
    return new_max, denom_sum, numer_sum


def solution(mesh):
    groups = mesh.shape['cp']

    def local_layer(x_loc, kp_loc, vp_loc, norm_attn, w_query, w_key, w_value, w_out, norm_mlp, w_gate, w_up, w_down):
        rows_loc = x_loc.shape[0]
        blk_len = rows_loc // 2
        pre_dev, kv_loc, head_dim = kp_loc.shape
        heads_loc = w_query.shape[1] // head_dim
        group_ratio = heads_loc // kv_loc
        prefix_len = pre_dev * groups
        my_idx = lax.axis_index('cp')
        q_pos = block_positions(my_idx, groups, blk_len, prefix_len)
        cos_tab, sin_tab = rope_tables(q_pos, head_dim)
        hidden = rms_norm(x_loc, norm_attn)
        q_proj = jnp.dot(hidden, w_query, preferred_element_type=jnp.float32).reshape(rows_loc, heads_loc, head_dim)
        q_rot = apply_rope(q_proj, cos_tab, sin_tab).astype(jnp.bfloat16).reshape(rows_loc, kv_loc, group_ratio, head_dim)
        k_proj = jnp.dot(hidden, w_key, preferred_element_type=jnp.float32).reshape(rows_loc, kv_loc, head_dim)
        k_new = apply_rope(k_proj, cos_tab, sin_tab).astype(jnp.bfloat16)
        v_new = jnp.dot(hidden, w_value, preferred_element_type=jnp.float32).astype(jnp.bfloat16).reshape(rows_loc, kv_loc, head_dim)
        k_bundle = jnp.concatenate([kp_loc, k_new], axis=0)
        v_bundle = jnp.concatenate([vp_loc, v_new], axis=0)
        pre_offsets = jnp.arange(pre_dev, dtype=jnp.int32)

        def key_positions(src_idx):
            return jnp.concatenate([src_idx * pre_dev + pre_offsets, block_positions(src_idx, groups, blk_len, prefix_len)])

        score_scale = head_dim ** -0.5
        stat_shape = (rows_loc, kv_loc, group_ratio)
        init_state = (jnp.full(stat_shape, -jnp.inf, dtype=jnp.float32), jnp.zeros(stat_shape, jnp.float32), jnp.zeros(stat_shape + (head_dim,), jnp.float32))
        first_state = attend_step(init_state, q_rot, k_bundle, v_bundle, q_pos, key_positions(my_idx), score_scale)
        perm_pairs = [(dev_idx, (dev_idx + 1) % groups) for dev_idx in range(groups)]

        def step_body(step_idx, loop_state):
            k_cur, v_cur, acc_state = loop_state
            k_cur, v_cur = lax.ppermute((k_cur, v_cur), 'cp', perm_pairs)
            src_idx = (my_idx - step_idx) % groups
            acc_state = attend_step(acc_state, q_rot, k_cur, v_cur, q_pos, key_positions(src_idx), score_scale)
            return k_cur, v_cur, acc_state

        final_state = lax.fori_loop(1, groups, step_body, (k_bundle, v_bundle, first_state))[2]
        attn_heads = (final_state[2] / final_state[1][..., None]).astype(jnp.bfloat16).reshape(rows_loc, heads_loc * head_dim)
        resid_mid = x_loc.astype(jnp.float32) + lax.psum(jnp.dot(attn_heads, w_out, preferred_element_type=jnp.float32), 'tp')
        hidden_mlp = rms_norm(resid_mid, norm_mlp)
        gate_proj = jnp.dot(hidden_mlp, w_gate, preferred_element_type=jnp.float32)
        up_proj = jnp.dot(hidden_mlp, w_up, preferred_element_type=jnp.float32)
        act_mid = (jax.nn.silu(gate_proj) * up_proj).astype(jnp.bfloat16)
        x_out = (resid_mid + lax.psum(jnp.dot(act_mid, w_down, preferred_element_type=jnp.float32), 'tp')).astype(jnp.bfloat16)
        return x_out, k_new, v_new

    row_spec = P(('dp', 'cp'), None)
    kv_spec = P(('dp', 'cp'), 'tp', None)
    col_spec = P(None, 'tp')
    row_split = P('tp', None)
    vec_spec = P(None)
    return jax.shard_map(local_layer, mesh=mesh, in_specs=(row_spec, kv_spec, kv_spec, vec_spec, col_spec, col_spec, col_spec, row_split, vec_spec, col_spec, col_spec, row_split), out_specs=(row_spec, kv_spec, kv_spec), check_vma=False)
```

profile of v0, /device:TPU:0, one launch (start us, length us, event | category | flops | bytes accessed | tf_op | source)
XLA Modules:
  0.0 1885.1 jit_solution(9680544355459955889)
XLA Ops:
  11.1 5.2 fusion.27
  24.3 14.4 fusion.46
  45.0 4.7 pad_maximum_fusion
  55.5 37.3 %fusion.23 = (f32[1024,2,4]{0,2,1:T(4,128)}, f32[2,3072,1024,4]{2,1,3,0:T(8,128)}) fusion(pred[1024,3072]{0,1:T(8,128)(4,1)S(1)} %broadcast_compare_fusion.1, bf16[1024,2,4,128]{3,0,2,1:T(8,128)(2,1)} %pad_maximum_fusion, bf16[3072,2,128]{2,0,1:T(8,128)(2,1)} %maximum_maximum_fusion), kind=kOutput, calls=%fused_computation.32 | convolution fusion | flops 6517940224 | bytes 107511808 | tf_op jit(solution)/shard_map/sgrd,kgd->sgrk/dot_general | solution.py:39
  92.9 31.4 %fusion.22 = f32[1024,2,4]{0,2,1:T(4,128)S(1)} fusion(f32[2,3072,1024,4]{2,1,3,0:T(8,128)} %get-tuple-element.397, f32[1024,2,4]{0,2,1:T(4,128)} %get-tuple-element.470, pred[1024,3072]{0,1:T(8,128)(4,1)S(1)} %broadcast_compare_fusion.1), kind=kLoop, calls=%fused_computation.31 | loop fusion | flops 100655104 | bytes 103874560 | tf_op jit(solution)/shard_map/reduce_sum | solution.py:45
  125.0 7.4 convolution_convert_fusion
  138.8 39.3 %bitcast_add_fusion.1 = f32[1024,2,4,128]{0,3,2,1:T(8,128)} fusion(f32[2,3072,1024,4]{2,1,3,0:T(8,128)} %get-tuple-element.397, f32[1024,2,4]{0,2,1:T(4,128)} %get-tuple-element.470, pred[1024,3072]{0,1:T(8,128)(4,1)S(1)} %broadcast_compare_fusion.1, f32[1024,2,4]{0,2,1:T(4,128)S(1)} %get-tuple-element.392, bf16[1024,2,128]{0,2,1:T(8,128)(2,1)} %bitcast.115, ...), kind=kOutput, calls=%fused_computation.48 | convolution fusion | flops 6547308544 | bytes 109641728 | tf_op jit(solution)/shard_map/sgrk,kgd->sgrd/dot_general | solution.py:46
  178.1 5.5 copy.55
  185.1 405.1 %while.26 = (s32[]{:T(128)}, bf16[3072,2,128]{2,0,1:T(8,128)(2,1)}, bf16[3072,2,128]{2,0,1:T(8,128)(2,1)}, f32[1024,2,4]{0,2,1:T(4,128)}, f32[1024,2,4]{0,2,1:T(...) while((s32[]{:T(128)}, bf16[3072,2,128]{2,0,1:T(8,128)(2,1)}, ...), condition=%wide.region_6.7_spmd.clone.clone, body=%wide.region_3.6_spmd.clone.clone.sunk | while | flops 13167012864 | bytes 347660672 | solution.py:89
  190.7 15.4 collective-permute-done
  206.1 36.6 %fusion.84 = (f32[1024,2,4]{0,2,1:T(4,128)S(1)}, f32[2,3072,1024,4]{2,1,3,0:T(8,128)}) fusion(pred[1024,3072]{0,1:T(8,128)(4,1)S(1)} %broadcast_compare_fusion.3, bf16[1024,2,4,128]{3,0,2,1:T(8,128)(2,1)} %get-tuple-element.504, bf16[3072,2,128]{2,0,1:T(8,128)(2,1)} %collective-permute-done), kind=kOutput, calls=%fused_computation.6.clone.1 | convolution fusion | flops 6517940224 | bytes 107511808 | tf_op jit(solution)/shard_map/while/body/eval_jaxpr/sgrd,kgd->sgrk/dot_general | solution.py:39
  243.4 31.3 %fusion.85 = f32[1024,2,4]{0,2,1:T(4,128)S(1)} fusion(f32[2,3072,1024,4]{2,1,3,0:T(8,128)} %get-tuple-element.464, f32[1024,2,4]{0,2,1:T(4,128)S(1)} %max.14, pred[1024,3072]{0,1:T(8,128)(4,1)S(1)} %broadcast_compare_fusion.3), kind=kLoop, calls=%fused_computation.5.clone.1 | loop fusion | flops 100655104 | bytes 103874560 | tf_op jit(solution)/shard_map/while/body/eval_jaxpr/reduce_sum | solution.py:45
  281.4 39.5 %bitcast_add_fusion.3 = f32[1024,2,4,128]{3,0,2,1:T(8,128)} fusion(f32[1024,2,4,128]{3,0,2,1:T(8,128)} %get-tuple-element.487, f32[2,3072,1024,4]{2,1,3,0:T(8,128)} %get-tuple-element.464, f32[1024,2,4]{0,2,1:T(4,128)S(1)} %max.14, pred[1024,3072]{0,1:T(8,128)(4,1)S(1)} %broadcast_compare_fusion.3, f32[1024,2,4]{0,2,1:T(4,128)S(1)} %bitcast.120, ...), kind=kOutput, calls=%fused_computation.10.clone.1 | convolution fusion | flops 6545211392 | bytes 113836032 | tf_op jit(solution)/shard_map/while/body/eval_jaxpr/sgrk,kgd->sgrd/dot_general | solution.py:46
  325.4 15.4 collective-permute-done
  340.8 36.6 %fusion.84 = (f32[1024,2,4]{0,2,1:T(4,128)S(1)}, f32[2,3072,1024,4]{2,1,3,0:T(8,128)}) fusion(pred[1024,3072]{0,1:T(8,128)(4,1)S(1)} %broadcast_compare_fusion.3, bf16[1024,2,4,128]{3,0,2,1:T(8,128)(2,1)} %get-tuple-element.504, bf16[3072,2,128]{2,0,1:T(8,128)(2,1)} %collective-permute-done), kind=kOutput, calls=%fused_computation.6.clone.1 | convolution fusion | flops 6517940224 | bytes 107511808 | tf_op jit(solution)/shard_map/while/body/eval_jaxpr/sgrd,kgd->sgrk/dot_general | solution.py:39
  378.1 31.3 %fusion.85 = f32[1024,2,4]{0,2,1:T(4,128)S(1)} fusion(f32[2,3072,1024,4]{2,1,3,0:T(8,128)} %get-tuple-element.464, f32[1024,2,4]{0,2,1:T(4,128)S(1)} %max.14, pred[1024,3072]{0,1:T(8,128)(4,1)S(1)} %broadcast_compare_fusion.3), kind=kLoop, calls=%fused_computation.5.clone.1 | loop fusion | flops 100655104 | bytes 103874560 | tf_op jit(solution)/shard_map/while/body/eval_jaxpr/reduce_sum | solution.py:45
  416.1 39.5 %bitcast_add_fusion.3 = f32[1024,2,4,128]{3,0,2,1:T(8,128)} fusion(f32[1024,2,4,128]{3,0,2,1:T(8,128)} %get-tuple-element.487, f32[2,3072,1024,4]{2,1,3,0:T(8,128)} %get-tuple-element.464, f32[1024,2,4]{0,2,1:T(4,128)S(1)} %max.14, pred[1024,3072]{0,1:T(8,128)(4,1)S(1)} %broadcast_compare_fusion.3, f32[1024,2,4]{0,2,1:T(4,128)S(1)} %bitcast.120, ...), kind=kOutput, calls=%fused_computation.10.clone.1 | convolution fusion | flops 6545211392 | bytes 113836032 | tf_op jit(solution)/shard_map/while/body/eval_jaxpr/sgrk,kgd->sgrd/dot_general | solution.py:46
  460.1 15.4 collective-permute-done
  475.4 36.6 %fusion.84 = (f32[1024,2,4]{0,2,1:T(4,128)S(1)}, f32[2,3072,1024,4]{2,1,3,0:T(8,128)}) fusion(pred[1024,3072]{0,1:T(8,128)(4,1)S(1)} %broadcast_compare_fusion.3, bf16[1024,2,4,128]{3,0,2,1:T(8,128)(2,1)} %get-tuple-element.504, bf16[3072,2,128]{2,0,1:T(8,128)(2,1)} %collective-permute-done), kind=kOutput, calls=%fused_computation.6.clone.1 | convolution fusion | flops 6517940224 | bytes 107511808 | tf_op jit(solution)/shard_map/while/body/eval_jaxpr/sgrd,kgd->sgrk/dot_general | solution.py:39
  512.8 31.3 %fusion.85 = f32[1024,2,4]{0,2,1:T(4,128)S(1)} fusion(f32[2,3072,1024,4]{2,1,3,0:T(8,128)} %get-tuple-element.464, f32[1024,2,4]{0,2,1:T(4,128)S(1)} %max.14, pred[1024,3072]{0,1:T(8,128)(4,1)S(1)} %broadcast_compare_fusion.3), kind=kLoop, calls=%fused_computation.5.clone.1 | loop fusion | flops 100655104 | bytes 103874560 | tf_op jit(solution)/shard_map/while/body/eval_jaxpr/reduce_sum | solution.py:45
  550.7 39.5 %bitcast_add_fusion.3 = f32[1024,2,4,128]{3,0,2,1:T(8,128)} fusion(f32[1024,2,4,128]{3,0,2,1:T(8,128)} %get-tuple-element.487, f32[2,3072,1024,4]{2,1,3,0:T(8,128)} %get-tuple-element.464, f32[1024,2,4]{0,2,1:T(4,128)S(1)} %max.14, pred[1024,3072]{0,1:T(8,128)(4,1)S(1)} %broadcast_compare_fusion.3, f32[1024,2,4]{0,2,1:T(4,128)S(1)} %bitcast.120, ...), kind=kOutput, calls=%fused_computation.10.clone.1 | convolution fusion | flops 6545211392 | bytes 113836032 | tf_op jit(solution)/shard_map/while/body/eval_jaxpr/sgrk,kgd->sgrd/dot_general | solution.py:46
  590.2 5.3 copy.56
  598.4 14.7 fusion.52
  613.8 561.1 %all-reduce.3.cloned.1.call-done = f32[1024,4096]{1,0:T(8,128)} async-done(((f32[1024,4096]{1,0:T(8,128)}), f32[1024,4096]{1,0:T(8,128)}) %all-reduce.3.cloned.1.call-update) | async-done | bytes 16777232 | tf_op jit(solution)/shard_map/psum | solution.py:91
  1174.8 9.3 multiply_reduce_fusion
  1184.1 3.7 copy-done.2
  1187.8 6.2 multiply_convert_fusion
  1194.0 35.2 %fusion.53 = f32[1024,3584]{1,0:T(8,128)} fusion(bf16[1024,4096]{1,0:T(8,128)(2,1)S(1)} %multiply_convert_fusion, bf16[4096,3584]{1,0:T(8,128)(2,1)} %param.23), kind=kOutput, calls=%fused_computation.86 | convolution fusion | flops 30064771072 | bytes 52428800 | tf_op jit(solution)/shard_map/dot_general | solution.py:93
  1229.2 36.2 %multiply_convert_fusion.1.clone.4 = bf16[1024,3584]{1,0:T(8,128)(2,1)S(1)} fusion(f32[1024,3584]{1,0:T(8,128)} %fusion.53, bf16[1024,4096]{1,0:T(8,128)(2,1)S(1)} %multiply_convert_fusion, bf16[4096,3584]{1,0:T(8,128)(2,1)} %param.24), kind=kOutput, calls=%fused_computation.44.clone.clone.clone.1 | convolution fusion | flops 30086791168 | bytes 59768832 | tf_op jit(solution)/shard_map/dot_general | solution.py:94
  1265.4 36.2 %fusion.30 = f32[1024,4096]{1,0:T(8,128)} fusion(bf16[3584,4096]{1,0:T(8,128)(2,1)} %param.25, bf16[1024,3584]{1,0:T(8,128)(2,1)S(1)} %multiply_convert_fusion.1.clone.4), kind=kOutput, calls=%fused_computation.45 | convolution fusion | flops 30064771072 | bytes 53477376 | tf_op jit(solution)/shard_map/dot_general | solution.py:96
  1305.4 554.9 %all-reduce.5.cloned.1.call-done = f32[1024,4096]{1,0:T(8,128)} async-done(((f32[1024,4096]{1,0:T(8,128)}), f32[1024,4096]{1,0:T(8,128)}) %all-reduce.5.cloned.1.call-update) | async-done | bytes 16777232 | tf_op jit(solution)/shard_map/psum | solution.py:96
  1860.3 17.8 add_convert_fusion
  (94 shorter events, 76.4 us)
Async XLA Ops:
  7.2 9.2 copy-start
  7.2 1167.7 %all-reduce.3.cloned.1.call-start = ((), (), s32[]{:S(2)}) async-start(), calls=%async_computation | async-start | bytes 33554432 | tf_op jit(solution)/shard_map/psum | solution.py:91
  10.3 6.1 copy-start.3
  51.9 0.8 copy-start.5
  51.9 1.0 copy-start.7
  178.1 5.5 copy-start.4
  185.5 20.6 %collective-permute-start = (bf16[3072,2,128]{2,0,1:T(8,128)(2,1)}, bf16[3072,2,128]{2,0,1:T(8,128)(2,1)}, u32[]{:S(2)}, u32[]{:S(2)}) collective-permute-start(bf16[3072,2,128]{2,0,1:T(8,128)(2,1)} %get-tuple-element.483), channel_id=1, source_target_pairs={{0,1},{1,2},{2,3},{3,0},{4,5},{5,6},{6,7},{7,4},{8,9},{9,10},{10,1... | collective-permute-start | bytes 4718600 | tf_op jit(solution)/shard_map/while/body/eval_jaxpr/ppermute | solution.py:84
  186.1 92.7 %collective-permute-start.1 = (bf16[3072,2,128]{2,0,1:T(8,128)(2,1)}, bf16[3072,2,128]{2,0,1:T(8,128)(2,1)}, u32[]{:S(2)}, u32[]{:S(2)}) collective-permute-start(bf16[3072,2,128]{2,0,1:T(8,128)(2,1)} %get-tuple-element.484), channel_id=1, source_target_pairs={{0,1},{1,2},{2,3},{3,0},{4,5},{5,6},{6,7},{7,4},{8,9},{9,10},{10,1... | collective-permute-start | bytes 4718600 | tf_op jit(solution)/shard_map/while/body/eval_jaxpr/ppermute | solution.py:84
  320.9 19.8 %collective-permute-start = (bf16[3072,2,128]{2,0,1:T(8,128)(2,1)}, bf16[3072,2,128]{2,0,1:T(8,128)(2,1)}, u32[]{:S(2)}, u32[]{:S(2)}) collective-permute-start(bf16[3072,2,128]{2,0,1:T(8,128)(2,1)} %get-tuple-element.483), channel_id=1, source_target_pairs={{0,1},{1,2},{2,3},{3,0},{4,5},{5,6},{6,7},{7,4},{8,9},{9,10},{10,1... | collective-permute-start | bytes 4718600 | tf_op jit(solution)/shard_map/while/body/eval_jaxpr/ppermute | solution.py:84
  320.9 92.5 %collective-permute-start.1 = (bf16[3072,2,128]{2,0,1:T(8,128)(2,1)}, bf16[3072,2,128]{2,0,1:T(8,128)(2,1)}, u32[]{:S(2)}, u32[]{:S(2)}) collective-permute-start(bf16[3072,2,128]{2,0,1:T(8,128)(2,1)} %get-tuple-element.484), channel_id=1, source_target_pairs={{0,1},{1,2},{2,3},{3,0},{4,5},{5,6},{6,7},{7,4},{8,9},{9,10},{10,1... | collective-permute-start | bytes 4718600 | tf_op jit(solution)/shard_map/while/body/eval_jaxpr/ppermute | solution.py:84
  455.6 19.8 %collective-permute-start = (bf16[3072,2,128]{2,0,1:T(8,128)(2,1)}, bf16[3072,2,128]{2,0,1:T(8,128)(2,1)}, u32[]{:S(2)}, u32[]{:S(2)}) collective-permute-start(bf16[3072,2,128]{2,0,1:T(8,128)(2,1)} %get-tuple-element.483), channel_id=1, source_target_pairs={{0,1},{1,2},{2,3},{3,0},{4,5},{5,6},{6,7},{7,4},{8,9},{9,10},{10,1... | collective-permute-start | bytes 4718600 | tf_op jit(solution)/shard_map/while/body/eval_jaxpr/ppermute | solution.py:84
  455.6 92.5 %collective-permute-start.1 = (bf16[3072,2,128]{2,0,1:T(8,128)(2,1)}, bf16[3072,2,128]{2,0,1:T(8,128)(2,1)}, u32[]{:S(2)}, u32[]{:S(2)}) collective-permute-start(bf16[3072,2,128]{2,0,1:T(8,128)(2,1)} %get-tuple-element.484), channel_id=1, source_target_pairs={{0,1},{1,2},{2,3},{3,0},{4,5},{5,6},{6,7},{7,4},{8,9},{9,10},{10,1... | collective-permute-start | bytes 4718600 | tf_op jit(solution)/shard_map/while/body/eval_jaxpr/ppermute | solution.py:84
  613.1 0.7 copy-start.10
  613.1 1247.2 %all-reduce.5.cloned.1.call-start = ((), (), s32[]{:S(2)}) async-start(), calls=%async_computation.1 | async-start | bytes 33554432 | tf_op jit(solution)/shard_map/psum | solution.py:96
  1174.8 13.0 copy-start.2
  1301.6 1.0 copy-start.9
  1301.6 2.1 copy-start.6
  1301.6 2.1 copy-start.8
  1860.3 17.8 copy-start.1
Sparse Core Ops, SparseCore 0:
  613.2 561.5 all-reduce.2
  1301.8 558.4 all-reduce.4
where the time goes:
time: 1890 us
  waiting for transfers between devices  1160 us (61%)
  matrix products  452 us (24%)
  other arithmetic  195 us (10%)
  local copies, waits for them, and re-layouts  53.2 us (3%)
    psum x1, waiting for transfers between devices, local_layer(): lax.psum(jnp.dot(attn_heads, w_out, preferred_element_type=jnp.float32),...  561 us
    psum x1, waiting for transfers between devices, local_layer(): lax.psum(jnp.dot(act_mid, w_down, preferred_element_type=jnp.float32), 'tp')  555 us
    dot_general x4, matrix products, attend_step(): jnp.einsum('sgrk,kgd->sgrd', weights.astype(jnp.bfloat16), v_blk, preferr...  158 us
    dot_general x4, matrix products, attend_step(): jnp.einsum('sgrd,kgd->sgrk', q_rot, k_blk, preferred_element_type=jnp.flo...  147 us
    reduce_sum x4, other arithmetic, attend_step(): denom_sum = denom_sum * correction + jnp.sum(weights, axis=-1)  125 us
    ppermute x6, waiting for transfers between devices, step_body(): k_cur, v_cur = lax.ppermute((k_cur, v_cur), 'cp', perm_pairs)  46.1 us
  transfers between devices with their start and end apart: 8, of which 5 were waited for; matrix products, arithmetic and copies ran while one was open for 12% of the time, Pallas kernels for 0%

commit v1 on v0

v1 whole, which is shorter than its diff:
```python
import functools
import math

import jax
import jax.numpy as jnp
from jax import lax
from jax.experimental import pallas as pl
from jax.experimental.pallas import tpu as pltpu
from jax.sharding import PartitionSpec as P

ROPE_THETA = 500000.0
NORM_EPS = 1e-5
F32 = jnp.float32
BF16 = jnp.bfloat16
ANY = pl.BlockSpec(memory_space=pl.ANY)
VMEM = pl.BlockSpec(memory_space=pltpu.VMEM)
NT = (((1,), (1,)), ((), ()))


def block_positions(owner, groups, blk_len, prefix_len):
    local_row = jnp.arange(2 * blk_len, dtype=jnp.int32)
    blk_idx = jnp.where(local_row < blk_len, owner, 2 * groups - 1 - owner)
    return prefix_len + blk_idx * blk_len + local_row % blk_len


def rope_tables(positions, head_dim):
    inv_freq = ROPE_THETA ** (-jnp.arange(0, head_dim, 2, dtype=F32) / head_dim)
    angles = positions.astype(F32)[:, None] * inv_freq[None, :]
    cos_tab, sin_tab = jnp.cos(angles), jnp.sin(angles)
    return jnp.concatenate([cos_tab, cos_tab], axis=1), jnp.concatenate([-sin_tab, sin_tab], axis=1)


def qkv_kernel(x_ref, g_ref, wq_ref, wk_ref, wv_ref, cos_ref, sin_ref, q_ref, k_ref, vt_ref, kf_ref, vf_ref, h_ref, *, nq):
    step = pl.program_id(0)
    rows = x_ref.shape[0]
    rt = 128

    @pl.when(step == 0)
    def _():
        @pl.loop(0, rows // rt)
        def _(i):
            sl = pl.ds(pl.multiple_of(i * rt, rt), rt)
            xv = x_ref[sl, :].astype(F32)
            inv = lax.rsqrt(jnp.mean(xv * xv, axis=-1, keepdims=True) + NORM_EPS)
            h_ref[sl, :] = (xv * inv * g_ref[...].astype(F32)).astype(BF16)

    def rope(block, sl):
        return (block * cos_ref[sl, :] + pltpu.roll(block, 64, axis=1) * sin_ref[sl, :]).astype(BF16)

    mt = 512

    def project(w_ref, store):
        @pl.loop(0, rows // mt)
        def _(i):
            sl = pl.ds(pl.multiple_of(i * mt, mt), mt)
            acc = jnp.dot(h_ref[sl, :], w_ref[...], preferred_element_type=F32)
            store(acc, sl)

    def store_q(acc, sl):
        for t in range(2):
            cs = slice(t * 128, (t + 1) * 128)
            q_ref[sl, cs] = rope(acc[:, cs], sl)

    def store_k(acc, sl):
        for t in range(2):
            cs = slice(t * 128, (t + 1) * 128)
            kv = rope(acc[:, cs], sl)
            k_ref[t, sl, :] = kv
            kf_ref[sl, cs] = kv

    def store_v(acc, sl):
        vf_ref[sl, :] = acc.astype(BF16)
        for t in range(2):
            vt_ref[t, :, sl] = acc[:, t * 128:(t + 1) * 128].T.astype(BF16)

    pl.when(step < nq)(lambda: project(wq_ref, store_q))
    pl.when(step == nq)(lambda: project(wk_ref, store_k))
    pl.when(step == nq + 1)(lambda: project(wv_ref, store_v))


def qkv(x, gain, wq, wk, wv, cos_tab, sin_tab):
    rows, depth = x.shape
    nq = wq.shape[1] // 256
    whole = lambda shape: pl.BlockSpec(shape, lambda j: (0,) * len(shape), pipeline_mode=pl.Buffered(1))
    return pl.pallas_call(
        functools.partial(qkv_kernel, nq=nq),
        grid=(nq + 2,),
        in_specs=[
            whole((rows, depth)), whole((1, depth)),
            pl.BlockSpec((depth, 256), lambda j: (0, jnp.minimum(j, nq - 1))),
            pl.BlockSpec((depth, 256), lambda j: (0, 0)),
            pl.BlockSpec((depth, 256), lambda j: (0, 0)),
            whole((rows, 128)), whole((rows, 128)),
        ],
        out_specs=[
            pl.BlockSpec((rows, 256), lambda j: (0, jnp.minimum(j, nq - 1))),
            pl.BlockSpec((2, rows, 128), lambda j: (0, 0, 0)),
            pl.BlockSpec((2, 128, rows), lambda j: (0, 0, 0)),
            pl.BlockSpec((rows, 256), lambda j: (0, 0)),
            pl.BlockSpec((rows, 256), lambda j: (0, 0)),
        ],
        out_shape=[
            jax.ShapeDtypeStruct((rows, nq * 256), BF16),
            jax.ShapeDtypeStruct((2, rows, 128), BF16),
            jax.ShapeDtypeStruct((2, 128, rows), BF16),
            jax.ShapeDtypeStruct((rows, 256), BF16),
            jax.ShapeDtypeStruct((rows, 256), BF16),
        ],
        scratch_shapes=[pltpu.VMEM((rows, depth), BF16)],
        compiler_params=pltpu.CompilerParams(dimension_semantics=("arbitrary",), vmem_limit_bytes=56 * 2**20),
        cost_estimate=pl.CostEstimate(flops=2 * rows * depth * (nq + 2) * 256, bytes_accessed=2 * depth * (rows + 1536), transcendentals=0),
        name="qkv",
    )(x, gain.reshape(1, depth), wq, wk, wv, cos_tab, sin_tab)


NQ = 512


def fetch_pieces(refs, bufs, sems, start):
    for i, (kr, vr) in enumerate(refs):
        n = kr.shape[1]
        for j, (src, dst) in enumerate(((kr, bufs[0].at[:, pl.ds(i * n, n), :]), (vr, bufs[1].at[:, :, pl.ds(i * n, n)]))):
            copy = pltpu.make_async_copy(src, dst, sems.at[i, j])
            copy.start() if start else copy.wait()


def q_block(q_ref, head, half):
    return q_ref[pl.ds(pl.multiple_of(half * NQ, NQ), NQ), pl.ds(pl.multiple_of(head * 128, 128), 128)]


def attend_items(q_ref, kb_ref, vb_ref, acc_ref, m_ref, l_ref, pbufs, n_items, item, bk, c2, diag):
    depth = len(pbufs)

    def scores(i, pb):
        head, half, start = item(i)
        n = head * 2 + half
        ks = kb_ref[head // 4, pl.ds(pl.multiple_of(start, bk), bk), :]
        s = lax.dot_general(ks, q_block(q_ref, head, half), NT, preferred_element_type=F32)
        e = jnp.exp2(s * c2 - m_ref[n])
        if diag:
            seen = lax.broadcasted_iota(jnp.int32, (bk, NQ), 0) <= lax.broadcasted_iota(jnp.int32, (bk, NQ), 1)
            e = jnp.where(seen, e, 0.0)
        pb[...] = e.astype(BF16)
        l_ref[n] += jnp.sum(e.reshape(bk // 8, 8, NQ), axis=0)

    def values(i, pb):
        head, half, start = item(i)
        vt = vb_ref[head // 4, :, pl.ds(pl.multiple_of(start, bk), bk)]
        acc_ref[head * 2 + half] += jnp.dot(vt, pb[...], preferred_element_type=F32)

    scores(0, pbufs[0])

    def body(g, carry):
        for u in range(depth):
            i = g * depth + u
            scores(i + 1, pbufs[(u + 1) % depth])
            values(i, pbufs[u])
        return carry

    trips = n_items // depth - 1
    lax.fori_loop(0, trips, body, 0)
    for u in range(depth):
        if u + 1 < depth:
            scores(trips * depth + u + 1, pbufs[u + 1])
        values(trips * depth + u, pbufs[u])


def prefix_kernel(*refs, first, heads, c2):
    refs = list(refs)
    q_ref, ka, va, kb, vb = refs[:5]
    refs = refs[5:]
    state_in = None
    if not first:
        state_in, refs = refs[:3], refs[3:]
    acc_ref, m_ref, l_ref, kbuf, vbuf, pa, pb, ksem, ssem = refs
    pieces = ((ka, va), (kb, vb))
    fetch_pieces(pieces, (kbuf, vbuf), ksem, True)
    copies = []
    if not first:
        copies = [pltpu.make_async_copy(src, dst, ssem.at[i]) for i, (src, dst) in enumerate(zip(state_in, (acc_ref, m_ref, l_ref)))]
        for copy in copies:
            copy.start()
    fetch_pieces(pieces, (kbuf, vbuf), ksem, False)
    for copy in copies:
        copy.wait()
    if first:
        @pl.loop(0, heads * 2)
        def _(n):
            head, half = n // 2, n % 2
            s = lax.dot_general(kbuf[head // 4, 0:128, :], q_block(q_ref, head, half), NT, preferred_element_type=F32)
            m_ref[n] = jnp.max(s, axis=0, keepdims=True) * c2
            acc_ref[n] = jnp.zeros((128, NQ), F32)
            l_ref[n] = jnp.zeros((8, NQ), F32)
    bk = 1024
    per = kbuf.shape[1] // bk

    def item(i):
        n = i // per
        return n // 2, n % 2, (i % per) * bk

    attend_items(q_ref, kbuf, vbuf, acc_ref, m_ref, l_ref, (pa, pb), heads * 2 * per, item, bk, c2, False)


def state_shapes(heads):
    return [
        jax.ShapeDtypeStruct((heads * 2, 128, NQ), F32),
        jax.ShapeDtypeStruct((heads * 2, 1, NQ), F32),
        jax.ShapeDtypeStruct((heads * 2, 8, NQ), F32),
    ]


def attend_prefix(q, pieces, state, c2):
    heads = q.shape[1] // 128
    n = pieces[0][0].shape[1]
    first = state is None
    flops = 4 * q.shape[0] * heads * 128 * 2 * n
    return pl.pallas_call(
        functools.partial(prefix_kernel, first=first, heads=heads, c2=c2),
        in_specs=[VMEM] + [ANY] * (4 if first else 7),
        out_specs=[VMEM] * 3,
        out_shape=state_shapes(heads),
        scratch_shapes=[
            pltpu.VMEM((2, 2 * n, 128), BF16), pltpu.VMEM((2, 128, 2 * n), BF16),
            pltpu.VMEM((1024, NQ), BF16), pltpu.VMEM((1024, NQ), BF16),
            pltpu.SemaphoreType.DMA((2, 2)), pltpu.SemaphoreType.DMA((3,)),
        ],
        compiler_params=pltpu.CompilerParams(vmem_limit_bytes=40 * 2**20),
        cost_estimate=pl.CostEstimate(flops=flops, bytes_accessed=8 * n * 256 + 8 * q.size, transcendentals=0),
        name="attend_prefix",
    )(q, *pieces[0], *pieces[1], *(() if first else state))


def suffix_kernel(*refs, heads, groups, c2, axis):
    refs = list(refs)
    q_ref = refs[0]
    pre = [(refs[1 + 2 * i], refs[2 + 2 * i]) for i in range(groups)]
    suf = [(refs[1 + 2 * groups + 2 * i], refs[2 + 2 * groups + 2 * i]) for i in range(groups)]
    state_in = refs[1 + 4 * groups:4 + 4 * groups]
    o_ref, kbuf, vbuf, acc_ref, m_ref, l_ref, bad_ref, ksem, ssem, *pbufs = refs[4 + 4 * groups:]
    me = lax.axis_index(axis)
    fetch_pieces(suf, (kbuf, vbuf), ksem, True)
    copies = [pltpu.make_async_copy(src, dst, ssem.at[i]) for i, (src, dst) in enumerate(zip(state_in, (acc_ref, m_ref, l_ref)))]
    for copy in copies:
        copy.start()
    fetch_pieces(suf, (kbuf, vbuf), ksem, False)
    for copy in copies:
        copy.wait()
    bk = NQ
    last = 2 * groups - 1

    def locate(blk):
        late = (blk >= groups).astype(jnp.int32)
        owner = jnp.where(blk < groups, blk, last - blk)
        diff = (owner % 2 != me % 2).astype(jnp.int32) + 2 * (owner // 2 != me // 2).astype(jnp.int32)
        return (diff * 2 + late) * bk

    def full_item(i):
        head, r = i // last, i % last
        half = (r >= me).astype(jnp.int32)
        blk = jnp.where(r < me, r, r - me)
        return head, half, locate(blk)

    def diag_item(i):
        half = i % 2
        return i // 2, half, locate(jnp.where(half == 0, me, last - me))

    attend_items(q_ref, kbuf, vbuf, acc_ref, m_ref, l_ref, pbufs[:4], heads * last, full_item, bk, c2, False)
    attend_items(q_ref, kbuf, vbuf, acc_ref, m_ref, l_ref, pbufs[:2], heads * 2, diag_item, bk, c2, True)

    bad_ref[...] = jnp.zeros_like(bad_ref)

    def write(n, acc, total):
        head, half = n // 2, n % 2
        out = (acc * (1.0 / total)).T.astype(BF16)
        o_ref[pl.ds(pl.multiple_of(half * NQ, NQ), NQ), pl.ds(pl.multiple_of(head * 128, 128), 128)] = out

    @pl.loop(0, heads * 2)
    def _(n):
        acc = acc_ref[n]
        total = jnp.sum(l_ref[n], axis=0, keepdims=True)
        fine = (jnp.abs(acc) < jnp.inf) & (total < jnp.inf)
        bad = jnp.where(fine, 0.0, 1.0)
        for j in range(NQ // 128):
            bad_ref[...] = jnp.maximum(bad_ref[...], jnp.max(bad[:, j * 128:(j + 1) * 128].reshape(16, 8, 128), axis=0))
        write(n, acc, total)

    @pl.when(jnp.max(bad_ref[...]) > 0.0)
    def _():
        n_pre = pre[0][0].shape[1]

        @pl.loop(0, heads * 2)
        def _(n):
            head, half = n // 2, n % 2
            q = q_block(q_ref, head, half)
            m_ref[n] = jnp.full((1, NQ), -jnp.inf, F32)
            l_ref[n] = jnp.zeros((8, NQ), F32)
            acc_ref[n] = jnp.zeros((128, NQ), F32)

            def update(ks, vt, seen):
                s = lax.dot_general(ks, q, NT, preferred_element_type=F32) * c2
                if seen is not None:
                    s = jnp.where(seen, s, -jnp.inf)
                m_old = m_ref[n]
                m_new = jnp.maximum(m_old, jnp.max(s, axis=0, keepdims=True))
                alpha = jnp.exp2(m_old - m_new)
                e = jnp.exp2(s - m_new)
                m_ref[n] = m_new
                l_ref[n] = l_ref[n] * alpha + jnp.sum(e.reshape(bk // 8, 8, NQ), axis=0)
                acc_ref[n] = acc_ref[n] * alpha + jnp.dot(vt, e.astype(BF16), preferred_element_type=F32)

            kpre, vpre = pbufs[0].at[:, 0:128], pbufs[1].at[0:128, :]
            for kr, vr in pre:
                @pl.loop(0, n_pre // bk)
                def _(j):
                    sl = pl.ds(pl.multiple_of(j * bk, bk), bk)
                    c0 = pltpu.make_async_copy(kr.at[head // 4, sl, :], kpre, ksem.at[0, 0])
                    c1 = pltpu.make_async_copy(vr.at[head // 4, :, sl], vpre, ksem.at[0, 1])
                    c0.start()
                    c1.start()
                    c0.wait()
                    c1.wait()
                    update(kpre[...], vpre[...], None)

            mine = jnp.where(half == 0, me, last - me)

            @pl.loop(0, 2 * groups)
            def _(blk):
                @pl.when(blk <= mine)
                def _():
                    start = pl.multiple_of(locate(blk), bk)
                    seen = (lax.broadcasted_iota(jnp.int32, (bk, NQ), 0) <= lax.broadcasted_iota(jnp.int32, (bk, NQ), 1)) | (blk < mine)
                    update(kbuf[head // 4, pl.ds(start, bk), :], vbuf[head // 4, :, pl.ds(start, bk)], seen)

            write(n, acc_ref[n], jnp.sum(l_ref[n], axis=0, keepdims=True))


def attend_suffix(q, pre, suf, state, c2, axis):
    rows = q.shape[0]
    heads, groups = q.shape[1] // 128, len(suf)
    n = suf[0][0].shape[1]
    flat = [a for p in list(pre) + list(suf) for a in p]
    st = state_shapes(heads)
    return pl.pallas_call(
        functools.partial(suffix_kernel, heads=heads, groups=groups, c2=c2, axis=axis),
        in_specs=[VMEM] + [ANY] * (len(flat) + 3),
        out_specs=VMEM,
        out_shape=jax.ShapeDtypeStruct(q.shape, BF16),
        scratch_shapes=[
            pltpu.VMEM((2, groups * n, 128), BF16), pltpu.VMEM((2, 128, groups * n), BF16),
            *(pltpu.VMEM(s.shape, F32) for s in st), pltpu.VMEM((8, 128), F32),
            pltpu.SemaphoreType.DMA((groups, 2)), pltpu.SemaphoreType.DMA((3,)),
            *(pltpu.VMEM((NQ, NQ), BF16) for _ in range(4)),
        ],
        compiler_params=pltpu.CompilerParams(vmem_limit_bytes=40 * 2**20),
        cost_estimate=pl.CostEstimate(flops=4 * heads * 128 * NQ * NQ * (2 * groups + 1), bytes_accessed=8 * n * 512, transcendentals=0),
        name="attend_suffix",
    )(q, *flat, *state)


def swap(arrays, axis, groups, bit):
    return tuple(lax.ppermute(a, axis, [(i, i ^ bit) for i in range(groups)]) for a in arrays)


def attend(q, own_pre, near_pre, far_pre, own_suf, near_suf, far_suf, c2, axis, groups):
    state = attend_prefix(q, (own_pre, near_pre), None, c2)
    far_pre, state = lax.optimization_barrier((far_pre, state))
    cross_pre = swap(far_pre, axis, groups, 1)
    state = attend_prefix(q, (far_pre, cross_pre), state, c2)
    far_suf, state = lax.optimization_barrier((far_suf, state))
    cross_suf = swap(far_suf, axis, groups, 1)
    return attend_suffix(q, (own_pre, near_pre, far_pre, cross_pre), (own_suf, near_suf, far_suf, cross_suf), state, c2, axis)


def solution(mesh):
    groups = mesh.shape['cp']
    tps = mesh.shape['tp']

    def local_layer(x_loc, kp_loc, vp_loc, norm_attn, w_query, w_key, w_value, w_out, norm_mlp, w_gate, w_up, w_down):
        rows = x_loc.shape[0]
        pre_dev, kv_loc, head_dim = kp_loc.shape
        c2 = head_dim ** -0.5 * math.log2(math.e)
        me = lax.axis_index('cp')
        z = lax.axis_index('tp')
        q_pos = block_positions(me, groups, rows // 2, pre_dev * groups)
        cos_tab, sin_tab = rope_tables(q_pos, head_dim)
        own_pre = (kp_loc.transpose(1, 0, 2), vp_loc.transpose(1, 2, 0))
        far_pre, near_pre = swap(own_pre, 'cp', groups, 2), swap(own_pre, 'cp', groups, 1)
        q, k_new, vt_new, k_flat, v_flat = qkv(x_loc, norm_attn, w_query, w_key, w_value, cos_tab, sin_tab)
        own_suf = (k_new, vt_new)
        far_suf, near_suf = swap(own_suf, 'cp', groups, 2), swap(own_suf, 'cp', groups, 1)
        o = attend(q, own_pre, near_pre, far_pre, own_suf, near_suf, far_suf, c2, 'cp', groups)

        n_chunks = 2
        ch = rows // n_chunks
        own = ch // tps
        outs = []
        for c in range(n_chunks):
            part = jnp.dot(o[c * ch:(c + 1) * ch], w_out, preferred_element_type=F32)
            y = lax.psum_scatter(part, 'tp', scatter_dimension=0, tiled=True)
            y = y + lax.dynamic_slice_in_dim(x_loc, c * ch + z * own, own, 0).astype(F32)
            inv = lax.rsqrt(jnp.mean(y * y, axis=-1, keepdims=True) + NORM_EPS)
            h2 = (y * inv * norm_mlp.astype(F32)).astype(BF16)
            h2 = lax.all_gather(h2, 'tp', axis=0, tiled=True)
            gate = jnp.dot(h2, w_gate, preferred_element_type=F32)
            up = jnp.dot(h2, w_up, preferred_element_type=F32)
            act = (jax.nn.silu(gate) * up).astype(BF16)
            part = jnp.dot(act, w_down, preferred_element_type=F32)
            fin = lax.psum_scatter(part, 'tp', scatter_dimension=0, tiled=True)
            outs.append(lax.all_gather((y + fin).astype(BF16), 'tp', axis=0, tiled=True))
        x_out = jnp.concatenate(outs, axis=0)
        return x_out, k_flat.reshape(rows, kv_loc, head_dim), v_flat.reshape(rows, kv_loc, head_dim)

    row_spec = P(('dp', 'cp'), None)
    kv_spec = P(('dp', 'cp'), 'tp', None)
    col_spec = P(None, 'tp')
    row_split = P('tp', None)
    vec_spec = P(None)
    return jax.shard_map(local_layer, mesh=mesh, in_specs=(row_spec, kv_spec, kv_spec, vec_spec, col_spec, col_spec, col_spec, row_split, vec_spec, col_spec, col_spec, row_split), out_specs=(row_spec, kv_spec, kv_spec), check_vma=False)
```

time: 1890 us -> 1120 us (0.59)
  waiting for transfers between devices: 1160 us -> 753 us
  matrix products: 452 us -> 163 us
  other arithmetic: 195 us -> 24.3 us
  Pallas kernels: 0 us -> 140 us
  local copies, waits for them, and re-layouts: 53.2 us -> 14 us
    psum x2 -> x0, waiting for transfers between devices: 1120 us -> none  [the longest x1 561 us: local_layer(): lax.psum(jnp.dot(attn_heads, w_out, preferred_element_type=jnp.float32),...]
    reduce_scatter x0 -> x4, waiting for transfers between devices: none -> 501 us  [the longest x2 280 us: local_layer(): y = lax.psum_scatter(part, 'tp', scatter_dimension=0, tiled=True)]
    dot_general x15 -> x8, matrix products: 452 us -> 163 us  [the longest x2 49 us: local_layer(): up = jnp.dot(h2, w_up, preferred_element_type=F32)]
    all_gather x0 -> x4, waiting for transfers between devices: none -> 247 us  [the longest x2 159 us: local_layer(): lax.all_gather((y + fin).astype(BF16), 'tp', axis=0, tiled=True)]
    pallas_call x0 -> x4, Pallas kernels: none -> 140 us  [the longest x2 82.2 us: attend_prefix(): pl.pallas_call(functools.partial(prefix_kernel, first=first, heads=heads,...]
    reduce_sum x6 -> x1, other arithmetic: 140 us -> 3.63 us  [local_layer(): inv = lax.rsqrt(jnp.mean(y * y, axis=-1, keepdims=True) + NORM_EPS)]
    ppermute x6 -> x12, waiting for transfers between devices: 46.1 us -> 3.6 us  [swap(): lax.ppermute(a, axis, [(i, i ^ bit) for i in range(groups)])]
    while x10 -> x0, local copies, waits for them, and re-layouts: 23.1 us -> none
  transfers between devices with their start and end apart: 8 -> 20, of which waited for: 5 -> 12; matrix products, arithmetic and copies ran while one was open for 12% -> 15% of each run, Pallas kernels for 0% -> 10%
where the time goes in v1:
time: 1120 us
  waiting for transfers between devices  753 us (67%)
  matrix products  163 us (15%)
  Pallas kernels  140 us (12%)
  other arithmetic  24.3 us (2%)
  between operations  14.6 us (1%)
  local copies, waits for them, and re-layouts  14 us (1%)
    reduce_scatter x2, waiting for transfers between devices, local_layer(): y = lax.psum_scatter(part, 'tp', scatter_dimension=0, tiled=True)  280 us
    reduce_scatter x2, waiting for transfers between devices, local_layer(): fin = lax.psum_scatter(part, 'tp', scatter_dimension=0, tiled=True)  220 us
    all_gather x2, waiting for transfers between devices, local_layer(): lax.all_gather((y + fin).astype(BF16), 'tp', axis=0, tiled=True)  159 us
    all_gather x2, waiting for transfers between devices, local_layer(): h2 = lax.all_gather(h2, 'tp', axis=0, tiled=True)  87.9 us
    pallas_call x2, Pallas kernels, attend_prefix(): pl.pallas_call(functools.partial(prefix_kernel, first=first, heads=heads,...  82.2 us
    dot_general x2, matrix products, local_layer(): up = jnp.dot(h2, w_up, preferred_element_type=F32)  49 us
    dot_general x2, matrix products, local_layer(): gate = jnp.dot(h2, w_gate, preferred_element_type=F32)  47.9 us
    dot_general x2, matrix products, local_layer(): part = jnp.dot(act, w_down, preferred_element_type=F32)  47.8 us
  transfers between devices with their start and end apart: 20, of which 12 were waited for; matrix products, arithmetic and copies ran while one was open for 15% of the time, Pallas kernels for 10%

profile of v1, /device:TPU:0, one launch (start us, length us, event | category | flops | bytes accessed | tf_op | source)
XLA Modules:
  0.0 1115.6 jit_solution(10412398544949417788)
XLA Ops:
  9.2 2.6 collective-permute-start.2
  11.8 2.4 copy.16
  15.4 1.9 fusion.8
  18.6 28.3 %qkv.1 = (bf16[1024,1024]{1,0:T(8,128)(2,1)}, bf16[2,1024,128]{2,1,0:T(8,128)(2,1)}, bf16[2,128,1024]{2,1,0:T(8,128)(2,1)}, bf16[1024,256]{1,0:T(8,128)(2,1)}, bf16[1024,256]{1,0:T(8,128)(2,1)}) custom-call(bf16[1024,4096]{1,0:T(8,128)(2,1)} %x_ref.1, bf16[1,4096]{1,0:T(2,128)(2,1)} %reshape.55.g_ref, bf16[4096,1024]{1,0:T(8,128)(2,1)} %wq_ref.1, ...), custom_call_target="tpu_custom_call" | custom-call | flops 12884901888 | bytes 20971520 | tf_op jit(solution)/shard_map/qkv/pallas_call | solution.py:85
  46.9 1.6 copy-done.3
  48.5 42.2 %attend_prefix.2 = (f32[16,128,512]{2,1,0:T(8,128)S(1)}, f32[16,1,512]{2,1,0:T(1,128)S(1)}, f32[16,8,512]{2,1,0:T(8,128)S(1)}) custom-call(bf16[1024,1024]{1,0:T(8,128)(2,1)S(1)} %copy-done.3, bf16[2,2048,128]{2,1,0:T(8,128)(2,1)S(1)} %bitcast.29, bf16[2,128,2048]{2,1,0:T(8,128)(2,1)S(1)} %bitcast.33, ...), custom_call_target="tpu_custom_call" | custom-call | flops 17179869184 | bytes 12582912 | tf_op jit(solution)/shard_map/attend_prefix/pallas_call | solution.py:217
  90.7 2.0 copy-done.5
  93.2 1.7 collective-permute-start.8
  96.9 40.0 %attend_prefix.3 = (f32[16,128,512]{2,1,0:T(8,128)S(1)}, f32[16,1,512]{2,1,0:T(1,128)S(1)}, f32[16,8,512]{2,1,0:T(8,128)S(1)}) custom-call(bf16[1024,1024]{1,0:T(8,128)(2,1)S(1)} %copy-done.4, bf16[2,2048,128]{2,1,0:T(8,128)(2,1)} %collective-permute-done.2.refs_1_.refs_5_, bf16[2,128,2048]{2,1,0:T(8,128)(2,1)} %collective-permute-done.3.refs_2_.refs_6_, ...), custom_call_target="tpu_custom_call" | custom-call | flops 17179869184 | bytes 12582912 | tf_op jit(solution)/shard_map/attend_prefix/pallas_call | solution.py:217
  136.9 2.0 copy-done.2
  141.7 29.3 %attend_suffix.1 = bf16[1024,1024]{1,0:T(8,128)(2,1)} custom-call(bf16[1024,1024]{1,0:T(8,128)(2,1)} %get-tuple-element.24.refs_0_, bf16[2,2048,128]{2,1,0:T(8,128)(2,1)S(1)} %bitcast.30, bf16[2,128,2048]{2,1,0:T(8,128)(2,1)S(1)} %bitcast.34, bf16[2,2048,128]{2,1,0:T(8,128)(2,1)S(1)} %collective-permute-done.refs_3_, ...), custom_call_target="tpu_custom_call" | custom-call | flops 9663676416 | bytes 4194304 | tf_op jit(solution)/shard_map/attend_suffix/pallas_call | solution.py:343
  171.0 7.9 fusion.6
  179.0 1.5 copy-done.13
  180.5 10.1 fusion.4
  191.3 133.4 %reduce-scatter.5.cloned.1.call-done = f32[128,4096]{1,0:T(8,128)} async-done(((f32[512,4096]{1,0:T(8,128)}), f32[128,4096]{1,0:T(8,128)}) %reduce-scatter.5.cloned.1.call-update) | async-done | bytes 2097168 | tf_op jit(solution)/shard_map/reduce_scatter | solution.py:399
  324.7 147.1 %reduce-scatter.9.cloned.1.call-done = f32[128,4096]{1,0:T(8,128)} async-done(((f32[512,4096]{1,0:T(8,128)}), f32[128,4096]{1,0:T(8,128)}) %reduce-scatter.9.cloned.1.call-update) | async-done | bytes 2097168 | tf_op jit(solution)/shard_map/reduce_scatter | solution.py:399
  471.8 3.6 multiply_reduce_fusion.1
  475.5 3.7 multiply_convert_fusion.3
  479.8 80.2 %all-gather.9.cloned.1.call-done = bf16[512,4096]{1,0:T(8,128)(2,1)} async-done(((bf16[128,4096]{1,0:T(8,128)(2,1)}), bf16[512,4096]{1,0:T(8,128)(2,1)}) %all-gather.9.cloned.1.call-update) | async-done | bytes 4194320 | tf_op jit(solution)/shard_map/all_gather | solution.py:403
  560.0 24.2 %fusion.17 = f32[512,3584]{1,0:T(8,128)} fusion(bf16[512,4096]{1,0:T(8,128)(2,1)} %all-gather.9.cloned.1.call-done, bf16[4096,3584]{1,0:T(8,128)(2,1)} %param.21), kind=kOutput, calls=%fused_computation.39 | convolution fusion | flops 15032385536 | bytes 40894464 | tf_op jit(solution)/shard_map/dot_general | solution.py:404
  584.2 24.5 %multiply_convert_fusion.clone.4 = bf16[512,3584]{1,0:T(8,128)(2,1)} fusion(f32[512,3584]{1,0:T(8,128)} %fusion.17, bf16[512,4096]{1,0:T(8,128)(2,1)} %all-gather.9.cloned.1.call-done, bf16[4096,3584]{1,0:T(8,128)(2,1)} %param.22), kind=kOutput, calls=%fused_computation.1.clone.clone.clone.1 | convolution fusion | flops 15043395584 | bytes 44564480 | tf_op jit(solution)/shard_map/dot_general | solution.py:405
  608.6 23.9 %fusion = f32[512,4096]{1,0:T(8,128)} fusion(bf16[3584,4096]{1,0:T(8,128)(2,1)} %param.23, bf16[512,3584]{1,0:T(8,128)(2,1)} %multiply_convert_fusion.clone.4), kind=kOutput, calls=%fused_computation.3 | convolution fusion | flops 15032385536 | bytes 41418752 | tf_op jit(solution)/shard_map/dot_general | solution.py:407
  632.6 7.7 all-gather.5.cloned.1.call-done
  640.3 23.7 %fusion.16 = f32[512,3584]{1,0:T(8,128)} fusion(bf16[512,4096]{1,0:T(8,128)(2,1)} %all-gather.5.cloned.1.call-done, bf16[4096,3584]{1,0:T(8,128)(2,1)} %param.21), kind=kOutput, calls=%fused_computation.38 | convolution fusion | flops 15032385536 | bytes 40894464 | tf_op jit(solution)/shard_map/dot_general | solution.py:404
  664.0 24.5 %multiply_convert_fusion.1.clone.2 = bf16[512,3584]{1,0:T(8,128)(2,1)} fusion(f32[512,3584]{1,0:T(8,128)} %fusion.16, bf16[512,4096]{1,0:T(8,128)(2,1)} %all-gather.5.cloned.1.call-done, bf16[4096,3584]{1,0:T(8,128)(2,1)} %param.22), kind=kOutput, calls=%fused_computation.2.clone.clone.clone | convolution fusion | flops 15043395584 | bytes 44564480 | tf_op jit(solution)/shard_map/dot_general | solution.py:405
  688.5 23.9 %fusion.1 = f32[512,4096]{1,0:T(8,128)} fusion(bf16[3584,4096]{1,0:T(8,128)(2,1)} %param.23, bf16[512,3584]{1,0:T(8,128)(2,1)} %multiply_convert_fusion.1.clone.2), kind=kOutput, calls=%fused_computation.4 | convolution fusion | flops 15032385536 | bytes 41418752 | tf_op jit(solution)/shard_map/dot_general | solution.py:407
  712.5 72.9 %reduce-scatter.11.cloned.1.call-done = f32[128,4096]{1,0:T(8,128)} async-done(((f32[512,4096]{1,0:T(8,128)}), f32[128,4096]{1,0:T(8,128)}) %reduce-scatter.11.cloned.1.call-update) | async-done | bytes 2097168 | tf_op jit(solution)/shard_map/reduce_scatter | solution.py:408
  785.4 147.5 %reduce-scatter.7.cloned.1.call-done = f32[128,4096]{1,0:T(8,128)} async-done(((f32[512,4096]{1,0:T(8,128)}), f32[128,4096]{1,0:T(8,128)}) %reduce-scatter.7.cloned.1.call-update) | async-done | bytes 2097168 | tf_op jit(solution)/shard_map/reduce_scatter | solution.py:408
  932.9 5.7 add_convert_fusion.1
  941.3 78.2 %all-gather.11.cloned.1.call-done = bf16[512,4096]{1,0:T(8,128)(2,1)} async-done(((bf16[128,4096]{1,0:T(8,128)(2,1)}), bf16[512,4096]{1,0:T(8,128)(2,1)}) %all-gather.11.cloned.1.call-update) | async-done | bytes 4194320 | tf_op jit(solution)/shard_map/all_gather | solution.py:409
  1019.5 81.1 %all-gather.7.cloned.1.call-done = bf16[512,4096]{1,0:T(8,128)(2,1)} async-done(((bf16[128,4096]{1,0:T(8,128)(2,1)}), bf16[512,4096]{1,0:T(8,128)(2,1)}) %all-gather.7.cloned.1.call-update) | async-done | bytes 4194320 | tf_op jit(solution)/shard_map/all_gather | solution.py:409
  1100.6 8.0 pad_maximum_fusion
  (77 shorter events, 13.7 us)
Async XLA Ops:
  7.2 7.6 copy-start.11
  7.2 317.6 %reduce-scatter.5.cloned.1.call-start = ((), (), s32[]{:S(2)}) async-start(), calls=%async_computation.4 | async-start | bytes 10485760 | tf_op jit(solution)/shard_map/reduce_scatter | solution.py:399
  8.6 38.3 %collective-permute-start = (bf16[2,2048,128]{2,1,0:T(8,128)(2,1)S(1)}, bf16[2,2048,128]{2,1,0:T(8,128)(2,1)S(1)}, u32[]{:S(2)}, u32[]{:S(2)}) collective-permute-start(bf16[2,2048,128]{2,1,0:T(8,128)(2,1)S(1)} %bitcast.27), channel_id=1, source_target_pairs={{0,1},{1,0},{2,3},{3,2},{4,5},{5,4},{6,7},{7,6},{8,9},{9,8},{10,11... | collective-permute-start | bytes 3145736 | tf_op jit(solution)/shard_map/ppermute | solution.py:361
  9.2 83.5 %collective-permute-start.2 = (bf16[2,2048,128]{2,1,0:T(8,128)(2,1)S(1)}, bf16[2,2048,128]{2,1,0:T(8,128)(2,1)}, u32[]{:S(2)}, u32[]{:S(2)}) collective-permute-start(bf16[2,2048,128]{2,1,0:T(8,128)(2,1)S(1)} %bitcast.28), channel_id=1, source_target_pairs={{0,2},{1,3},{2,0},{3,1},{4,6},{5,7},{6,4},{7,5},{8,10},{9,11},{10,... | collective-permute-start | bytes 3145736 | tf_op jit(solution)/shard_map/ppermute | solution.py:361
  14.2 32.7 %collective-permute-start.1 = (bf16[2,128,2048]{2,1,0:T(8,128)(2,1)S(1)}, bf16[2,128,2048]{2,1,0:T(8,128)(2,1)}, u32[]{:S(2)}, u32[]{:S(2)}) collective-permute-start(bf16[2,128,2048]{2,1,0:T(8,128)(2,1)S(1)} %bitcast.31), channel_id=1, source_target_pairs={{0,1},{1,0},{2,3},{3,2},{4,5},{5,4},{6,7},{7,6},{8,9},{9,8},{10,11... | collective-permute-start | bytes 3145736 | tf_op jit(solution)/shard_map/ppermute | solution.py:361
  14.4 78.3 %collective-permute-start.3 = (bf16[2,128,2048]{2,1,0:T(8,128)(2,1)S(1)}, bf16[2,128,2048]{2,1,0:T(8,128)(2,1)}, u32[]{:S(2)}, u32[]{:S(2)}) collective-permute-start(bf16[2,128,2048]{2,1,0:T(8,128)(2,1)S(1)} %bitcast.32), channel_id=1, source_target_pairs={{0,2},{1,3},{2,0},{3,1},{4,6},{5,7},{6,4},{7,5},{8,10},{9,11},{10,... | collective-permute-start | bytes 3145736 | tf_op jit(solution)/shard_map/ppermute | solution.py:361
  48.5 44.7 %copy-start = (bf16[2,1024,128]{2,1,0:T(8,128)(2,1)S(1)}, bf16[2,1024,128]{2,1,0:T(8,128)(2,1)}, u32[]{:S(2)}) copy-start(bf16[2,1024,128]{2,1,0:T(8,128)(2,1)} %get-tuple-element.30.refs_9_) | copy-start | bytes 1572868
  48.5 46.5 %copy-start.1 = (bf16[2,128,1024]{2,1,0:T(8,128)(2,1)S(1)}, bf16[2,128,1024]{2,1,0:T(8,128)(2,1)}, u32[]{:S(2)}) copy-start(bf16[2,128,1024]{2,1,0:T(8,128)(2,1)} %get-tuple-element.31.refs_10_) | copy-start | bytes 1572868
  48.5 48.4 %copy-start.4 = (bf16[1024,1024]{1,0:T(8,128)(2,1)S(1)}, bf16[1024,1024]{1,0:T(8,128)(2,1)}, u32[]{:S(2)}) copy-start(bf16[1024,1024]{1,0:T(8,128)(2,1)} %get-tuple-element.24.refs_0_) | copy-start | bytes 6291460
  90.7 2.0 copy-start.5
  92.7 2.7 collective-permute-start.4
  92.8 4.1 collective-permute-start.5
  93.2 45.7 %collective-permute-start.8 = (bf16[2,1024,128]{2,1,0:T(8,128)(2,1)S(1)}, bf16[2,1024,128]{2,1,0:T(8,128)(2,1)S(1)}, u32[]{:S(2)}, u32[]{:S(2)}) collective-permute-start(bf16[2,1024,128]{2,1,0:T(8,128)(2,1)S(1)} %copy-done), channel_id=1, source_target_pairs={{0,2},{1,3},{2,0},{3,1},{4,6},{5,7},{6,4},{7,5},{8,10},{9,11},{10,... | collective-permute-start | bytes 1572872 | tf_op jit(solution)/shard_map/ppermute | solution.py:361
  94.9 44.6 %collective-permute-start.6 = (bf16[2,1024,128]{2,1,0:T(8,128)(2,1)S(1)}, bf16[2,1024,128]{2,1,0:T(8,128)(2,1)S(1)}, u32[]{:S(2)}, u32[]{:S(2)}) collective-permute-start(bf16[2,1024,128]{2,1,0:T(8,128)(2,1)S(1)} %copy-done), channel_id=1, source_target_pairs={{0,1},{1,0},{2,3},{3,2},{4,5},{5,4},{6,7},{7,6},{8,9},{9,8},{10,11... | collective-permute-start | bytes 1572872 | tf_op jit(solution)/shard_map/ppermute | solution.py:361
  95.0 44.0 %collective-permute-start.9 = (bf16[2,128,1024]{2,1,0:T(8,128)(2,1)S(1)}, bf16[2,128,1024]{2,1,0:T(8,128)(2,1)S(1)}, u32[]{:S(2)}, u32[]{:S(2)}) collective-permute-start(bf16[2,128,1024]{2,1,0:T(8,128)(2,1)S(1)} %copy-done.1), channel_id=1, source_target_pairs={{0,2},{1,3},{2,0},{3,1},{4,6},{5,7},{6,4},{7,5},{8,10},{9,11},{10,... | collective-permute-start | bytes 1572872 | tf_op jit(solution)/shard_map/ppermute | solution.py:361
  95.4 44.2 %collective-permute-start.7 = (bf16[2,128,1024]{2,1,0:T(8,128)(2,1)S(1)}, bf16[2,128,1024]{2,1,0:T(8,128)(2,1)S(1)}, u32[]{:S(2)}, u32[]{:S(2)}) collective-permute-start(bf16[2,128,1024]{2,1,0:T(8,128)(2,1)S(1)} %copy-done.1), channel_id=1, source_target_pairs={{0,1},{1,0},{2,3},{3,2},{4,5},{5,4},{6,7},{7,6},{8,9},{9,8},{10,11... | collective-permute-start | bytes 1572872 | tf_op jit(solution)/shard_map/ppermute | solution.py:361
  138.9 32.0 %slice-start = ((s8[8388608]{0:T(1024)(128)(4,1)}), s8[4194304]{0:T(1024)(128)(4,1)S(1)}, s32[]{:S(2)}) async-start(s8[8388608]{0:T(1024)(128)(4,1)} %bitcast.35), calls=%async_computation.12 | async-start | bytes 8388608
  138.9 32.0 %slice-start.1 = ((s8[8388608]{0:T(1024)(128)(4,1)}), s8[4194304]{0:T(1024)(128)(4,1)S(1)}, s32[]{:S(2)}) async-start(s8[8388608]{0:T(1024)(128)(4,1)} %bitcast.35), calls=%async_computation.13 | async-start | bytes 8388608
  138.9 2.0 collective-permute-start.10
  139.2 2.5 collective-permute-start.11
  179.0 292.8 %reduce-scatter.9.cloned.1.call-start = ((), (), s32[]{:S(2)}) async-start(), calls=%async_computation.8 | async-start | bytes 10485760 | tf_op jit(solution)/shard_map/reduce_scatter | solution.py:399
  190.7 369.3 %all-gather.9.cloned.1.call-start = ((), (), s32[]{:S(2)}) async-start(), calls=%async_computation.9 | async-start | bytes 5242880 | tf_op jit(solution)/shard_map/all_gather | solution.py:403
  324.7 150.7 %copy-start.6 = (f32[128,4096]{1,0:T(8,128)S(1)}, f32[128,4096]{1,0:T(8,128)}, u32[]{:S(2)}) copy-start(f32[128,4096]{1,0:T(8,128)} %reduce-scatter.5.cloned.1.call-done) | copy-start | bytes 6291460
  471.8 3.7 copy-start.8
  479.2 161.1 %all-gather.5.cloned.1.call-start = ((), (), s32[]{:S(2)}) async-start(), calls=%async_computation.5 | async-start | bytes 5242880 | tf_op jit(solution)/shard_map/all_gather | solution.py:403
  479.7 305.7 %reduce-scatter.11.cloned.1.call-start = ((), (), s32[]{:S(2)}) async-start(), calls=%async_computation.10 | async-start | bytes 10485760 | tf_op jit(solution)/shard_map/reduce_scatter | solution.py:408
  632.5 300.4 %reduce-scatter.7.cloned.1.call-start = ((), (), s32[]{:S(2)}) async-start(), calls=%async_computation.6 | async-start | bytes 10485760 | tf_op jit(solution)/shard_map/reduce_scatter | solution.py:408
  712.4 220.5 %copy-start.7 = (f32[128,4096]{1,0:T(8,128)S(1)}, f32[128,4096]{1,0:T(8,128)}, u32[]{:S(2)}) copy-start(f32[128,4096]{1,0:T(8,128)} %reduce-scatter.5.cloned.1.call-done) | copy-start | bytes 6291460
  712.5 227.0 %copy-start.10 = (bf16[1024,256]{1,0:T(8,128)(2,1)S(1)}, bf16[1024,256]{1,0:T(8,128)(2,1)}, u32[]{:S(2)}) copy-start(bf16[1024,256]{1,0:T(8,128)(2,1)} %get-tuple-element.43) | copy-start | bytes 1572868
  712.5 227.9 %copy-start.9 = (bf16[1024,256]{1,0:T(8,128)(2,1)S(1)}, bf16[1024,256]{1,0:T(8,128)(2,1)}, u32[]{:S(2)}) copy-start(bf16[1024,256]{1,0:T(8,128)(2,1)} %get-tuple-element.44) | copy-start | bytes 1572868
  712.5 307.0 %all-gather.11.cloned.1.call-start = ((), (), s32[]{:S(2)}) async-start(), calls=%async_computation.11 | async-start | bytes 5242880 | tf_op jit(solution)/shard_map/all_gather | solution.py:409
  938.7 161.9 %all-gather.7.cloned.1.call-start = ((), (), s32[]{:S(2)}) async-start(), calls=%async_computation.7 | async-start | bytes 5242880 | tf_op jit(solution)/shard_map/all_gather | solution.py:409
  (4 other events, 5.9 us)
Sparse Core Ops, SparseCore 0:
  179.1 145.6 reduce-scatter.4
  327.1 144.6 reduce-scatter.8
  479.3 80.6 all-gather.8
  561.4 78.8 all-gather.4
  642.5 142.8 reduce-scatter.10
  788.2 144.6 reduce-scatter.6
  938.8 80.6 all-gather.10
  1021.6 78.8 all-gather.6

commit v2 on v1

v2 whole, which is shorter than its diff:
```python
import functools
import math

import jax
import jax.numpy as jnp
from jax import lax
from jax.experimental import pallas as pl
from jax.experimental.pallas import tpu as pltpu
from jax.sharding import PartitionSpec as P


ROPE_THETA = 500000.0
NORM_EPS = 1e-5
F32 = jnp.float32
BF16 = jnp.bfloat16
ANY = pl.BlockSpec(memory_space=pl.ANY)
VMEM = pl.BlockSpec(memory_space=pltpu.VMEM)
LANES = 128
PAIR = 2 * LANES
NT = (((1,), (1,)), ((), ()))
each = functools.partial(pl.loop, 0)


def tile(i, n):
    return pl.ds(pl.multiple_of(i * n, n), n)


def params(mib, **more):
    return pltpu.CompilerParams(vmem_limit_bytes=mib * 2**20, **more)


def cost(flops, moved):
    return pl.CostEstimate(flops=flops, bytes_accessed=moved, transcendentals=0)


def struct(shape, dtype):
    return jax.ShapeDtypeStruct(shape, dtype)


def block_positions(owner, groups, blk_len, prefix_len):
    local_row = jnp.arange(2 * blk_len, dtype=jnp.int32)
    blk_idx = jnp.where(local_row < blk_len, owner, 2 * groups - 1 - owner)
    return prefix_len + blk_idx * blk_len + local_row % blk_len


def rope_tables(positions, head_dim):
    inv_freq = ROPE_THETA ** (-jnp.arange(0, head_dim, 2, dtype=F32) / head_dim)
    angles = positions.astype(F32)[:, None] * inv_freq[None, :]
    cos_tab, sin_tab = jnp.cos(angles), jnp.sin(angles)
    return jnp.concatenate([cos_tab, cos_tab], axis=1), jnp.concatenate([-sin_tab, sin_tab], axis=1)


def qkv_kernel(x_ref, g_ref, wq_ref, wk_ref, wv_ref, cos_ref, sin_ref, q_ref, k_ref, vt_ref, kf_ref, vf_ref, h_ref, *, nq):
    step = pl.program_id(0)
    rows = x_ref.shape[0]
    rt = 128

    @pl.when(step == 0)
    def _():
        @each(rows // rt)
        def _(i):
            sl = tile(i, rt)
            xv = x_ref[sl, :].astype(F32)
            inv = lax.rsqrt(jnp.mean(xv * xv, axis=-1, keepdims=True) + NORM_EPS)
            h_ref[sl, :] = (xv * inv * g_ref[...].astype(F32)).astype(BF16)

    def rope(block, sl):
        return (block * cos_ref[sl, :] + pltpu.roll(block, 64, axis=1) * sin_ref[sl, :]).astype(BF16)

    mt = 512

    def project(w_ref, store):
        @each(rows // mt)
        def _(i):
            sl = tile(i, mt)
            acc = jnp.dot(h_ref[sl, :], w_ref[...], preferred_element_type=F32)
            store(acc, sl)

    def heads_of(acc):
        return [(t, slice(t * LANES, (t + 1) * LANES), acc[:, t * LANES:(t + 1) * LANES]) for t in range(2)]

    def store_q(acc, sl):
        for _, cs, part in heads_of(acc):
            q_ref[sl, cs] = rope(part, sl)

    def store_k(acc, sl):
        for t, cs, part in heads_of(acc):
            kf_ref[sl, cs] = rope(part, sl)
            k_ref[t, sl, :] = kf_ref[sl, cs]

    def store_v(acc, sl):
        vf_ref[sl, :] = acc.astype(BF16)
        for t, _, part in heads_of(acc):
            vt_ref[t, :, sl] = part.T.astype(BF16)

    pl.when(step < nq)(lambda: project(wq_ref, store_q))
    pl.when(step == nq)(lambda: project(wk_ref, store_k))
    pl.when(step == nq + 1)(lambda: project(wv_ref, store_v))


def qkv(x, gain, wq, wk, wv, cos_tab, sin_tab):
    rows, depth = x.shape
    nq = wq.shape[1] // PAIR

    def fixed(shape):
        return pl.BlockSpec(shape, lambda j: tuple(0 for _ in shape))

    def whole(shape):
        return pl.BlockSpec(shape, lambda j: tuple(0 for _ in shape), pipeline_mode=pl.Buffered(1))

    def columns(n):
        return pl.BlockSpec((n, PAIR), lambda j: (0, jnp.minimum(j, nq - 1)))

    flat, by_head, by_head_t = (rows, PAIR), (2, rows, LANES), (2, LANES, rows)
    return pl.pallas_call(
        functools.partial(qkv_kernel, nq=nq),
        grid=(nq + 2,),
        in_specs=[whole(x.shape), whole((1, depth)), columns(depth), fixed(wk.shape), fixed(wv.shape), whole(cos_tab.shape), whole(sin_tab.shape)],
        out_specs=[columns(rows), fixed(by_head), fixed(by_head_t), fixed(flat), fixed(flat)],
        out_shape=[struct(s, BF16) for s in ((rows, nq * PAIR), by_head, by_head_t, flat, flat)],
        scratch_shapes=[pltpu.VMEM((rows, depth), BF16)],
        compiler_params=params(56, dimension_semantics=("arbitrary",)),
        cost_estimate=cost(2 * rows * depth * (nq + 2) * PAIR, 2 * depth * rows),
        name="qkv",
    )(x, gain.reshape(1, depth), wq, wk, wv, cos_tab, sin_tab)


NQ = 512


def fetch_pieces(refs, bufs, sems, start):
    for i, (kr, vr) in enumerate(refs):
        n = kr.shape[1]
        for j, (src, dst) in enumerate(((kr, bufs[0].at[:, pl.ds(i * n, n), :]), (vr, bufs[1].at[:, :, pl.ds(i * n, n)]))):
            copy = pltpu.make_async_copy(src, dst, sems.at[i, j])
            copy.start() if start else copy.wait()


def q_block(q_ref, head, half):
    return q_ref[tile(half, NQ), tile(head, 128)]


def attend_items(q_ref, kb_ref, vb_ref, acc_ref, m_ref, l_ref, pbufs, n_items, item, bk, c2, diag):
    depth = len(pbufs)

    def scores(i, pb):
        head, half, start = item(i)
        n = head * 2 + half
        ks = kb_ref[head // 4, pl.ds(pl.multiple_of(start, bk), bk), :]
        s = lax.dot_general(ks, q_block(q_ref, head, half), NT, preferred_element_type=F32)
        e = jnp.exp2(s * c2 - m_ref[n])
        if diag:
            seen = lax.broadcasted_iota(jnp.int32, (bk, NQ), 0) <= lax.broadcasted_iota(jnp.int32, (bk, NQ), 1)
            e = jnp.where(seen, e, 0.0)
        pb[...] = e.astype(BF16)
        l_ref[n] += jnp.sum(e.reshape(-1, *l_ref.shape[1:]), axis=0)

    def values(i, pb):
        head, half, start = item(i)
        vt = vb_ref[head // 4, :, pl.ds(pl.multiple_of(start, bk), bk)]
        acc_ref[head * 2 + half] += jnp.dot(vt, pb[...], preferred_element_type=F32)

    scores(0, pbufs[0])

    def body(g, carry):
        for u in range(depth):
            i = g * depth + u
            scores(i + 1, pbufs[(u + 1) % depth])
            values(i, pbufs[u])
        return carry

    trips = n_items // depth - 1
    lax.fori_loop(0, trips, body, 0)
    for u in range(depth):
        if u + 1 < depth:
            scores(trips * depth + u + 1, pbufs[u + 1])
        values(trips * depth + u, pbufs[u])


def prefix_kernel(*refs, first, heads, c2):
    refs = list(refs)
    q_ref, ka, va, kb, vb = refs[:5]
    refs = refs[5:]
    state_in, refs = (None, refs) if first else (refs[:3], refs[3:])
    acc_ref, m_ref, l_ref, kbuf, vbuf, pa, pb, ksem, ssem = refs
    pieces = ((ka, va), (kb, vb))
    fetch_pieces(pieces, (kbuf, vbuf), ksem, True)
    copies = []
    if not first:
        copies = [pltpu.make_async_copy(src, dst, ssem.at[i]) for i, (src, dst) in enumerate(zip(state_in, (acc_ref, m_ref, l_ref)))]
        for copy in copies:
            copy.start()
    fetch_pieces(pieces, (kbuf, vbuf), ksem, False)
    for copy in copies:
        copy.wait()
    if first:
        @each(heads * 2)
        def _(n):
            head, half = n // 2, n % 2
            s = lax.dot_general(kbuf[head // 4, tile(0, LANES), :], q_block(q_ref, head, half), NT, preferred_element_type=F32)
            m_ref[n] = jnp.max(s, axis=0, keepdims=True) * c2
            for ref in (acc_ref, l_ref):
                ref[n] = jnp.zeros(ref.shape[1:], F32)
    bk = 2 * NQ
    per = kbuf.shape[1] // bk

    def item(i):
        n = i // per
        return n // 2, n % 2, (i % per) * bk

    attend_items(q_ref, kbuf, vbuf, acc_ref, m_ref, l_ref, (pa, pb), heads * 2 * per, item, bk, c2, False)


def state_shapes(heads):
    return [struct((heads * 2, n, NQ), F32) for n in (LANES, 1, 8)]


def attend_prefix(q, pieces, state, c2):
    heads = q.shape[1] // LANES
    flat = [a for p in pieces for a in p] + list(state or ())
    n = 2 * pieces[0][0].shape[1]
    dma = pltpu.SemaphoreType.DMA
    return pl.pallas_call(
        functools.partial(prefix_kernel, first=state is None, heads=heads, c2=c2),
        in_specs=[VMEM] + [ANY] * len(flat),
        out_specs=[VMEM] * 3,
        out_shape=state_shapes(heads),
        scratch_shapes=[pltpu.VMEM((2, n, LANES), BF16), pltpu.VMEM((2, LANES, n), BF16), *[pltpu.VMEM((2 * NQ, NQ), BF16)] * 2, dma((2, 2)), dma((3,))],
        compiler_params=params(40),
        cost_estimate=cost(4 * q.size * n, 4 * q.size),
        name="attend_prefix",
    )(q, *flat)


def suffix_kernel(*refs, heads, groups, c2, axis):
    q_ref, *refs = refs
    flat, refs = refs[:4 * groups], refs[4 * groups:]
    pairs = list(zip(flat[::2], flat[1::2]))
    pre, suf = pairs[:groups], pairs[groups:]
    *state_in, o_ref, kbuf, vbuf, acc_ref, m_ref, l_ref, bad_ref, ksem, ssem, pa, pb, pc, pd = refs
    pbufs = (pa, pb, pc, pd)
    me = lax.axis_index(axis)
    fetch_pieces(suf, (kbuf, vbuf), ksem, True)
    copies = [pltpu.make_async_copy(src, dst, ssem.at[i]) for i, (src, dst) in enumerate(zip(state_in, (acc_ref, m_ref, l_ref)))]
    for copy in copies:
        copy.start()
    fetch_pieces(suf, (kbuf, vbuf), ksem, False)
    for copy in copies:
        copy.wait()
    bk = NQ
    last = 2 * groups - 1

    def locate(blk):
        late = (blk >= groups).astype(jnp.int32)
        owner = jnp.where(blk < groups, blk, last - blk)
        diff = (owner % 2 != me % 2).astype(jnp.int32) + 2 * (owner // 2 != me // 2).astype(jnp.int32)
        return (diff * 2 + late) * bk

    def full_item(i):
        head, r = i // last, i % last
        half = (r >= me).astype(jnp.int32)
        blk = jnp.where(r < me, r, r - me)
        return head, half, locate(blk)

    def diag_item(i):
        half = i % 2
        return i // 2, half, locate(jnp.where(half == 0, me, last - me))

    attend_items(q_ref, kbuf, vbuf, acc_ref, m_ref, l_ref, pbufs, heads * last, full_item, bk, c2, False)
    attend_items(q_ref, kbuf, vbuf, acc_ref, m_ref, l_ref, (pa, pb), heads * 2, diag_item, bk, c2, True)

    bad_ref[...] = jnp.zeros_like(bad_ref)

    def write(n, acc, total):
        head, half = n // 2, n % 2
        out = (acc * (1.0 / total)).T.astype(BF16)
        o_ref[tile(half, NQ), tile(head, 128)] = out

    @each(heads * 2)
    def _(n):
        acc = acc_ref[n]
        total = jnp.sum(l_ref[n], axis=0, keepdims=True)
        fine = (jnp.abs(acc) < jnp.inf) & (total < jnp.inf)
        bad = jnp.where(fine, 0.0, 1.0)
        for j in range(NQ // LANES):
            part = bad[:, j * LANES:(j + 1) * LANES]
            bad_ref[...] = jnp.maximum(bad_ref[...], jnp.max(part.reshape(-1, *bad_ref.shape), axis=0))
        write(n, acc, total)

    @pl.when(jnp.max(bad_ref[...]) > 0.0)
    def _():
        n_pre = pre[0][0].shape[1]

        @each(heads * 2)
        def _(n):
            head, half = n // 2, n % 2
            q = q_block(q_ref, head, half)
            m_ref[n] = jnp.full((1, NQ), -jnp.inf, F32)
            for ref in (acc_ref, l_ref):
                ref[n] = jnp.zeros(ref.shape[1:], F32)

            def update(ks, vt, seen):
                s = lax.dot_general(ks, q, NT, preferred_element_type=F32) * c2
                if seen is not None:
                    s = jnp.where(seen, s, -jnp.inf)
                m_old = m_ref[n]
                m_new = jnp.maximum(m_old, jnp.max(s, axis=0, keepdims=True))
                alpha = jnp.exp2(m_old - m_new)
                e = jnp.exp2(s - m_new)
                m_ref[n] = m_new
                l_ref[n] = l_ref[n] * alpha + jnp.sum(e.reshape(-1, *l_ref.shape[1:]), axis=0)
                acc_ref[n] = acc_ref[n] * alpha + jnp.dot(vt, e.astype(BF16), preferred_element_type=F32)

            kpre, vpre = pa.at[:, tile(0, LANES)], pb.at[tile(0, LANES), :]
            for kr, vr in pre:
                @each(n_pre // bk)
                def _(j):
                    sl = tile(j, bk)
                    pltpu.sync_copy(kr.at[head // 4, sl, :], kpre)
                    pltpu.sync_copy(vr.at[head // 4, :, sl], vpre)
                    update(kpre[...], vpre[...], None)

            mine = jnp.where(half == 0, me, last - me)

            @each(2 * groups)
            def _(blk):
                @pl.when(blk <= mine)
                def _():
                    start = pl.multiple_of(locate(blk), bk)
                    seen = (lax.broadcasted_iota(jnp.int32, (bk, NQ), 0) <= lax.broadcasted_iota(jnp.int32, (bk, NQ), 1)) | (blk < mine)
                    update(kbuf[head // 4, pl.ds(start, bk), :], vbuf[head // 4, :, pl.ds(start, bk)], seen)

            write(n, acc_ref[n], jnp.sum(l_ref[n], axis=0, keepdims=True))


def attend_suffix(q, pre, suf, state, c2, axis):
    heads, groups = q.shape[1] // LANES, len(suf)
    n = groups * suf[0][0].shape[1]
    flat = [a for p in list(pre) + list(suf) for a in p]
    dma = pltpu.SemaphoreType.DMA
    return pl.pallas_call(
        functools.partial(suffix_kernel, heads=heads, groups=groups, c2=c2, axis=axis),
        in_specs=[VMEM] + [ANY] * (len(flat) + 3),
        out_specs=VMEM,
        out_shape=struct(q.shape, BF16),
        scratch_shapes=[
            pltpu.VMEM((2, n, LANES), BF16), pltpu.VMEM((2, LANES, n), BF16), *(pltpu.VMEM(s.shape, F32) for s in state_shapes(heads)),
            pltpu.VMEM((8, LANES), F32), dma((groups, 2)), dma((3,)), *[pltpu.VMEM((NQ, NQ), BF16)] * 4,
        ],
        compiler_params=params(40),
        cost_estimate=cost(2 * q.size * n, 4 * q.size),
        name="attend_suffix",
    )(q, *flat, *state)


def swap(arrays, axis, groups, bit):
    return tuple(lax.ppermute(a, axis, [(i, i ^ bit) for i in range(groups)]) for a in arrays)


def attend(q, own_pre, near_pre, far_pre, own_suf, near_suf, far_suf, wo_z, wo_x, c2, groups, dps):
    state = attend_prefix(q, (own_pre, near_pre), None, c2)
    far_pre, wo_z, wo_x, state = lax.optimization_barrier((far_pre, wo_z, wo_x, state))
    cross_pre = swap(far_pre, 'cp', groups, 1)
    wo_x = wo_x + swap(wo_z[1:], 'dp', dps, 1)
    state = attend_prefix(q, (far_pre, cross_pre), state, c2)
    far_suf, wo_x, state = lax.optimization_barrier((far_suf, wo_x, state))
    cross_suf = swap(far_suf, 'cp', groups, 1)
    wo_mate = swap(wo_z + wo_x, 'cp', groups, 1)
    o = attend_suffix(q, (own_pre, near_pre, far_pre, cross_pre), (own_suf, near_suf, far_suf, cross_suf), state, c2, 'cp')
    return o, wo_z + wo_x + wo_mate


MESH = pl.DeviceIdType.MESH
ROWS_CH = 256
DOT_N = 512


def side_of(z):
    return lax.div(z, 2)


def colhalf_of(z):
    return lax.rem(lax.div(z + 1, 2), 2)


def line_kernel(o_ref, x_ref, wo_ref, *refs, nc, heads_k):
    wo_pieces, refs = refs[:12], refs[12:]
    wg_ref, wu_ref, wd_ref, gain_ref, xout_ref, land_ref = refs[:6]
    (obuf, h2, ybuf, ring, psum, act, stage, xs, xo, sstat, rstat,
     ring_sem, loc_sem, o_send, o_recv, st_send, st_recv, a1_send, a1_recv, rs_send, rs_recv, a2_send, a2_recv) = refs[6:]
    R, H = ROWS_CH, ROWS_CH // 2
    depth = wg_ref.shape[0]
    ff = wg_ref.shape[1]
    half = depth // 2
    kz = heads_k
    n_ct = half // DOT_N
    nd, ne = ff // PAIR, depth // DOT_N
    per = 4 + nd + ne
    total_loads = nc * per
    big = 1024

    z = lax.axis_index('tp')
    dp = lax.axis_index('dp')
    core = lax.rem(lax.axis_index('cp'), 2)
    side, q = side_of(z), colhalf_of(z)
    is_mid = q == 1
    is_end = q != 1
    near = 1 + side
    outer = 3 * side
    inner = 2 - side
    far_end = 3 - 3 * side
    peers = {1: z + 1 - 2 * lax.rem(z, 2), 2: lax.rem(z + 2, 4), 3: 3 - z}
    mate = peers[1]

    def rdma(src, dst, ssem, rsem, dev):
        return pltpu.make_async_remote_copy(src_ref=src, dst_ref=dst, send_sem=ssem, recv_sem=rsem, device_id={'tp': dev}, device_id_type=MESH)

    def rows_at(zz):
        return tile(side_of(zz), H)

    def cols_at(zz):
        return tile(colhalf_of(zz), half)

    barrier = pltpu.get_barrier_semaphore()
    for d in (1, 2, 3):
        pl.semaphore_signal(barrier, inc=1, device_id={'tp': peers[d]}, device_id_type=MESH)
    pl.semaphore_wait(barrier, 3)

    def load_kind(ld):
        u = ld + (per - 4)
        i1 = lax.div(u, per)
        a = lax.div(i1 + big - 1, big)
        t = lax.rem(u, per) + 4 * lax.div(i1, nc)
        return a * t + (1 - a) * ld

    def issue(ld):
        slot = lax.rem(ld, 3)
        sem = ring_sem.at[slot]
        t = load_kind(ld)

        def start(src, dst):
            pltpu.make_async_copy(src, dst, sem).start()

        for d in range(4):
            @pl.when(t == d)
            def _():
                @each(n_ct)
                def _(ct):
                    c0 = pl.multiple_of(ct * DOT_N, DOT_N)
                    if d == 0:
                        cs = tile(q * n_ct + ct, DOT_N)
                        start(wo_ref.at[:, cs], ring.at[slot, tile(ct, kz), :])
                    else:
                        for dpx in range(2):
                            for cx in range(2):
                                piece = wo_pieces[(dpx + 2 * cx) * 3 + d - 1]
                                n = piece.shape[0]
                                j = (dp + dpx - 2 * dp * dpx) * 2 + (core + cx - 2 * core * cx)
                                r0 = pl.multiple_of(ct * kz + j * n, n)
                                start(piece.at[:, pl.ds(c0, DOT_N)], ring.at[slot, pl.ds(r0, n), :])

        @pl.when((t >= 4) & (t < 4 + nd))
        def _():
            cs = pl.ds(pl.multiple_of((t - 4) * 256, 256), 256)
            start(wg_ref.at[:, cs], ring.at[slot, :depth, :PAIR])
            start(wu_ref.at[:, cs], ring.at[slot, :depth, PAIR:])

        @pl.when(t >= 4 + nd)
        def _():
            cs = pl.ds(pl.multiple_of((t - 4 - nd) * DOT_N, DOT_N), DOT_N)
            start(wd_ref.at[:, cs], ring.at[slot, :ff, :])

    def take(ld, n_rows):
        slot = lax.rem(ld, 3)
        whole = ring.at[slot, :n_rows, :]
        pltpu.make_async_copy(whole, whole, ring_sem.at[slot]).wait()
        pl.when(ld + 2 < total_loads)(lambda: issue(ld + 2))
        return slot

    def o_rows(c, zz):
        return tile(c * 2 + side_of(zz), H)

    def o_copy(c, d):
        return rdma(o_ref.at[o_rows(c, peers[d]), :], obuf.at[c, d], o_send.at[c, d - 1], o_recv.at[c, d - 1], peers[d])

    def o_start(c):
        for d in (1, 2, 3):
            o_copy(c, d).start()

    def project(c, ld0):
        own_o = pltpu.make_async_copy(o_ref.at[o_rows(c, z), :], obuf.at[c, 0], loc_sem.at[0])
        own_x = pltpu.make_async_copy(x_ref.at[o_rows(c, z), cols_at(z)], xs, loc_sem.at[1])
        own_o.start()
        own_x.start()
        for d in (1, 2, 3):
            o_copy(c, d).wait_recv()
        own_o.wait()
        own_x.wait()

        @each(n_ct)
        def _(ct):
            cs = tile(ct, DOT_N)
            ybuf[c, :, cs] = xs[:, cs].astype(F32)

        @each(4)
        def _(d):
            slot = take(ld0 + d, n_ct * kz)

            @each(n_ct)
            def _(ct):
                cs = tile(ct, DOT_N)
                w = ring[slot, tile(ct, kz), :]
                ybuf[c, :, cs] += jnp.dot(obuf[c, d], w, preferred_element_type=F32)

        sstat[c] = jnp.zeros((H, LANES), F32)

        @each(n_ct)
        def _(ct):
            yv = ybuf[c, :, tile(ct, DOT_N)]
            sstat[c] += jnp.broadcast_to(jnp.sum(yv * yv, axis=-1, keepdims=True), (H, LANES))

        swap_stat = rdma(sstat.at[c], rstat.at[c], st_send.at[c, 0], st_recv.at[c, 0], mate)
        swap_stat.start()
        swap_stat.wait_recv()
        inv = lax.rsqrt((sstat[c] + rstat[c])[:, 0:1] * (1.0 / depth) + NORM_EPS)

        @each(n_ct)
        def _(ct):
            cs = tile(ct, DOT_N)
            gs = tile(q * n_ct + ct, DOT_N)
            h2[c, rows_at(z), gs] = (ybuf[c, :, cs] * inv * gain_ref[:, gs].astype(F32)).astype(BF16)

    class Spread:
        def __init__(self, block, send, recv, own=None):
            self.block, self.send, self.recv, self.own = block, send, recv, own

        def copy(self, c, zz, s, r, dev, own=False):
            src = self.own(c) if own and self.own is not None else self.block(c, zz)
            return rdma(src, self.block(c, zz), self.send.at[c, s], self.recv.at[c, r], dev)

        def to_near(self, c):
            return self.copy(c, z, 0, 0, near, own=True)

        def to_outer(self, c):
            return self.copy(c, z, 0, 0, outer, own=True)

        def to_inner(self, c):
            return self.copy(c, z, 1, 1, inner, own=True)

        def end_to_inner(self, c):
            return self.copy(c, outer, 2, 2, inner)

        def inner_to_outer(self, c):
            return self.copy(c, inner, 3, 1, outer)

        def far_to_outer(self, c):
            return self.copy(c, far_end, 4, 2, outer)

        def start(self, c):
            pl.when(is_end)(lambda: self.to_near(c).start())

            @pl.when(is_mid)
            def _():
                self.to_outer(c).start()
                self.to_inner(c).start()

        def wait(self, c, r):
            self.copy(c, z, 0, r, mate).wait_recv()

        def serve1(self, c):
            self.wait(c, 0)
            self.end_to_inner(c).start()
            self.wait(c, 1)
            self.inner_to_outer(c).start()

        def serve2(self, c):
            self.wait(c, 2)
            self.far_to_outer(c).start()

        def drain(self, c):
            @pl.when(is_end)
            def _():
                self.to_near(c).wait_send()

            @pl.when(is_mid)
            def _():
                for copy in (self.to_outer(c), self.to_inner(c), self.end_to_inner(c), self.inner_to_outer(c), self.far_to_outer(c)):
                    copy.wait_send()

    hidden = Spread(lambda c, zz: h2.at[c, rows_at(zz), cols_at(zz)], a1_send, a1_recv)

    def out_block(c, zz):
        return xout_ref.at[tile(c * 2 + side_of(zz), H), cols_at(zz)]

    done = Spread(out_block, a2_send, a2_recv, own=lambda c: xo.at[c])

    def gate_up(c, ld0):
        @each(nd)
        def _(i):
            slot = take(ld0 + i, depth)
            gu = jnp.dot(h2[c], ring[slot, :depth, :], preferred_element_type=F32)
            g, u = gu[:, :PAIR], gu[:, PAIR:]
            a = g * (1.0 / (1.0 + jnp.exp(-g))) * u
            act[:, tile(i, PAIR)] = a.astype(BF16)

    def ps_copy(c, k_send, zz, k_recv, dev):
        return rdma(psum.at[lax.rem(c, 2), zz], land_ref.at[c, k_recv], rs_send.at[c, k_send], rs_recv.at[c, k_recv], dev)

    def sums_out(c):
        ends = (ps_copy(c, 0, far_end, 0, near), ps_copy(c, 1, inner, 2, near), ps_copy(c, 2, near, 3, near))
        mids = (ps_copy(c, 0, far_end, 1, inner), ps_copy(c, 1, outer, 0, outer), ps_copy(c, 2, inner, 4, inner))
        return ends, mids

    def wait_sums_out(c):
        ends, mids = sums_out(c)
        for flag, copies in ((is_end, ends), (is_mid, mids)):
            @pl.when(flag)
            def _():
                for copy in copies:
                    copy.wait_send()

    def down(c, ld0):
        ps = lax.rem(c, 2)
        ends, _ = sums_out(c)
        pl.when(c >= 2)(lambda: wait_sums_out(c - 2))
        for part in range(2):
            @each(ne // 2)
            def _(i):
                slot = take(ld0 + part * (ne // 2) + i, ff)
                pv = jnp.dot(act[...], ring[slot, :ff, :], preferred_element_type=F32)
                cs = tile(i, DOT_N)
                psum[ps, part, :, cs] = pv[:H]
                psum[ps, 3 - part, :, cs] = pv[H:R]

            @pl.when(is_end)
            def _():
                for copy in (ends[:1], ends[1:])[part]:
                    copy.start()

    def arrive(c, k, buf):
        ps_copy(c, 0, z, k, mate).wait_recv()
        copy = pltpu.make_async_copy(land_ref.at[c, k], stage.at[buf], loc_sem.at[2 + buf])
        copy.start()
        return copy

    def tiles(fn):
        @each(4)
        def _(i):
            fn(tile(i, H // 4))

    def pass_on(c, k, zz, send):
        arrive(c, k, 0).wait()

        def add(rs):
            psum[lax.rem(c, 2), zz, rs, :] += stage[0, rs, :]

        tiles(add)
        send.start()

    def finish(c, ks):
        for copy in [arrive(c, k, i) for i, k in enumerate(ks)]:
            copy.wait()

        def add(rs):
            v = psum[lax.rem(c, 2), z, rs, :] + stage[0, rs, :]
            if len(ks) == 2:
                v = v + stage[1, rs, :]
            xo[c, rs, :] = (ybuf[c, rs, :] + v).astype(BF16)

        tiles(add)
        done.start(c)
        pltpu.make_async_copy(xo.at[c], out_block(c, z), loc_sem.at[4]).start()
        pltpu.make_async_copy(xo.at[c], out_block(c, z), loc_sem.at[4]).wait()

    def relay(c):
        _, mids = sums_out(c)
        pass_on(c, 0, far_end, mids[0])
        pass_on(c, 1, outer, mids[1])
        pass_on(c, 2, inner, mids[2])
        finish(c, (3, 4))

    issue(jnp.int32(0))
    issue(jnp.int32(1))
    o_start(0)
    o_start(1)

    @each(nc + 3)
    def _(j):
        c = j - 1
        in_mlp = (j >= 1) & (j <= nc)
        ld_b = per * j - (per - 4) * lax.div(j + big - 1, big)
        ld_d = per * j - (per - 8) - 4 * lax.div(j, nc)
        pl.when((j >= 1) & (j + 1 < nc))(lambda: o_start(j + 1))

        @pl.when(j < nc)
        def _():
            project(j, ld_b)
            hidden.start(j)

        @pl.when(in_mlp & is_end)
        def _():
            for r in range(3):
                hidden.wait(c, r)

        pl.when(in_mlp)(lambda: gate_up(c, ld_d))
        pl.when((j < nc) & is_mid)(lambda: hidden.serve1(j))
        pl.when(in_mlp)(lambda: down(c, ld_d + nd))
        pl.when((j < nc) & is_mid)(lambda: hidden.serve2(j))
        pl.when(in_mlp & is_mid)(lambda: relay(c))
        pl.when((j >= 2) & (j <= nc + 1) & is_end)(lambda: finish(j - 2, (0,)))

        @pl.when((j >= 3) & is_mid)
        def _():
            done.serve1(j - 3)
            done.serve2(j - 3)

    @each(nc)
    def _(c):
        @pl.when(is_end)
        def _():
            for r in range(3):
                done.wait(c, r)

        for d in (1, 2, 3):
            o_copy(c, d).wait_send()
        rdma(sstat.at[c], rstat.at[c], st_send.at[c, 0], st_recv.at[c, 0], mate).wait_send()
        hidden.drain(c)
        done.drain(c)
        pl.when(c >= nc - 2)(lambda: wait_sums_out(c))


def line_block(o, x, w_out, pieces, w_gate, w_up, w_down, gain):
    rows, depth = x.shape
    ff = w_gate.shape[1]
    kz = o.shape[1]
    nc = rows // ROWS_CH
    h, half = ROWS_CH // 2, depth // 2
    ring_rows = max(depth, ff, half // DOT_N * kz)
    sems = [pltpu.SemaphoreType.DMA((nc, n)) for n in (3, 3, 1, 1, 5, 3, 3, 5, 5, 3)]
    xout, _ = pl.pallas_call(
        functools.partial(line_kernel, nc=nc, heads_k=kz),
        in_specs=[ANY] * (6 + len(pieces)) + [VMEM],
        out_specs=[ANY] * 2,
        out_shape=[struct(x.shape, BF16), struct((nc, 5, h, half), F32)],
        scratch_shapes=[
            pltpu.VMEM((nc, 4, h, kz), BF16), pltpu.VMEM((nc, ROWS_CH, depth), BF16), pltpu.VMEM((nc, h, half), F32),
            pltpu.VMEM((3, ring_rows, DOT_N), BF16), pltpu.VMEM((2, 4, h, half), F32), pltpu.VMEM((ROWS_CH, ff), BF16),
            pltpu.VMEM((2, h, half), F32), pltpu.VMEM((h, half), BF16), pltpu.VMEM((nc, h, half), BF16),
            *[pltpu.VMEM((nc, h, LANES), F32)] * 2, pltpu.SemaphoreType.DMA((3,)), pltpu.SemaphoreType.DMA((5,)), *sems,
        ],
        compiler_params=params(60, collective_id=1, has_side_effects=True),
        cost_estimate=cost(6 * x.size * ff, 2 * x.size),
        name="line_block",
    )(o, x, w_out, *pieces, w_gate, w_up, w_down, gain.reshape(1, depth))
    return xout


def gather_w_out(w_out, tps):
    z, dp, core = lax.axis_index('tp'), lax.axis_index('dp'), lax.axis_index('cp') % 2
    n, half = w_out.shape[0] // 4, w_out.shape[1] // 2
    q = (z + 1) // 2 % 2
    quarter = lax.dynamic_slice_in_dim(w_out, (dp * 2 + core) * n, n, 0)
    same = lax.dynamic_slice_in_dim(quarter, q * half, half, 1)
    other = lax.dynamic_slice_in_dim(quarter, (1 - q) * half, half, 1)
    return tuple(lax.ppermute(a, 'tp', [(i, i ^ d) for i in range(tps)]) for d, a in ((1, other), (2, other), (3, same)))


def solution(mesh):
    groups = mesh.shape['cp']
    tps = mesh.shape['tp']
    dps = mesh.shape['dp']

    def local_layer(x_loc, kp_loc, vp_loc, norm_attn, w_query, w_key, w_value, w_out, norm_mlp, w_gate, w_up, w_down):
        rows = x_loc.shape[0]
        pre_dev, kv_loc, head_dim = kp_loc.shape
        c2 = head_dim ** -0.5 * math.log2(math.e)
        me = lax.axis_index('cp')
        q_pos = block_positions(me, groups, rows // 2, pre_dev * groups)
        own_pre = (kp_loc.transpose(1, 0, 2), vp_loc.transpose(1, 2, 0))
        far_pre = swap(own_pre, 'cp', groups, 2)
        near_pre = swap(own_pre, 'cp', groups, 1)
        wo_z = gather_w_out(w_out, tps)
        cos_tab, sin_tab = rope_tables(q_pos, head_dim)
        q, k_new, vt_new, k_flat, v_flat = qkv(x_loc, norm_attn, w_query, w_key, w_value, cos_tab, sin_tab)
        own_suf = (k_new, vt_new)
        first, q = lax.optimization_barrier((wo_z[0], q))
        wo_z = (first,) + wo_z[1:]
        wo_x = swap(wo_z[:1], 'dp', dps, 1)
        far_suf = swap(own_suf, 'cp', groups, 2)
        near_suf = swap(own_suf, 'cp', groups, 1)
        o, wo_pieces = attend(q, own_pre, near_pre, far_pre, own_suf, near_suf, far_suf, wo_z, wo_x, c2, groups, dps)
        x_out = line_block(o, x_loc, w_out, wo_pieces, w_gate, w_up, w_down, norm_mlp)
        return x_out, k_flat.reshape(rows, kv_loc, head_dim), v_flat.reshape(rows, kv_loc, head_dim)

    row_spec = P(('dp', 'cp'), None)
    kv_spec = P(('dp', 'cp'), 'tp', None)
    col_spec = P(None, 'tp')
    row_split = P('tp', None)
    vec_spec = P(None)
    return jax.shard_map(local_layer, mesh=mesh, in_specs=(row_spec, kv_spec, kv_spec, vec_spec, col_spec, col_spec, col_spec, row_split, vec_spec, col_spec, col_spec, row_split), out_specs=(row_spec, kv_spec, kv_spec), check_vma=False)
```

time: 1120 us -> 840 us (0.75)
  waiting for transfers between devices: 753 us -> 23.8 us
  Pallas kernels: 140 us -> 742 us
  matrix products: 163 us -> 0 us
  local copies, waits for them, and re-layouts: 14 us -> 42.2 us
  other arithmetic: 24.3 us -> 3.22 us
  between operations: 14.6 us -> 0.83 us
    pallas_call x2 -> x3, Pallas kernels: 82.2 us -> 685 us  [the longest x1 603 us: line_block(): pl.pallas_call(functools.partial(line_kernel, nc=nc, heads_k=kz), in_spec...]
    reduce_scatter x4 -> x0, waiting for transfers between devices: 501 us -> none  [the longest x2 280 us: local_layer(): y = lax.psum_scatter(part, 'tp', scatter_dimension=0, tiled=True)]
    all_gather x4 -> x0, waiting for transfers between devices: 247 us -> none  [the longest x2 159 us: local_layer(): lax.all_gather((y + fin).astype(BF16), 'tp', axis=0, tiled=True)]
    dot_general x8 -> x0, matrix products: 163 us -> none  [the longest x2 49 us: local_layer(): up = jnp.dot(h2, w_up, preferred_element_type=F32)]
    unnamed x34 -> x57, local copies, waits for them, and re-layouts: 11.6 us -> 33 us
    ppermute x0 -> x3, waiting for transfers between devices: none -> 20.9 us  [gather_w_out(): lax.ppermute(a, 'tp', [(i, i ^ d) for i in range(tps)])]
  transfers between devices with their start and end apart: 20 -> 24, of which waited for: 12 -> 3; matrix products, arithmetic and copies ran while one was open for 15% -> 2% of each run, Pallas kernels for 10% -> 17%
where the time goes in v2:
time: 840 us; the launch traced here: 830 us
  Pallas kernels  742 us (88%)
  local copies, waits for them, and re-layouts  42.2 us (5%)
  waiting for transfers between devices  23.8 us (3%)
  starting transfers between devices  17.5 us (2%)
    pallas_call x1, Pallas kernels, line_block(): pl.pallas_call(functools.partial(line_kernel, nc=nc, heads_k=kz), in_spec...  603 us
    pallas_call x2, Pallas kernels, attend_prefix(): pl.pallas_call(functools.partial(prefix_kernel, first=state is None, head...  82.2 us
    unnamed x57, local copies, waits for them, and re-layouts  33 us
    pallas_call x1, Pallas kernels, attend_suffix(): pl.pallas_call(functools.partial(suffix_kernel, heads=heads, groups=group...  29.1 us
    pallas_call x1, Pallas kernels, qkv(): pl.pallas_call(functools.partial(qkv_kernel, nq=nq), grid=(nq + 2,), in_s...  28.3 us
    ppermute x3, waiting for transfers between devices, gather_w_out(): lax.ppermute(a, 'tp', [(i, i ^ d) for i in range(tps)])  20.9 us
  transfers between devices with their start and end apart: 24, of which 3 were waited for; matrix products, arithmetic and copies ran while one was open for 2% of the time, Pallas kernels for 17%

profile of v2, /device:TPU:0, one launch (start us, length us, event | category | flops | bytes accessed | tf_op | source)
XLA Modules:
  0.0 829.7 jit_solution(2594849383023416520)
XLA Ops:
  0.6 2.4 copy.16
  3.1 3.1 collective-permute-start.4
  6.2 1.4 copy.18
  8.2 4.0 fusion.6
  12.2 1.7 collective-permute-start
  14.6 1.9 fusion
  16.5 1.3 pad_maximum_fusion
  17.8 28.3 %qkv.1 = (bf16[1024,1024]{1,0:T(8,128)(2,1)}, bf16[2,1024,128]{2,1,0:T(8,128)(2,1)}, bf16[2,128,1024]{2,1,0:T(8,128)(2,1)}, bf16[1024,256]{1,0:T(8,128)(2,1)}, bf16[1024,256]{1,0:T(8,128)(2,1)}) custom-call(bf16[1024,4096]{1,0:T(8,128)(2,1)} %x_ref.3, bf16[1,4096]{1,0:T(2,128)(2,1)} %reshape.41.g_ref, bf16[4096,1024]{1,0:T(8,128)(2,1)} %wq_ref.1, ...), custom_call_target="tpu_custom_call" | custom-call | flops 12884901888 | bytes 8388608 | tf_op jit(solution)/shard_map/qkv/pallas_call | solution.py:115
  46.0 2.6 collective-permute-start.5
  48.9 1.6 collective-permute-start.7
  50.5 1.6 copy-done.21
  52.1 42.3 %attend_prefix.2 = (f32[16,128,512]{2,1,0:T(8,128)S(1)}, f32[16,1,512]{2,1,0:T(1,128)S(1)}, f32[16,8,512]{2,1,0:T(8,128)S(1)}) custom-call(bf16[1024,1024]{1,0:T(8,128)(2,1)S(1)} %copy-done.21, bf16[2,2048,128]{2,1,0:T(8,128)(2,1)S(1)} %bitcast.10, bf16[2,128,2048]{2,1,0:T(8,128)(2,1)S(1)} %bitcast.6, bf16[2,2048,128]{2,1,0:T(8,128)(2,1)} %collective-permute-done.1.refs_3_, ...), custom_call_target="tpu_custom_call" | custom-call | flops 17179869184 | bytes 4194304 | tf_op jit(solution)/shard_map/attend_prefix/pallas_call | solution.py:223
  94.4 2.0 copy-done.22
  96.4 20.8 %collective-permute-done.5.refs_1_ = bf16[256,2048]{1,0:T(8,128)(2,1)} collective-permute-done((bf16[256,2048]{1,0:T(8,128)(2,1)}, bf16[256,2048]{1,0:T(8,128)(2,1)}, u32[]{:S(2)}, u32[]{:S(2)}) %collective-permute-start.5) | collective-permute-done | bytes 1048608 | tf_op jit(solution)/shard_map/ppermute | solution.py:765
  117.8 1.6 collective-permute-start.12
  120.1 1.5 collective-permute-start.14
  121.7 1.5 collective-permute-start.15
  123.2 39.9 %attend_prefix.3 = (f32[16,128,512]{2,1,0:T(8,128)S(1)}, f32[16,1,512]{2,1,0:T(1,128)S(1)}, f32[16,8,512]{2,1,0:T(8,128)S(1)}) custom-call(bf16[1024,1024]{1,0:T(8,128)(2,1)S(1)} %copy-done.21, bf16[2,2048,128]{2,1,0:T(8,128)(2,1)} %collective-permute-done.3.refs_1_.refs_5_, bf16[2,128,2048]{2,1,0:T(8,128)(2,1)S(1)} %collective-permute-done.4.refs_2_.refs_6_, ...), custom_call_target="tpu_custom_call" | custom-call | flops 17179869184 | bytes 4194304 | tf_op jit(solution)/shard_map/attend_prefix/pallas_call | solution.py:223
  163.1 2.0 copy-done.20
  165.6 2.6 collective-permute-done.15.refs_5_
  175.4 2.0 reshape.43
  177.3 2.0 reshape.44
  179.3 1.2 copy-done.1
  180.5 1.2 copy-done.3
  182.8 1.0 copy-done.7
  183.8 1.0 copy-done.9
  185.9 1.0 copy-done.13
  186.9 1.0 copy-done.15
  188.0 1.0 copy-done.17
  190.1 29.1 %attend_suffix.1.o_ref = bf16[1024,1024]{1,0:T(8,128)(2,1)} custom-call(bf16[1024,1024]{1,0:T(8,128)(2,1)} %get-tuple-element.35.refs_0_, bf16[2,2048,128]{2,1,0:T(8,128)(2,1)S(1)} %bitcast.11, bf16[2,128,2048]{2,1,0:T(8,128)(2,1)S(1)} %bitcast.7, bf16[2,2048,128]{2,1,0:T(8,128)(2,1)} %collective-permute-done.1.refs_3_, ...), custom_call_target="tpu_custom_call" | custom-call | flops 8589934592 | bytes 4194304 | tf_op jit(solution)/shard_map/attend_suffix/pallas_call | solution.py:341
  219.2 602.6 %line_block.1 = (bf16[1024,4096]{1,0:T(8,128)(2,1)}, f32[4,5,128,2048]{3,2,1,0:T(8,128)}) custom-call(bf16[1024,1024]{1,0:T(8,128)(2,1)} %attend_suffix.1.o_ref, bf16[1024,4096]{1,0:T(8,128)(2,1)} %x_ref.3, bf16[1024,4096]{1,0:T(8,128)(2,1)} %wo_ref.1, bf16[256,2048]{1,0:T(8,128)(2,1)} %collective-permute-done.refs_0_, ...), custom_call_target="tpu_custom_call" | custom-call | flops 90194313216 | bytes 8388608 | tf_op jit(solution)/shard_map/line_block/pallas_call | solution.py:740
  821.9 7.9 copy.20
  (87 shorter events, 13.6 us)
Async XLA Ops:
  0.6 13.3 %copy-start.24 = (bf16[4096]{0:T(1024)(128)(2,1)S(1)}, bf16[4096]{0:T(1024)(128)(2,1)}, u32[]{:S(2)}) copy-start(bf16[4096]{0:T(1024)(128)(2,1)} %param.15) | copy-start | bytes 24580
  3.1 93.3 %collective-permute-start.4 = (bf16[2,128,2048]{2,1,0:T(8,128)(2,1)S(1)}, bf16[2,128,2048]{2,1,0:T(8,128)(2,1)S(1)}, u32[]{:S(2)}, u32[]{:S(2)}) collective-permute-start(bf16[2,128,2048]{2,1,0:T(8,128)(2,1)S(1)} %bitcast.4), channel_id=1, source_target_pairs={{0,2},{1,3},{2,0},{3,1},{4,6},{5,7},{6,4},{7,5},{8,10},{9,11},{10,... | collective-permute-start | bytes 3145736 | tf_op jit(solution)/shard_map/ppermute | solution.py:357
  6.2 42.5 %collective-permute-start.2 = (bf16[2,128,2048]{2,1,0:T(8,128)(2,1)S(1)}, bf16[2,128,2048]{2,1,0:T(8,128)(2,1)}, u32[]{:S(2)}, u32[]{:S(2)}) collective-permute-start(bf16[2,128,2048]{2,1,0:T(8,128)(2,1)S(1)} %bitcast.5), channel_id=1, source_target_pairs={{0,1},{1,0},{2,3},{3,2},{4,5},{5,4},{6,7},{7,6},{8,9},{9,8},{10,11... | collective-permute-start | bytes 3145736 | tf_op jit(solution)/shard_map/ppermute | solution.py:357
  7.5 88.9 %collective-permute-start.3 = (bf16[2,2048,128]{2,1,0:T(8,128)(2,1)S(1)}, bf16[2,2048,128]{2,1,0:T(8,128)(2,1)}, u32[]{:S(2)}, u32[]{:S(2)}) collective-permute-start(bf16[2,2048,128]{2,1,0:T(8,128)(2,1)S(1)} %bitcast.8), channel_id=1, source_target_pairs={{0,2},{1,3},{2,0},{3,1},{4,6},{5,7},{6,4},{7,5},{8,10},{9,11},{10,... | collective-permute-start | bytes 3145736 | tf_op jit(solution)/shard_map/ppermute | solution.py:357
  7.7 41.2 %collective-permute-start.1 = (bf16[2,2048,128]{2,1,0:T(8,128)(2,1)S(1)}, bf16[2,2048,128]{2,1,0:T(8,128)(2,1)}, u32[]{:S(2)}, u32[]{:S(2)}) collective-permute-start(bf16[2,2048,128]{2,1,0:T(8,128)(2,1)S(1)} %bitcast.9), channel_id=1, source_target_pairs={{0,1},{1,0},{2,3},{3,2},{4,5},{5,4},{6,7},{7,6},{8,9},{9,8},{10,11... | collective-permute-start | bytes 3145736 | tf_op jit(solution)/shard_map/ppermute | solution.py:357
  12.2 33.8 %collective-permute-start = (bf16[256,2048]{1,0:T(8,128)(2,1)}, bf16[256,2048]{1,0:T(8,128)(2,1)}, u32[]{:S(2)}, u32[]{:S(2)}) collective-permute-start(bf16[256,2048]{1,0:T(8,128)(2,1)} %get-tuple-element.66), channel_id=1, source_target_pairs={{0,4},{4,0},{8,12},{12,8},{1,5},{5,1},{9,13},{13,9},{2,6},{6,2},{1... | collective-permute-start | bytes 3145736 | tf_op jit(solution)/shard_map/ppermute | solution.py:765
  17.8 30.9 %copy-start.23 = (bf16[256,2048]{1,0:T(8,128)(2,1)S(1)}, bf16[256,2048]{1,0:T(8,128)(2,1)}, u32[]{:S(2)}) copy-start(bf16[256,2048]{1,0:T(8,128)(2,1)} %get-tuple-element.65) | copy-start | bytes 3145732
  46.0 71.2 %collective-permute-start.5 = (bf16[256,2048]{1,0:T(8,128)(2,1)}, bf16[256,2048]{1,0:T(8,128)(2,1)}, u32[]{:S(2)}, u32[]{:S(2)}) collective-permute-start(bf16[256,2048]{1,0:T(8,128)(2,1)} %get-tuple-element.66), channel_id=1, source_target_pairs={{0,8},{4,12},{8,0},{12,4},{1,9},{5,13},{9,1},{13,5},{2,10},{6,14},... | collective-permute-start | bytes 3145736 | tf_op jit(solution)/shard_map/ppermute | solution.py:765
  48.7 69.1 %copy-start.4 = (bf16[2,1024,128]{2,1,0:T(8,128)(2,1)S(1)}, bf16[2,1024,128]{2,1,0:T(8,128)(2,1)}, u32[]{:S(2)}) copy-start(bf16[2,1024,128]{2,1,0:T(8,128)(2,1)} %get-tuple-element.42.refs_9_) | copy-start | bytes 1572868
  48.7 70.6 %copy-start.6 = (bf16[2,128,1024]{2,1,0:T(8,128)(2,1)S(1)}, bf16[2,128,1024]{2,1,0:T(8,128)(2,1)}, u32[]{:S(2)}) copy-start(bf16[2,128,1024]{2,1,0:T(8,128)(2,1)} %get-tuple-element.43.refs_10_) | copy-start | bytes 1572868
  48.7 47.7 %collective-permute-start.6 = (bf16[256,2048]{1,0:T(8,128)(2,1)S(1)}, bf16[256,2048]{1,0:T(8,128)(2,1)}, u32[]{:S(2)}, u32[]{:S(2)}) collective-permute-start(bf16[256,2048]{1,0:T(8,128)(2,1)S(1)} %copy-done.23), channel_id=1, source_target_pairs={{0,12},{4,8},{8,4},{12,0},{1,13},{5,9},{9,5},{13,1},{2,14},{6,10},... | collective-permute-start | bytes 3145736 | tf_op jit(solution)/shard_map/ppermute | solution.py:765
  48.9 68.4 %collective-permute-start.7 = (bf16[256,2048]{1,0:T(8,128)(2,1)}, bf16[256,2048]{1,0:T(8,128)(2,1)}, u32[]{:S(2)}, u32[]{:S(2)}) collective-permute-start(bf16[256,2048]{1,0:T(8,128)(2,1)} %collective-permute-done.refs_0_), channel_id=1, source_target_pairs={{0,16},{16,0},{1,17},{17,1},{2,18},{18,2},{3,19},{19,3},{4,20},{20... | collective-permute-start | bytes 3145736 | tf_op jit(solution)/shard_map/ppermute | solution.py:357
  117.3 2.9 collective-permute-start.8
  117.3 4.4 collective-permute-start.9
  117.8 47.3 %collective-permute-start.12 = (bf16[2,1024,128]{2,1,0:T(8,128)(2,1)S(1)}, bf16[2,1024,128]{2,1,0:T(8,128)(2,1)S(1)}, u32[]{:S(2)}, u32[]{:S(2)}) collective-permute-start(bf16[2,1024,128]{2,1,0:T(8,128)(2,1)S(1)} %copy-done.4), channel_id=1, source_target_pairs={{0,2},{1,3},{2,0},{3,1},{4,6},{5,7},{6,4},{7,5},{8,10},{9,11},{10,... | collective-permute-start | bytes 1572872 | tf_op jit(solution)/shard_map/ppermute | solution.py:357
  119.3 55.4 %copy-start.25 = (bf16[4096]{0:T(1024)(128)(2,1)S(1)}, bf16[4096]{0:T(1024)(128)(2,1)}, u32[]{:S(2)}) copy-start(bf16[4096]{0:T(1024)(128)(2,1)} %param.20) | copy-start | bytes 24580
  119.3 45.8 %collective-permute-start.13 = (bf16[2,128,1024]{2,1,0:T(8,128)(2,1)S(1)}, bf16[2,128,1024]{2,1,0:T(8,128)(2,1)S(1)}, u32[]{:S(2)}, u32[]{:S(2)}) collective-permute-start(bf16[2,128,1024]{2,1,0:T(8,128)(2,1)S(1)} %copy-done.6), channel_id=1, source_target_pairs={{0,2},{1,3},{2,0},{3,1},{4,6},{5,7},{6,4},{7,5},{8,10},{9,11},{10,... | collective-permute-start | bytes 1572872 | tf_op jit(solution)/shard_map/ppermute | solution.py:357
  119.8 52.6 %collective-permute-start.18 = (bf16[256,2048]{1,0:T(8,128)(2,1)}, bf16[256,2048]{1,0:T(8,128)(2,1)S(1)}, u32[]{:S(2)}, u32[]{:S(2)}) collective-permute-start(bf16[256,2048]{1,0:T(8,128)(2,1)} %collective-permute-done.refs_0_), channel_id=1, source_target_pairs={{0,1},{1,0},{2,3},{3,2},{4,5},{5,4},{6,7},{7,6},{8,9},{9,8},{10,11... | collective-permute-start | bytes 3145736 | tf_op jit(solution)/shard_map/ppermute | solution.py:357
  120.1 42.9 %copy-start = (bf16[2,2048,128]{2,1,0:T(8,128)(2,1)}, bf16[2,2048,128]{2,1,0:T(8,128)(2,1)S(1)}, u32[]{:S(2)}) copy-start(bf16[2,2048,128]{2,1,0:T(8,128)(2,1)S(1)} %collective-permute-done.8.refs_3_.refs_7_) | copy-start | bytes 3145732
  120.1 45.5 %collective-permute-start.14 = (bf16[256,2048]{1,0:T(8,128)(2,1)}, bf16[256,2048]{1,0:T(8,128)(2,1)}, u32[]{:S(2)}, u32[]{:S(2)}) collective-permute-start(bf16[256,2048]{1,0:T(8,128)(2,1)} %collective-permute-done.5.refs_1_), channel_id=1, source_target_pairs={{0,16},{16,0},{1,17},{17,1},{2,18},{18,2},{3,19},{19,3},{4,20},{20... | collective-permute-start | bytes 3145736 | tf_op jit(solution)/shard_map/ppermute | solution.py:357
  121.7 41.4 %copy-start.2 = (bf16[2,128,2048]{2,1,0:T(8,128)(2,1)}, bf16[2,128,2048]{2,1,0:T(8,128)(2,1)S(1)}, u32[]{:S(2)}) copy-start(bf16[2,128,2048]{2,1,0:T(8,128)(2,1)S(1)} %collective-permute-done.9.refs_4_.refs_8_) | copy-start | bytes 3145732
  121.7 46.5 %collective-permute-start.15 = (bf16[256,2048]{1,0:T(8,128)(2,1)}, bf16[256,2048]{1,0:T(8,128)(2,1)}, u32[]{:S(2)}, u32[]{:S(2)}) collective-permute-start(bf16[256,2048]{1,0:T(8,128)(2,1)} %collective-permute-done.6.refs_2_), channel_id=1, source_target_pairs={{0,16},{16,0},{1,17},{17,1},{2,18},{18,2},{3,19},{19,3},{4,20},{20... | collective-permute-start | bytes 3145736 | tf_op jit(solution)/shard_map/ppermute | solution.py:357
  165.1 5.2 collective-permute-start.10
  165.1 6.0 collective-permute-start.11
  168.2 4.3 collective-permute-start.16
  169.0 4.8 collective-permute-start.17
  171.1 48.1 %collective-permute-start.19 = (bf16[256,2048]{1,0:T(8,128)(2,1)}, bf16[256,2048]{1,0:T(8,128)(2,1)}, u32[]{:S(2)}, u32[]{:S(2)}) collective-permute-start(bf16[256,2048]{1,0:T(8,128)(2,1)} %collective-permute-done.5.refs_1_), channel_id=1, source_target_pairs={{0,1},{1,0},{2,3},{3,2},{4,5},{5,4},{6,7},{7,6},{8,9},{9,8},{10,11... | collective-permute-start | bytes 3145736 | tf_op jit(solution)/shard_map/ppermute | solution.py:357
  171.9 47.3 %collective-permute-start.20 = (bf16[256,2048]{1,0:T(8,128)(2,1)}, bf16[256,2048]{1,0:T(8,128)(2,1)}, u32[]{:S(2)}, u32[]{:S(2)}) collective-permute-start(bf16[256,2048]{1,0:T(8,128)(2,1)} %collective-permute-done.6.refs_2_), channel_id=1, source_target_pairs={{0,1},{1,0},{2,3},{3,2},{4,5},{5,4},{6,7},{7,6},{8,9},{9,8},{10,11... | collective-permute-start | bytes 3145736 | tf_op jit(solution)/shard_map/ppermute | solution.py:357
  172.4 3.0 copy-start.26
  172.4 46.8 %collective-permute-start.21 = (bf16[256,2048]{1,0:T(8,128)(2,1)}, bf16[256,2048]{1,0:T(8,128)(2,1)}, u32[]{:S(2)}, u32[]{:S(2)}) collective-permute-start(bf16[256,2048]{1,0:T(8,128)(2,1)} %collective-permute-done.7.refs_3_), channel_id=1, source_target_pairs={{0,1},{1,0},{2,3},{3,2},{4,5},{5,4},{6,7},{7,6},{8,9},{9,8},{10,11... | collective-permute-start | bytes 3145736 | tf_op jit(solution)/shard_map/ppermute | solution.py:357
  173.4 45.8 %collective-permute-start.22 = (bf16[256,2048]{1,0:T(8,128)(2,1)}, bf16[256,2048]{1,0:T(8,128)(2,1)}, u32[]{:S(2)}, u32[]{:S(2)}) collective-permute-start(bf16[256,2048]{1,0:T(8,128)(2,1)} %collective-permute-done.14.refs_4_), channel_id=1, source_target_pairs={{0,1},{1,0},{2,3},{3,2},{4,5},{5,4},{6,7},{7,6},{8,9},{9,8},{10,11... | collective-permute-start | bytes 3145736 | tf_op jit(solution)/shard_map/ppermute | solution.py:357
  174.6 44.6 %collective-permute-start.23 = (bf16[256,2048]{1,0:T(8,128)(2,1)}, bf16[256,2048]{1,0:T(8,128)(2,1)}, u32[]{:S(2)}, u32[]{:S(2)}) collective-permute-start(bf16[256,2048]{1,0:T(8,128)(2,1)} %collective-permute-done.15.refs_5_), channel_id=1, source_target_pairs={{0,1},{1,0},{2,3},{3,2},{4,5},{5,4},{6,7},{7,6},{8,9},{9,8},{10,11... | collective-permute-start | bytes 3145736 | tf_op jit(solution)/shard_map/ppermute | solution.py:357
  (19 other events, 21.3 us)

commit v3 on v2

--- a/solution.py
+++ b/solution.py
@@ -11,9 +11,10 @@
 
 ROPE_THETA = 500000.0
 NORM_EPS = 1e-5
+ROWS_CH = 256
 F32 = jnp.float32
 BF16 = jnp.bfloat16
-ANY = pl.BlockSpec(memory_space=pl.ANY)
+HBM = pl.BlockSpec(memory_space=pl.ANY)
 VMEM = pl.BlockSpec(memory_space=pltpu.VMEM)
 LANES = 128
 PAIR = 2 * LANES
@@ -50,19 +51,26 @@
     return jnp.concatenate([cos_tab, cos_tab], axis=1), jnp.concatenate([-sin_tab, sin_tab], axis=1)
 
 
-def qkv_kernel(x_ref, g_ref, wq_ref, wk_ref, wv_ref, cos_ref, sin_ref, q_ref, k_ref, vt_ref, kf_ref, vf_ref, h_ref, *, nq):
+def qkv_kernel(x_hbm, g_ref, wq_ref, wk_ref, wv_ref, cos_ref, sin_ref, q_ref, k_ref, vt_ref, kf_ref, vf_ref, x_ref, h_ref, sems, *, nq):
     step = pl.program_id(0)
     rows = x_ref.shape[0]
-    rt = 128
+    parts, rt = sems.shape[0], 32
 
     @pl.when(step == 0)
     def _():
-        @each(rows // rt)
-        def _(i):
-            sl = tile(i, rt)
-            xv = x_ref[sl, :].astype(F32)
-            inv = lax.rsqrt(jnp.mean(xv * xv, axis=-1, keepdims=True) + NORM_EPS)
-            h_ref[sl, :] = (xv * inv * g_ref[...].astype(F32)).astype(BF16)
+        n = rows // parts
+        copies = [pltpu.make_async_copy(x_hbm.at[tile(i, n), :], x_ref.at[tile(i, n), :], sems.at[i]) for i in range(parts)]
+        for copy in copies:
+            copy.start()
+        for i, copy in enumerate(copies):
+            copy.wait()
+
+            @pl.loop(i * n // rt, (i + 1) * n // rt)
+            def _(j):
+                sl = tile(j, rt)
+                xv = x_ref[sl, :].astype(F32)
+                inv = lax.rsqrt(jnp.mean(xv * xv, axis=-1, keepdims=True) + NORM_EPS)
+                h_ref[sl, :] = (xv * inv * g_ref[...].astype(F32)).astype(BF16)
 
     def rope(block, sl):
         return (block * cos_ref[sl, :] + pltpu.roll(block, 64, axis=1) * sin_ref[sl, :]).astype(BF16)
@@ -115,38 +123,50 @@
     return pl.pallas_call(
         functools.partial(qkv_kernel, nq=nq),
         grid=(nq + 2,),
-        in_specs=[whole(x.shape), whole((1, depth)), columns(depth), fixed(wk.shape), fixed(wv.shape), whole(cos_tab.shape), whole(sin_tab.shape)],
+        in_specs=[HBM, whole((1, depth)), columns(depth), fixed(wk.shape), fixed(wv.shape), whole(cos_tab.shape), whole(sin_tab.shape)],
         out_specs=[columns(rows), fixed(by_head), fixed(by_head_t), fixed(flat), fixed(flat)],
         out_shape=[struct(s, BF16) for s in ((rows, nq * PAIR), by_head, by_head_t, flat, flat)],
-        scratch_shapes=[pltpu.VMEM((rows, depth), BF16)],
-        compiler_params=params(56, dimension_semantics=("arbitrary",)),
+        scratch_shapes=[pltpu.VMEM((rows, depth), BF16), pltpu.VMEM((rows, depth), BF16), pltpu.SemaphoreType.DMA((4,))],
+        compiler_params=params(40, dimension_semantics=("arbitrary",)),
         cost_estimate=cost(2 * rows * depth * (nq + 2) * PAIR, 2 * depth * rows),
         name="qkv",
     )(x, gain.reshape(1, depth), wq, wk, wv, cos_tab, sin_tab)
 
 
 NQ = 512
-
-
-def fetch_pieces(refs, bufs, sems, start):
-    for i, (kr, vr) in enumerate(refs):
-        n = kr.shape[1]
-        for j, (src, dst) in enumerate(((kr, bufs[0].at[:, pl.ds(i * n, n), :]), (vr, bufs[1].at[:, :, pl.ds(i * n, n)]))):
-            copy = pltpu.make_async_copy(src, dst, sems.at[i, j])
-            copy.start() if start else copy.wait()
+PER_KV = 4
+
+
+class Fetch:
+    def __init__(self, sems):
+        self.sems, self.used = sems, 0
+
+    def start(self, pairs):
+        copies = []
+        for src, dst in pairs:
+            copies.append(pltpu.make_async_copy(src, dst, self.sems.at[self.used]))
+            self.used += 1
+        for copy in copies:
+            copy.start()
+        return copies
+
+
+def settle(copies):
+    for copy in copies:
+        copy.wait()
 
 
 def q_block(q_ref, head, half):
-    return q_ref[tile(half, NQ), tile(head, 128)]
-
-
-def attend_items(q_ref, kb_ref, vb_ref, acc_ref, m_ref, l_ref, pbufs, n_items, item, bk, c2, diag):
+    return q_ref[tile(half, NQ), tile(head, LANES)]
+
+
+def attend_items(q_ref, kb_ref, vb_ref, acc_ref, m_ref, l_ref, pbufs, n_items, item, bk, c2, diag=False):
     depth = len(pbufs)
 
     def scores(i, pb):
         head, half, start = item(i)
         n = head * 2 + half
-        ks = kb_ref[head // 4, pl.ds(pl.multiple_of(start, bk), bk), :]
+        ks = kb_ref[head // PER_KV, pl.ds(pl.multiple_of(start, bk), bk), :]
         s = lax.dot_general(ks, q_block(q_ref, head, half), NT, preferred_element_type=F32)
         e = jnp.exp2(s * c2 - m_ref[n])
         if diag:
@@ -157,7 +177,7 @@
 
     def values(i, pb):
         head, half, start = item(i)
-        vt = vb_ref[head // 4, :, pl.ds(pl.multiple_of(start, bk), bk)]
+        vt = vb_ref[head // PER_KV, :, pl.ds(pl.multiple_of(start, bk), bk)]
         acc_ref[head * 2 + half] += jnp.dot(vt, pb[...], preferred_element_type=F32)
 
     scores(0, pbufs[0])
@@ -177,179 +197,189 @@
         values(trips * depth + u, pbufs[u])
 
 
-def prefix_kernel(*refs, first, heads, c2):
-    refs = list(refs)
-    q_ref, ka, va, kb, vb = refs[:5]
-    refs = refs[5:]
-    state_in, refs = (None, refs) if first else (refs[:3], refs[3:])
-    acc_ref, m_ref, l_ref, kbuf, vbuf, pa, pb, ksem, ssem = refs
-    pieces = ((ka, va), (kb, vb))
-    fetch_pieces(pieces, (kbuf, vbuf), ksem, True)
-    copies = []
-    if not first:
-        copies = [pltpu.make_async_copy(src, dst, ssem.at[i]) for i, (src, dst) in enumerate(zip(state_in, (acc_ref, m_ref, l_ref)))]
-        for copy in copies:
-            copy.start()
-    fetch_pieces(pieces, (kbuf, vbuf), ksem, False)
-    for copy in copies:
-        copy.wait()
-    if first:
-        @each(heads * 2)
-        def _(n):
-            head, half = n // 2, n % 2
-            s = lax.dot_general(kbuf[head // 4, tile(0, LANES), :], q_block(q_ref, head, half), NT, preferred_element_type=F32)
-            m_ref[n] = jnp.max(s, axis=0, keepdims=True) * c2
-            for ref in (acc_ref, l_ref):
-                ref[n] = jnp.zeros(ref.shape[1:], F32)
+def prefix_kernel(q_ref, ka, va, kb, vb, acc_ref, m_ref, l_ref, kbuf, vbuf, pa, pb, sems, *, heads, c2):
+    fetch = Fetch(sems)
+    n = ka.shape[1]
+    settle(fetch.start([(ka, kbuf.at[:, tile(0, n), :]), (va, vbuf.at[:, :, tile(0, n)]), (kb, kbuf.at[:, tile(1, n), :]), (vb, vbuf.at[:, :, tile(1, n)])]))
+
+    @each(heads * 2)
+    def _(i):
+        head, half = i // 2, i % 2
+        s = lax.dot_general(kbuf[head // PER_KV, tile(0, LANES), :], q_block(q_ref, head, half), NT, preferred_element_type=F32)
+        m_ref[i] = jnp.max(s, axis=0, keepdims=True) * c2
+        for ref in (acc_ref, l_ref):
+            ref[i] = jnp.zeros(ref.shape[1:], F32)
+
     bk = 2 * NQ
     per = kbuf.shape[1] // bk
 
     def item(i):
-        n = i // per
-        return n // 2, n % 2, (i % per) * bk
-
-    attend_items(q_ref, kbuf, vbuf, acc_ref, m_ref, l_ref, (pa, pb), heads * 2 * per, item, bk, c2, False)
+        pair = i // per
+        return pair // 2, pair % 2, (i % per) * bk
+
+    attend_items(q_ref, kbuf, vbuf, acc_ref, m_ref, l_ref, (pa, pb), heads * 2 * per, item, bk, c2)
 
 
 def state_shapes(heads):
     return [struct((heads * 2, n, NQ), F32) for n in (LANES, 1, 8)]
 
 
-def attend_prefix(q, pieces, state, c2):
+def vmem_like(shapes):
+    return [pltpu.VMEM(s.shape, s.dtype) for s in shapes]
+
+
+def attend_prefix(q, pieces, c2):
     heads = q.shape[1] // LANES
-    flat = [a for p in pieces for a in p] + list(state or ())
+    flat = [a for p in pieces for a in p]
     n = 2 * pieces[0][0].shape[1]
-    dma = pltpu.SemaphoreType.DMA
+    shapes = state_shapes(heads)
     return pl.pallas_call(
-        functools.partial(prefix_kernel, first=state is None, heads=heads, c2=c2),
-        in_specs=[VMEM] + [ANY] * len(flat),
-        out_specs=[VMEM] * 3,
-        out_shape=state_shapes(heads),
-        scratch_shapes=[pltpu.VMEM((2, n, LANES), BF16), pltpu.VMEM((2, LANES, n), BF16), *[pltpu.VMEM((2 * NQ, NQ), BF16)] * 2, dma((2, 2)), dma((3,))],
-        compiler_params=params(40),
+        functools.partial(prefix_kernel, heads=heads, c2=c2),
+        in_specs=[VMEM] + [HBM] * len(flat),
+        out_specs=[VMEM] * len(shapes),
+        out_shape=shapes,
+        scratch_shapes=[
+            pltpu.VMEM((2, n, LANES), BF16), pltpu.VMEM((2, LANES, n), BF16),
+            *[pltpu.VMEM((2 * NQ, NQ), BF16)] * 2, pltpu.SemaphoreType.DMA((8,)),
+        ],
+        compiler_params=params(20),
         cost_estimate=cost(4 * q.size * n, 4 * q.size),
         name="attend_prefix",
     )(q, *flat)
 
 
-def suffix_kernel(*refs, heads, groups, c2, axis):
-    q_ref, *refs = refs
+def rest_kernel(*refs, group, groups, c2, axis):
+    q_hbm, *refs = refs
     flat, refs = refs[:4 * groups], refs[4 * groups:]
     pairs = list(zip(flat[::2], flat[1::2]))
     pre, suf = pairs[:groups], pairs[groups:]
-    *state_in, o_ref, kbuf, vbuf, acc_ref, m_ref, l_ref, bad_ref, ksem, ssem, pa, pb, pc, pd = refs
-    pbufs = (pa, pb, pc, pd)
+    acc_in, m_in, l_in, o_out, q_ref, kbuf, vbuf, ksuf, vsuf, acc_ref, m_ref, l_ref, o_ref, bad_ref, sems, wa, wb, pa, pb, pc, pd = refs
+    heads = PER_KV
     me = lax.axis_index(axis)
-    fetch_pieces(suf, (kbuf, vbuf), ksem, True)
-    copies = [pltpu.make_async_copy(src, dst, ssem.at[i]) for i, (src, dst) in enumerate(zip(state_in, (acc_ref, m_ref, l_ref)))]
-    for copy in copies:
-        copy.start()
-    fetch_pieces(suf, (kbuf, vbuf), ksem, False)
-    for copy in copies:
-        copy.wait()
-    bk = NQ
+    fetch = Fetch(sems)
+    mine = group * heads * 2
+    n_pre, n_suf = pre[0][0].shape[1], suf[0][0].shape[1]
+    first = fetch.start([(q_hbm.at[:, tile(group, heads * LANES)], q_ref)])
+    for i, (kr, vr) in enumerate(pre[2:]):
+        first += fetch.start([(kr.at[group], kbuf.at[0, tile(i, n_pre), :]), (vr.at[group], vbuf.at[0, :, tile(i, n_pre)])])
+    second = []
+    for i, (kr, vr) in enumerate(suf):
+        second += fetch.start([(kr.at[group], ksuf.at[0, tile(i, n_suf), :]), (vr.at[group], vsuf.at[0, :, tile(i, n_suf)])])
+    for ref, old in ((acc_ref, acc_in), (m_ref, m_in), (l_ref, l_in)):
+        ref[...] = old[pl.ds(mine, heads * 2)]
+    settle(first)
+    bk = 2 * NQ
+    per = kbuf.shape[1] // bk
+
+    def pre_item(i):
+        pair = i // per
+        return pair // 2, pair % 2, (i % per) * bk
+
+    attend_items(q_ref, kbuf, vbuf, acc_ref, m_ref, l_ref, (wa, wb), heads * 2 * per, pre_item, bk, c2)
+    settle(second)
     last = 2 * groups - 1
 
     def locate(blk):
         late = (blk >= groups).astype(jnp.int32)
         owner = jnp.where(blk < groups, blk, last - blk)
         diff = (owner % 2 != me % 2).astype(jnp.int32) + 2 * (owner // 2 != me // 2).astype(jnp.int32)
-        return (diff * 2 + late) * bk
+        return (diff * 2 + late) * NQ
 
     def full_item(i):
         head, r = i // last, i % last
         half = (r >= me).astype(jnp.int32)
-        blk = jnp.where(r < me, r, r - me)
-        return head, half, locate(blk)
+        return head, half, locate(jnp.where(r < me, r, r - me))
 
     def diag_item(i):
         half = i % 2
         return i // 2, half, locate(jnp.where(half == 0, me, last - me))
 
-    attend_items(q_ref, kbuf, vbuf, acc_ref, m_ref, l_ref, pbufs, heads * last, full_item, bk, c2, False)
-    attend_items(q_ref, kbuf, vbuf, acc_ref, m_ref, l_ref, (pa, pb), heads * 2, diag_item, bk, c2, True)
-
+    attend_items(q_ref, ksuf, vsuf, acc_ref, m_ref, l_ref, (pa, pb, pc, pd), heads * last, full_item, NQ, c2)
+    attend_items(q_ref, ksuf, vsuf, acc_ref, m_ref, l_ref, (pa, pb), heads * 2, diag_item, NQ, c2, diag=True)
     bad_ref[...] = jnp.zeros_like(bad_ref)
-
-    def write(n, acc, total):
-        head, half = n // 2, n % 2
+    chunk = ROWS_CH // 2
+
+    def write(i, acc, total):
+        head, half = i // 2, i % 2
         out = (acc * (1.0 / total)).T.astype(BF16)
-        o_ref[tile(half, NQ), tile(head, 128)] = out
+        n_p = NQ // chunk
+        for p in range(n_p):
+            o_ref[p % 2, tile(half * (n_p // 2) + p // 2, chunk), tile(head, LANES)] = out[p * chunk:(p + 1) * chunk]
 
     @each(heads * 2)
-    def _(n):
-        acc = acc_ref[n]
-        total = jnp.sum(l_ref[n], axis=0, keepdims=True)
-        fine = (jnp.abs(acc) < jnp.inf) & (total < jnp.inf)
-        bad = jnp.where(fine, 0.0, 1.0)
+    def _(i):
+        acc = acc_ref[i]
+        total = jnp.sum(l_ref[i], axis=0, keepdims=True)
+        bad = jnp.where((jnp.abs(acc) < jnp.inf) & (total < jnp.inf), 0.0, 1.0)
         for j in range(NQ // LANES):
             part = bad[:, j * LANES:(j + 1) * LANES]
             bad_ref[...] = jnp.maximum(bad_ref[...], jnp.max(part.reshape(-1, *bad_ref.shape), axis=0))
-        write(n, acc, total)
+        write(i, acc, total)
 
     @pl.when(jnp.max(bad_ref[...]) > 0.0)
     def _():
-        n_pre = pre[0][0].shape[1]
-
         @each(heads * 2)
-        def _(n):
-            head, half = n // 2, n % 2
+        def _(i):
+            head, half = i // 2, i % 2
             q = q_block(q_ref, head, half)
-            m_ref[n] = jnp.full((1, NQ), -jnp.inf, F32)
+            m_ref[i] = jnp.full((1, NQ), -jnp.inf, F32)
             for ref in (acc_ref, l_ref):
-                ref[n] = jnp.zeros(ref.shape[1:], F32)
+                ref[i] = jnp.zeros(ref.shape[1:], F32)
 
             def update(ks, vt, seen):
                 s = lax.dot_general(ks, q, NT, preferred_element_type=F32) * c2
                 if seen is not None:
                     s = jnp.where(seen, s, -jnp.inf)
-                m_old = m_ref[n]
+                m_old = m_ref[i]
                 m_new = jnp.maximum(m_old, jnp.max(s, axis=0, keepdims=True))
                 alpha = jnp.exp2(m_old - m_new)
                 e = jnp.exp2(s - m_new)
-                m_ref[n] = m_new
-                l_ref[n] = l_ref[n] * alpha + jnp.sum(e.reshape(-1, *l_ref.shape[1:]), axis=0)
-                acc_ref[n] = acc_ref[n] * alpha + jnp.dot(vt, e.astype(BF16), preferred_element_type=F32)
+                m_ref[i] = m_new
+                l_ref[i] = l_ref[i] * alpha + jnp.sum(e.reshape(-1, *l_ref.shape[1:]), axis=0)
+                acc_ref[i] = acc_ref[i] * alpha + jnp.dot(vt, e.astype(BF16), preferred_element_type=F32)
 
             kpre, vpre = pa.at[:, tile(0, LANES)], pb.at[tile(0, LANES), :]
             for kr, vr in pre:
-                @each(n_pre // bk)
+                @each(n_pre // NQ)
                 def _(j):
-                    sl = tile(j, bk)
-                    pltpu.sync_copy(kr.at[head // 4, sl, :], kpre)
-                    pltpu.sync_copy(vr.at[head // 4, :, sl], vpre)
+                    pltpu.sync_copy(kr.at[group, tile(j, NQ), :], kpre)
+                    pltpu.sync_copy(vr.at[group, :, tile(j, NQ)], vpre)
                     update(kpre[...], vpre[...], None)
 
-            mine = jnp.where(half == 0, me, last - me)
+            mine_blk = jnp.where(half == 0, me, last - me)
 
             @each(2 * groups)
             def _(blk):
-                @pl.when(blk <= mine)
+                @pl.when(blk <= mine_blk)
                 def _():
-                    start = pl.multiple_of(locate(blk), bk)
-                    seen = (lax.broadcasted_iota(jnp.int32, (bk, NQ), 0) <= lax.broadcasted_iota(jnp.int32, (bk, NQ), 1)) | (blk < mine)
-                    update(kbuf[head // 4, pl.ds(start, bk), :], vbuf[head // 4, :, pl.ds(start, bk)], seen)
-
-            write(n, acc_ref[n], jnp.sum(l_ref[n], axis=0, keepdims=True))
-
-
-def attend_suffix(q, pre, suf, state, c2, axis):
-    heads, groups = q.shape[1] // LANES, len(suf)
-    n = groups * suf[0][0].shape[1]
+                    start = pl.ds(pl.multiple_of(locate(blk), NQ), NQ)
+                    seen = (lax.broadcasted_iota(jnp.int32, (NQ, NQ), 0) <= lax.broadcasted_iota(jnp.int32, (NQ, NQ), 1)) | (blk < mine_blk)
+                    update(ksuf[0, start, :], vsuf[0, :, start], seen)
+
+            write(i, acc_ref[i], jnp.sum(l_ref[i], axis=0, keepdims=True))
+
+    pltpu.sync_copy(o_ref, o_out)
+
+
+def attend_rest(q, pre, suf, state, c2, axis, group):
+    rows, groups, width = q.shape[0], len(suf), PER_KV * LANES
+    n_pre, n_suf = 2 * pre[0][0].shape[1], groups * suf[0][0].shape[1]
     flat = [a for p in list(pre) + list(suf) for a in p]
-    dma = pltpu.SemaphoreType.DMA
+    acc, m, total = state_shapes(PER_KV)
+    out = struct((2, rows // 2, width), BF16)
     return pl.pallas_call(
-        functools.partial(suffix_kernel, heads=heads, groups=groups, c2=c2, axis=axis),
-        in_specs=[VMEM] + [ANY] * (len(flat) + 3),
-        out_specs=VMEM,
-        out_shape=struct(q.shape, BF16),
+        functools.partial(rest_kernel, group=group, groups=groups, c2=c2, axis=axis),
+        in_specs=[HBM] * (len(flat) + 1) + [VMEM] * 3,
+        out_specs=HBM,
+        out_shape=pltpu.HBM(out.shape, out.dtype),
         scratch_shapes=[
-            pltpu.VMEM((2, n, LANES), BF16), pltpu.VMEM((2, LANES, n), BF16), *(pltpu.VMEM(s.shape, F32) for s in state_shapes(heads)),
-            pltpu.VMEM((8, LANES), F32), dma((groups, 2)), dma((3,)), *[pltpu.VMEM((NQ, NQ), BF16)] * 4,
+            pltpu.VMEM((rows, width), BF16), pltpu.VMEM((1, n_pre, LANES), BF16), pltpu.VMEM((1, LANES, n_pre), BF16),
+            pltpu.VMEM((1, n_suf, LANES), BF16), pltpu.VMEM((1, LANES, n_suf), BF16), *vmem_like([acc, m, total, out]),
+            pltpu.VMEM((8, LANES), F32), pltpu.SemaphoreType.DMA((20,)), *[pltpu.VMEM((2 * NQ, NQ), BF16)] * 2, *[pltpu.VMEM((NQ, NQ), BF16)] * 4,
         ],
-        compiler_params=params(40),
-        cost_estimate=cost(2 * q.size * n, 4 * q.size),
-        name="attend_suffix",
+        compiler_params=params(20),
+        cost_estimate=cost(2 * rows * width * (2 * n_pre + n_suf), 4 * q.size),
+        name="attend_rest",
     )(q, *flat, *state)
 
 
@@ -357,22 +387,30 @@
     return tuple(lax.ppermute(a, axis, [(i, i ^ bit) for i in range(groups)]) for a in arrays)
 
 
-def attend(q, own_pre, near_pre, far_pre, own_suf, near_suf, far_suf, wo_z, wo_x, c2, groups, dps):
-    state = attend_prefix(q, (own_pre, near_pre), None, c2)
-    far_pre, wo_z, wo_x, state = lax.optimization_barrier((far_pre, wo_z, wo_x, state))
+def attend(q, own_pre, near_pre, far_pre, own_suf, near_suf, far_suf, wo_z, c2, groups, tps, dps):
+    state = attend_prefix(q, (own_pre, near_pre), c2)
+    far_pre, far_suf, wo_z, state = lax.optimization_barrier((far_pre, far_suf, wo_z, state))
     cross_pre = swap(far_pre, 'cp', groups, 1)
-    wo_x = wo_x + swap(wo_z[1:], 'dp', dps, 1)
-    state = attend_prefix(q, (far_pre, cross_pre), state, c2)
-    far_suf, wo_x, state = lax.optimization_barrier((far_suf, wo_x, state))
     cross_suf = swap(far_suf, 'cp', groups, 1)
-    wo_mate = swap(wo_z + wo_x, 'cp', groups, 1)
-    o = attend_suffix(q, (own_pre, near_pre, far_pre, cross_pre), (own_suf, near_suf, far_suf, cross_suf), state, c2, 'cp')
-    return o, wo_z + wo_x + wo_mate
+    wo_x = swap(wo_z, 'dp', dps, 1)
+    wo_near = swap(wo_z, 'cp', groups, 1)
+    pre, suf = (own_pre, near_pre, far_pre, cross_pre), (own_suf, near_suf, far_suf, cross_suf)
+    o_first = attend_rest(q, pre, suf, state, c2, 'cp', 0)
+    side = lax.axis_index('tp') // 2
+    here, there = (lax.dynamic_index_in_dim(o_first, s, keepdims=False) for s in (side, 1 - side))
+    o_got = tuple(lax.ppermute(a, 'tp', [(i, i ^ d) for i in range(tps)]) for d, a in ((1, here), (2, there), (3, there)))
+    o_first, q = lax.optimization_barrier((o_first, q))
+    o_last = attend_rest(q, pre, suf, state, c2, 'cp', 1)
+    wo_x, o_last = lax.optimization_barrier((wo_x, o_last))
+    wo_cross = swap(wo_x, 'cp', groups, 1)
+    return (here,) + o_got, o_last, wo_z + wo_x + wo_near + wo_cross
 
 
 MESH = pl.DeviceIdType.MESH
-ROWS_CH = 256
 DOT_N = 512
+MID_PLAN = ((), (('r2', -1), ('ha', 1), ('O', 3), ('xa', -2),), (('r4', -1),), (('xc', -2),), (('hb', 1),), (('xb', -1),), (('r1', 0), ('hc', 1), ('r3', 0),))
+END_PLAN = ((('f', -2), ('hw', 0), ('O', 3),), (), (), (), (), (), ())
+AHEAD, BEHIND = 3, 2
 
 
 def side_of(z):
@@ -383,7 +421,8 @@
     return lax.rem(lax.div(z + 1, 2), 2)
 
 
-def line_kernel(o_ref, x_ref, wo_ref, *refs, nc, heads_k):
+def line_kernel(*refs, nc):
+    o_first, o_ref, x_ref, wo_ref, *refs = refs[:4], *refs[4:]
     wo_pieces, refs = refs[:12], refs[12:]
     wg_ref, wu_ref, wd_ref, gain_ref, xout_ref, land_ref = refs[:6]
     (obuf, h2, ybuf, ring, psum, act, stage, xs, xo, sstat, rstat,
@@ -392,7 +431,8 @@
     depth = wg_ref.shape[0]
     ff = wg_ref.shape[1]
     half = depth // 2
-    kz = heads_k
+    width = o_ref.shape[-1]
+    kz = 2 * width
     n_ct = half // DOT_N
     nd, ne = ff // PAIR, depth // DOT_N
     per = 4 + nd + ne
@@ -477,19 +517,19 @@
         pl.when(ld + 2 < total_loads)(lambda: issue(ld + 2))
         return slot
 
-    def o_rows(c, zz):
-        return tile(c * 2 + side_of(zz), H)
+    def late(c, d):
+        return obuf.at[c, d, :, tile(1, width)]
 
     def o_copy(c, d):
-        return rdma(o_ref.at[o_rows(c, peers[d]), :], obuf.at[c, d], o_send.at[c, d - 1], o_recv.at[c, d - 1], peers[d])
+        return rdma(o_ref.at[side_of(peers[d]), tile(c, H), :], late(c, d), o_send.at[c, d - 1], o_recv.at[c, d - 1], peers[d])
 
     def o_start(c):
         for d in (1, 2, 3):
             o_copy(c, d).start()
 
     def project(c, ld0):
-        own_o = pltpu.make_async_copy(o_ref.at[o_rows(c, z), :], obuf.at[c, 0], loc_sem.at[0])
-        own_x = pltpu.make_async_copy(x_ref.at[o_rows(c, z), cols_at(z)], xs, loc_sem.at[1])
+        own_o = pltpu.make_async_copy(o_ref.at[side, tile(c, H), :], late(c, 0), loc_sem.at[0])
+        own_x = pltpu.make_async_copy(x_ref.at[tile(c * 2 + side, H), cols_at(z)], xs, loc_sem.at[1])
         own_o.start()
         own_x.start()
         for d in (1, 2, 3):
@@ -567,15 +607,9 @@
         def wait(self, c, r):
             self.copy(c, z, 0, r, mate).wait_recv()
 
-        def serve1(self, c):
-            self.wait(c, 0)
-            self.end_to_inner(c).start()
-            self.wait(c, 1)
-            self.inner_to_outer(c).start()
-
-        def serve2(self, c):
-            self.wait(c, 2)
-            self.far_to_outer(c).start()
+        def serve(self, r, c):
+            self.wait(c, r)
+            (self.end_to_inner, self.inner_to_outer, self.far_to_outer)[r](c).start()
 
         def drain(self, c):
             @pl.when(is_end)
@@ -594,14 +628,18 @@
 
     done = Spread(out_block, a2_send, a2_recv, own=lambda c: xo.at[c])
 
-    def gate_up(c, ld0):
+    def gate_up(c, ld0, active, after):
         @each(nd)
         def _(i):
-            slot = take(ld0 + i, depth)
-            gu = jnp.dot(h2[c], ring[slot, :depth, :], preferred_element_type=F32)
-            g, u = gu[:, :PAIR], gu[:, PAIR:]
-            a = g * (1.0 / (1.0 + jnp.exp(-g))) * u
-            act[:, tile(i, PAIR)] = a.astype(BF16)
+            @pl.when(active)
+            def _():
+                slot = take(ld0 + i, depth)
+                gu = jnp.dot(h2[c], ring[slot, :depth, :], preferred_element_type=F32)
+                g, u = gu[:, :PAIR], gu[:, PAIR:]
+                act[:, tile(i, PAIR)] = (g * (1.0 / (1.0 + jnp.exp(-g))) * u).astype(BF16)
+
+            for k in range(4):
+                pl.when(i == (k + 1) * nd // 4 - 1)(functools.partial(after, k + 1))
 
     def ps_copy(c, k_send, zz, k_recv, dev):
         return rdma(psum.at[lax.rem(c, 2), zz], land_ref.at[c, k_recv], rs_send.at[c, k_send], rs_recv.at[c, k_recv], dev)
@@ -619,23 +657,24 @@
                 for copy in copies:
                     copy.wait_send()
 
-    def down(c, ld0):
+    def down(c, ld0, part):
         ps = lax.rem(c, 2)
         ends, _ = sums_out(c)
-        pl.when(c >= 2)(lambda: wait_sums_out(c - 2))
-        for part in range(2):
-            @each(ne // 2)
-            def _(i):
-                slot = take(ld0 + part * (ne // 2) + i, ff)
-                pv = jnp.dot(act[...], ring[slot, :ff, :], preferred_element_type=F32)
-                cs = tile(i, DOT_N)
-                psum[ps, part, :, cs] = pv[:H]
-                psum[ps, 3 - part, :, cs] = pv[H:R]
-
-            @pl.when(is_end)
-            def _():
-                for copy in (ends[:1], ends[1:])[part]:
-                    copy.start()
+        if part == 0:
+            pl.when(c >= 2)(lambda: wait_sums_out(c - 2))
+
+        @each(ne // 2)
+        def _(i):
+            slot = take(ld0 + part * (ne // 2) + i, ff)
+            pv = jnp.dot(act[...], ring[slot, :ff, :], preferred_element_type=F32)
+            cs = tile(i, DOT_N)
+            psum[ps, part, :, cs] = pv[:H]
+            psum[ps, 3 - part, :, cs] = pv[H:R]
+
+        @pl.when(is_end)
+        def _():
+            for copy in (ends[:1], ends[1:])[part]:
+                copy.start()
 
     def arrive(c, k, buf):
         ps_copy(c, 0, z, k, mate).wait_recv()
@@ -672,47 +711,54 @@
         pltpu.make_async_copy(xo.at[c], out_block(c, z), loc_sem.at[4]).start()
         pltpu.make_async_copy(xo.at[c], out_block(c, z), loc_sem.at[4]).wait()
 
-    def relay(c):
-        _, mids = sums_out(c)
-        pass_on(c, 0, far_end, mids[0])
-        pass_on(c, 1, outer, mids[1])
-        pass_on(c, 2, inner, mids[2])
-        finish(c, (3, 4))
-
+    def relay(k, c):
+        pass_on(c, k, (far_end, outer, inner)[k], sums_out(c)[1][k])
+
+    def hidden_wait(c):
+        for r in range(3):
+            hidden.wait(c, r)
+
+    steps = {'O': o_start, 'hw': hidden_wait, 'f': lambda c: finish(c, (0,)), 'r4': lambda c: finish(c, (3, 4))}
+    for r in range(3):
+        steps['h' + 'abc'[r]] = functools.partial(hidden.serve, r)
+        steps['x' + 'abc'[r]] = functools.partial(done.serve, r)
+        steps['r' + '123'[r]] = functools.partial(relay, r)
+
+    early = [pltpu.make_async_copy(src, obuf.at[:, d, :, tile(0, width)], loc_sem.at[5 + d]) for d, src in enumerate(o_first)]
+    for copy in early:
+        copy.start()
     issue(jnp.int32(0))
     issue(jnp.int32(1))
-    o_start(0)
-    o_start(1)
-
-    @each(nc + 3)
-    def _(j):
-        c = j - 1
-        in_mlp = (j >= 1) & (j <= nc)
-        ld_b = per * j - (per - 4) * lax.div(j + big - 1, big)
-        ld_d = per * j - (per - 8) - 4 * lax.div(j, nc)
-        pl.when((j >= 1) & (j + 1 < nc))(lambda: o_start(j + 1))
-
-        @pl.when(j < nc)
+    for copy in early:
+        copy.wait()
+
+    @each(AHEAD + nc + BEHIND)
+    def _(t):
+        j = t - AHEAD
+        jj = j + 1
+        active = (j >= 0) & (j < nc)
+
+        def after(k):
+            for flag, plan in ((is_mid, MID_PLAN[k]), (is_end, END_PLAN[k])):
+                def run(plan=plan):
+                    for name, ahead in plan:
+                        c = j + ahead
+                        pl.when((c >= 0) & (c < nc))(functools.partial(steps[name], c))
+
+                if plan:
+                    pl.when(flag)(run)
+
+        @pl.when((jj >= 0) & (jj < nc))
         def _():
-            project(j, ld_b)
-            hidden.start(j)
-
-        @pl.when(in_mlp & is_end)
-        def _():
-            for r in range(3):
-                hidden.wait(c, r)
-
-        pl.when(in_mlp)(lambda: gate_up(c, ld_d))
-        pl.when((j < nc) & is_mid)(lambda: hidden.serve1(j))
-        pl.when(in_mlp)(lambda: down(c, ld_d + nd))
-        pl.when((j < nc) & is_mid)(lambda: hidden.serve2(j))
-        pl.when(in_mlp & is_mid)(lambda: relay(c))
-        pl.when((j >= 2) & (j <= nc + 1) & is_end)(lambda: finish(j - 2, (0,)))
-
-        @pl.when((j >= 3) & is_mid)
-        def _():
-            done.serve1(j - 3)
-            done.serve2(j - 3)
+            project(jj, per * jj - (per - 4) * lax.div(jj + big - 1, big))
+            hidden.start(jj)
+
+        after(0)
+        ld_d = per * jj - (per - 8) - 4 * lax.div(jj, nc)
+        gate_up(j, ld_d, active, after)
+        for part in range(2):
+            pl.when(active)(lambda: down(j, ld_d + nd, part))
+            after(5 + part)
 
     @each(nc)
     def _(c):
@@ -729,29 +775,30 @@
         pl.when(c >= nc - 2)(lambda: wait_sums_out(c))
 
 
-def line_block(o, x, w_out, pieces, w_gate, w_up, w_down, gain):
+def line_block(o_first, o_last, x, w_out, pieces, w_gate, w_up, w_down, gain):
     rows, depth = x.shape
     ff = w_gate.shape[1]
-    kz = o.shape[1]
+    width = o_last.shape[-1]
+    kz = 2 * width
     nc = rows // ROWS_CH
     h, half = ROWS_CH // 2, depth // 2
     ring_rows = max(depth, ff, half // DOT_N * kz)
     sems = [pltpu.SemaphoreType.DMA((nc, n)) for n in (3, 3, 1, 1, 5, 3, 3, 5, 5, 3)]
     xout, _ = pl.pallas_call(
-        functools.partial(line_kernel, nc=nc, heads_k=kz),
-        in_specs=[ANY] * (6 + len(pieces)) + [VMEM],
-        out_specs=[ANY] * 2,
+        functools.partial(line_kernel, nc=nc),
+        in_specs=[HBM] * (10 + len(pieces)) + [VMEM],
+        out_specs=[HBM] * 2,
         out_shape=[struct(x.shape, BF16), struct((nc, 5, h, half), F32)],
         scratch_shapes=[
             pltpu.VMEM((nc, 4, h, kz), BF16), pltpu.VMEM((nc, ROWS_CH, depth), BF16), pltpu.VMEM((nc, h, half), F32),
             pltpu.VMEM((3, ring_rows, DOT_N), BF16), pltpu.VMEM((2, 4, h, half), F32), pltpu.VMEM((ROWS_CH, ff), BF16),
             pltpu.VMEM((2, h, half), F32), pltpu.VMEM((h, half), BF16), pltpu.VMEM((nc, h, half), BF16),
-            *[pltpu.VMEM((nc, h, LANES), F32)] * 2, pltpu.SemaphoreType.DMA((3,)), pltpu.SemaphoreType.DMA((5,)), *sems,
+            *[pltpu.VMEM((nc, h, LANES), F32)] * 2, pltpu.SemaphoreType.DMA((3,)), pltpu.SemaphoreType.DMA((9,)), *sems,
         ],
         compiler_params=params(60, collective_id=1, has_side_effects=True),
         cost_estimate=cost(6 * x.size * ff, 2 * x.size),
         name="line_block",
-    )(o, x, w_out, *pieces, w_gate, w_up, w_down, gain.reshape(1, depth))
+    )(*(a.reshape(nc, h, width) for a in o_first), o_last, x, w_out, *pieces, w_gate, w_up, w_down, gain.reshape(1, depth))
     return xout
 
 
@@ -783,13 +830,10 @@
         cos_tab, sin_tab = rope_tables(q_pos, head_dim)
         q, k_new, vt_new, k_flat, v_flat = qkv(x_loc, norm_attn, w_query, w_key, w_value, cos_tab, sin_tab)
         own_suf = (k_new, vt_new)
-        first, q = lax.optimization_barrier((wo_z[0], q))
-        wo_z = (first,) + wo_z[1:]
-        wo_x = swap(wo_z[:1], 'dp', dps, 1)
         far_suf = swap(own_suf, 'cp', groups, 2)
         near_suf = swap(own_suf, 'cp', groups, 1)
-        o, wo_pieces = attend(q, own_pre, near_pre, far_pre, own_suf, near_suf, far_suf, wo_z, wo_x, c2, groups, dps)
-        x_out = line_block(o, x_loc, w_out, wo_pieces, w_gate, w_up, w_down, norm_mlp)
+        o_first, o_last, wo_pieces = attend(q, own_pre, near_pre, far_pre, own_suf, near_suf, far_suf, wo_z, c2, groups, tps, dps)
+        x_out = line_block(o_first, o_last, x_loc, w_out, wo_pieces, w_gate, w_up, w_down, norm_mlp)
         return x_out, k_flat.reshape(rows, kv_loc, head_dim), v_flat.reshape(rows, kv_loc, head_dim)
 
     row_spec = P(('dp', 'cp'), None)

time: 840 us -> 763 us (0.908); the launches traced: 830 us -> 762 us
  Pallas kernels: 742 us -> 599 us
  waiting for transfers between devices: 23.8 us -> 79.4 us
  starting transfers between devices: 17.5 us -> 47.8 us
  local copies, waits for them, and re-layouts: 42.2 us -> 32.9 us
    pallas_call x4, Pallas kernels: 714 us -> 572 us  [the longest x1 465 us: line_block(): pl.pallas_call(functools.partial(line_kernel, nc=nc), in_specs=[HBM] * (1...]
    ppermute x0 -> x3, waiting for transfers between devices: none -> 38.1 us  [attend(): lax.ppermute(a, 'tp', [(i, i ^ d) for i in range(tps)])]
    ppermute x0 -> x3, starting transfers between devices: none -> 29.8 us  [attend(): lax.ppermute(a, 'tp', [(i, i ^ d) for i in range(tps)])]
    ppermute x21, waiting for transfers between devices: 2.93 us -> 21.1 us  [swap(): lax.ppermute(a, axis, [(i, i ^ bit) for i in range(groups)])]
    unnamed x57 -> x45, local copies, waits for them, and re-layouts: 33 us -> 27 us
  transfers between devices with their start and end apart: 24 -> 27, of which waited for: 3 -> 8; matrix products, arithmetic and copies ran while one was open for 2% -> 1% of each run, Pallas kernels for 17% -> 18%
where the time goes in v3:
time: 763 us; the launch traced here: 762 us
  Pallas kernels  599 us (79%)
  waiting for transfers between devices  79.4 us (10%)
  starting transfers between devices  47.8 us (6%)
  local copies, waits for them, and re-layouts  32.9 us (4%)
    pallas_call x1, Pallas kernels, line_block(): pl.pallas_call(functools.partial(line_kernel, nc=nc), in_specs=[HBM] * (1...  465 us
    pallas_call x2, Pallas kernels, attend_rest(): pl.pallas_call(functools.partial(rest_kernel, group=group, groups=groups,...  65 us
    pallas_call x1, Pallas kernels, attend_prefix(): pl.pallas_call(functools.partial(prefix_kernel, heads=heads, c2=c2), in_s...  42.3 us
    ppermute x3, waiting for transfers between devices, attend(): lax.ppermute(a, 'tp', [(i, i ^ d) for i in range(tps)])  38.1 us
    ppermute x3, starting transfers between devices, attend(): lax.ppermute(a, 'tp', [(i, i ^ d) for i in range(tps)])  29.8 us
    unnamed x45, local copies, waits for them, and re-layouts  27 us
    pallas_call x1, Pallas kernels, qkv(): pl.pallas_call(functools.partial(qkv_kernel, nq=nq), grid=(nq + 2,), in_s...  26.4 us
    ppermute x21, waiting for transfers between devices, swap(): lax.ppermute(a, axis, [(i, i ^ bit) for i in range(groups)])  21.1 us
  transfers between devices with their start and end apart: 27, of which 8 were waited for; matrix products, arithmetic and copies ran while one was open for 1% of the time, Pallas kernels for 18%

profile of v3, /device:TPU:0, one launch (start us, length us, event | category | flops | bytes accessed | tf_op | source)
XLA Modules:
  0.0 761.8 jit_solution(8748702184390778321)
XLA Ops:
  0.6 2.4 copy.16
  3.6 1.4 copy.18
  5.8 1.9 fusion
  8.1 1.6 copy-done
  9.7 1.6 copy-done.1
  11.3 26.4 %qkv.1 = (bf16[1024,1024]{1,0:T(8,128)(2,1)S(1)}, bf16[2,1024,128]{2,1,0:T(8,128)(2,1)}, bf16[2,128,1024]{2,1,0:T(8,128)(2,1)}, bf16[1024,256]{1,0:T(8,128)(2,1)S(1)}, bf16[1024,256]{1,0:T(8,128)(2,1)S(1)}) custom-call(bf16[1024,4096]{1,0:T(8,128)(2,1)} %refs_5_.1, bf16[1,4096]{1,0:T(2,128)(2,1)S(1)} %reshape.54.g_ref, bf16[4096,1024]{1,0:T(8,128)(2,1)} %wq_ref.1, ...), custom_call_target="tpu_custom_call" | custom-call | flops 12884901888 | bytes 8388608 | tf_op jit(solution)/shard_map/qkv/pallas_call | solution.py:123
  39.0 3.0 collective-permute-start.4
  42.0 2.0 collective-permute-start.3
  44.0 2.7 fusion.6
  46.7 8.4 %collective-permute-done.4.refs_13_ = bf16[2,1024,128]{2,1,0:T(8,128)(2,1)} collective-permute-done((bf16[2,1024,128]{2,1,0:T(8,128)(2,1)}, bf16[2,1024,128]{2,1,0:T(8,128)(2,1)}, u32[]{:S(2)}, u32[]{:S(2)}) %collective-permute-start.4) | collective-permute-done | bytes 524320 | tf_op jit(solution)/shard_map/ppermute | solution.py:387
  55.1 2.0 collective-permute-start.2
  57.1 9.2 %collective-permute-done.5.refs_14_ = bf16[2,128,1024]{2,1,0:T(8,128)(2,1)} collective-permute-done((bf16[2,128,1024]{2,1,0:T(8,128)(2,1)}, bf16[2,128,1024]{2,1,0:T(8,128)(2,1)}, u32[]{:S(2)}, u32[]{:S(2)}) %collective-permute-start.5) | collective-permute-done | bytes 524320 | tf_op jit(solution)/shard_map/ppermute | solution.py:387
  66.3 3.1 collective-permute-start.7
  69.4 1.6 collective-permute-start.6
  71.0 1.6 copy-done.7
  72.6 42.3 %attend_prefix.1 = (f32[16,128,512]{2,1,0:T(8,128)S(1)}, f32[16,1,512]{2,1,0:T(1,128)S(1)}, f32[16,8,512]{2,1,0:T(8,128)S(1)}) custom-call(bf16[1024,1024]{1,0:T(8,128)(2,1)S(1)} %copy-done.7, bf16[2,2048,128]{2,1,0:T(8,128)(2,1)S(1)} %bitcast.18, bf16[2,128,2048]{2,1,0:T(8,128)(2,1)S(1)} %bitcast.13, bf16[2,2048,128]{2,1,0:T(8,128)(2,1)} %collective-permute-done.kb.refs_3_, ...), custom_call_target="tpu_custom_call" | custom-call | flops 17179869184 | bytes 4194304 | tf_op jit(solution)/shard_map/attend_prefix/pallas_call | solution.py:236
  114.9 2.0 copy-done.4
  116.9 20.2 %collective-permute-done.8.refs_9_ = bf16[256,2048]{1,0:T(8,128)(2,1)S(1)} collective-permute-done((bf16[256,2048]{1,0:T(8,128)(2,1)S(1)}, bf16[256,2048]{1,0:T(8,128)(2,1)S(1)}, u32[]{:S(2)}, u32[]{:S(2)}) %collective-permute-start.8) | collective-permute-done | bytes 1048608 | tf_op jit(solution)/shard_map/ppermute | solution.py:812
  139.5 2.9 collective-permute-done.12.refs_12_
  143.2 1.5 collective-permute-start.18
  146.7 2.2 copy-done.5
  148.9 1.6 copy-done.8
  150.5 32.5 %attend_rest.2 = bf16[2,512,512]{2,1,0:T(8,128)(2,1)} custom-call(bf16[1024,1024]{1,0:T(8,128)(2,1)S(1)} %copy-done.8, bf16[2,2048,128]{2,1,0:T(8,128)(2,1)S(1)} %bitcast.19, bf16[2,128,2048]{2,1,0:T(8,128)(2,1)S(1)} %bitcast.14, bf16[2,2048,128]{2,1,0:T(8,128)(2,1)} %collective-permute-done.kb.refs_3_, ...), custom_call_target="tpu_custom_call" | custom-call | flops 12884901888 | bytes 4194304 | tf_op jit(solution)/shard_map/attend_rest/pallas_call | solution.py:370
  184.5 32.5 %attend_rest.3.refs_4_ = bf16[2,512,512]{2,1,0:T(8,128)(2,1)} custom-call(bf16[1024,1024]{1,0:T(8,128)(2,1)S(1)} %copy-done.8, bf16[2,2048,128]{2,1,0:T(8,128)(2,1)S(1)} %bitcast.20, bf16[2,128,2048]{2,1,0:T(8,128)(2,1)S(1)} %bitcast.15, bf16[2,2048,128]{2,1,0:T(8,128)(2,1)} %collective-permute-done.kb.refs_3_, ...), custom_call_target="tpu_custom_call" | custom-call | flops 12884901888 | bytes 4194304 | tf_op jit(solution)/shard_map/attend_rest/pallas_call | solution.py:370
  217.1 22.1 %collective-permute-start.15 = (bf16[512,512]{1,0:T(8,128)(2,1)S(1)}, bf16[512,512]{1,0:T(8,128)(2,1)S(1)}, u32[]{:S(2)}, u32[]{:S(2)}) collective-permute-start(bf16[512,512]{1,0:T(8,128)(2,1)S(1)} %bitcast.21), channel_id=1, source_target_pairs={{0,4},{4,0},{8,12},{12,8},{1,5},{5,1},{9,13},{13,9},{2,6},{6,2},{1... | collective-permute-start | bytes 1572872 | tf_op jit(solution)/shard_map/ppermute | solution.py:401
  239.7 3.4 collective-permute-start.17
  243.1 8.3 %collective-permute-done.15 = bf16[512,512]{1,0:T(8,128)(2,1)S(1)} collective-permute-done((bf16[512,512]{1,0:T(8,128)(2,1)S(1)}, bf16[512,512]{1,0:T(8,128)(2,1)S(1)}, u32[]{:S(2)}, u32[]{:S(2)}) %collective-permute-start.15) | collective-permute-done | bytes 524320 | tf_op jit(solution)/shard_map/ppermute | solution.py:401
  251.4 4.4 collective-permute-start.16
  258.3 8.4 %collective-permute-done.17 = bf16[512,512]{1,0:T(8,128)(2,1)} collective-permute-done((bf16[512,512]{1,0:T(8,128)(2,1)S(1)}, bf16[512,512]{1,0:T(8,128)(2,1)}, u32[]{:S(2)}, u32[]{:S(2)}) %collective-permute-start.17) | collective-permute-done | bytes 524320 | tf_op jit(solution)/shard_map/ppermute | solution.py:401
  266.7 21.4 %collective-permute-done.16 = bf16[512,512]{1,0:T(8,128)(2,1)} collective-permute-done((bf16[512,512]{1,0:T(8,128)(2,1)S(1)}, bf16[512,512]{1,0:T(8,128)(2,1)}, u32[]{:S(2)}, u32[]{:S(2)}) %collective-permute-start.16) | collective-permute-done | bytes 524320 | tf_op jit(solution)/shard_map/ppermute | solution.py:401
  289.1 464.8 %line_block.1 = (bf16[1024,4096]{1,0:T(8,128)(2,1)}, f32[4,5,128,2048]{3,2,1,0:T(8,128)}) custom-call(bf16[4,128,512]{2,1,0:T(8,128)(2,1)} %bitcast.22, bf16[4,128,512]{2,1,0:T(8,128)(2,1)} %bitcast.23, bf16[4,128,512]{2,1,0:T(8,128)(2,1)} %bitcast.6.refs_2_, bf16[4,128,512]{2,1,0:T(8,128)(2,1)} %bitcast.7.refs_3_, bf16[2,512,512]{2,1,0:T(8,128)(2,1)} %attend_rest.3.refs_4_, ...), custom_call_target="tpu_custom_call" | custom-call | flops 90194313216 | bytes 8388608 | tf_op jit(solution)/shard_map/line_block/pallas_call | solution.py:787
  753.9 7.9 %copy.20 = bf16[1024,4096]{1,0:T(8,128)(2,1)} copy(bf16[1024,4096]{1,0:T(8,128)(2,1)} %get-tuple-element.63) | data formatting | bytes 16777216
  (82 shorter events, 13.8 us)
Async XLA Ops:
  3.1 66.3 %collective-permute-start.1 = (bf16[2,128,2048]{2,1,0:T(8,128)(2,1)S(1)}, bf16[2,128,2048]{2,1,0:T(8,128)(2,1)}, u32[]{:S(2)}, u32[]{:S(2)}) collective-permute-start(bf16[2,128,2048]{2,1,0:T(8,128)(2,1)S(1)} %bitcast.11), channel_id=1, source_target_pairs={{0,1},{1,0},{2,3},{3,2},{4,5},{5,4},{6,7},{7,6},{8,9},{9,8},{10,11... | collective-permute-start | bytes 3145736 | tf_op jit(solution)/shard_map/ppermute | solution.py:387
  5.0 66.0 %collective-permute-start = (bf16[2,2048,128]{2,1,0:T(8,128)(2,1)S(1)}, bf16[2,2048,128]{2,1,0:T(8,128)(2,1)}, u32[]{:S(2)}, u32[]{:S(2)}) collective-permute-start(bf16[2,2048,128]{2,1,0:T(8,128)(2,1)S(1)} %bitcast.16), channel_id=1, source_target_pairs={{0,1},{1,0},{2,3},{3,2},{4,5},{5,4},{6,7},{7,6},{8,9},{9,8},{10,11... | collective-permute-start | bytes 3145736 | tf_op jit(solution)/shard_map/ppermute | solution.py:387
  39.0 16.1 %collective-permute-start.4 = (bf16[2,1024,128]{2,1,0:T(8,128)(2,1)}, bf16[2,1024,128]{2,1,0:T(8,128)(2,1)}, u32[]{:S(2)}, u32[]{:S(2)}) collective-permute-start(bf16[2,1024,128]{2,1,0:T(8,128)(2,1)} %get-tuple-element.28.refs_9_), channel_id=1, source_target_pairs={{0,2},{1,3},{2,0},{3,1},{4,6},{5,7},{6,4},{7,5},{8,10},{9,11},{10,... | collective-permute-start | bytes 1572872 | tf_op jit(solution)/shard_map/ppermute | solution.py:387
  42.0 24.3 %collective-permute-start.5 = (bf16[2,128,1024]{2,1,0:T(8,128)(2,1)}, bf16[2,128,1024]{2,1,0:T(8,128)(2,1)}, u32[]{:S(2)}, u32[]{:S(2)}) collective-permute-start(bf16[2,128,1024]{2,1,0:T(8,128)(2,1)} %get-tuple-element.29.refs_10_), channel_id=1, source_target_pairs={{0,2},{1,3},{2,0},{3,1},{4,6},{5,7},{6,4},{7,5},{8,10},{9,11},{10,... | collective-permute-start | bytes 1572872 | tf_op jit(solution)/shard_map/ppermute | solution.py:387
  42.0 74.9 %collective-permute-start.3 = (bf16[2,128,2048]{2,1,0:T(8,128)(2,1)S(1)}, bf16[2,128,2048]{2,1,0:T(8,128)(2,1)}, u32[]{:S(2)}, u32[]{:S(2)}) collective-permute-start(bf16[2,128,2048]{2,1,0:T(8,128)(2,1)S(1)} %bitcast.12), channel_id=1, source_target_pairs={{0,2},{1,3},{2,0},{3,1},{4,6},{5,7},{6,4},{7,5},{8,10},{9,11},{10,... | collective-permute-start | bytes 3145736 | tf_op jit(solution)/shard_map/ppermute | solution.py:387
  55.1 61.8 %collective-permute-start.2 = (bf16[2,2048,128]{2,1,0:T(8,128)(2,1)S(1)}, bf16[2,2048,128]{2,1,0:T(8,128)(2,1)}, u32[]{:S(2)}, u32[]{:S(2)}) collective-permute-start(bf16[2,2048,128]{2,1,0:T(8,128)(2,1)S(1)} %bitcast.17), channel_id=1, source_target_pairs={{0,2},{1,3},{2,0},{3,1},{4,6},{5,7},{6,4},{7,5},{8,10},{9,11},{10,... | collective-permute-start | bytes 3145736 | tf_op jit(solution)/shard_map/ppermute | solution.py:387
  66.3 70.8 %collective-permute-start.7 = (bf16[256,2048]{1,0:T(8,128)(2,1)S(1)}, bf16[256,2048]{1,0:T(8,128)(2,1)S(1)}, u32[]{:S(2)}, u32[]{:S(2)}) collective-permute-start(bf16[256,2048]{1,0:T(8,128)(2,1)S(1)} %get-tuple-element.52), channel_id=1, source_target_pairs={{0,8},{4,12},{8,0},{12,4},{1,9},{5,13},{9,1},{13,5},{2,10},{6,14},... | collective-permute-start | bytes 3145736 | tf_op jit(solution)/shard_map/ppermute | solution.py:812
  69.4 67.7 %collective-permute-start.6 = (bf16[256,2048]{1,0:T(8,128)(2,1)S(1)}, bf16[256,2048]{1,0:T(8,128)(2,1)S(1)}, u32[]{:S(2)}, u32[]{:S(2)}) collective-permute-start(bf16[256,2048]{1,0:T(8,128)(2,1)S(1)} %get-tuple-element.52), channel_id=1, source_target_pairs={{0,4},{4,0},{8,12},{12,8},{1,5},{5,1},{9,13},{13,9},{2,6},{6,2},{1... | collective-permute-start | bytes 3145736 | tf_op jit(solution)/shard_map/ppermute | solution.py:812
  71.0 66.1 %collective-permute-start.8 = (bf16[256,2048]{1,0:T(8,128)(2,1)S(1)}, bf16[256,2048]{1,0:T(8,128)(2,1)S(1)}, u32[]{:S(2)}, u32[]{:S(2)}) collective-permute-start(bf16[256,2048]{1,0:T(8,128)(2,1)S(1)} %get-tuple-element.51), channel_id=1, source_target_pairs={{0,12},{4,8},{8,4},{12,0},{1,13},{5,9},{9,5},{13,1},{2,14},{6,10},... | collective-permute-start | bytes 3145736 | tf_op jit(solution)/shard_map/ppermute | solution.py:812
  116.9 21.3 %collective-permute-start.11 = (bf16[2,1024,128]{2,1,0:T(8,128)(2,1)}, bf16[2,1024,128]{2,1,0:T(8,128)(2,1)S(1)}, u32[]{:S(2)}, u32[]{:S(2)}) collective-permute-start(bf16[2,1024,128]{2,1,0:T(8,128)(2,1)} %get-tuple-element.28.refs_9_), channel_id=1, source_target_pairs={{0,1},{1,0},{2,3},{3,2},{4,5},{5,4},{6,7},{7,6},{8,9},{9,8},{10,11... | collective-permute-start | bytes 1572872 | tf_op jit(solution)/shard_map/ppermute | solution.py:387
  137.1 7.6 collective-permute-start.9
  137.2 8.4 %collective-permute-start.10 = (bf16[2,128,2048]{2,1,0:T(8,128)(2,1)}, bf16[2,128,2048]{2,1,0:T(8,128)(2,1)}, u32[]{:S(2)}, u32[]{:S(2)}) collective-permute-start(bf16[2,128,2048]{2,1,0:T(8,128)(2,1)} %collective-permute-done.3.refs_6_), channel_id=1, source_target_pairs={{0,1},{1,0},{2,3},{3,2},{4,5},{5,4},{6,7},{7,6},{8,9},{9,8},{10,11... | collective-permute-start | bytes 3145736 | tf_op jit(solution)/shard_map/ppermute | solution.py:387
  137.7 4.7 collective-permute-start.12
  137.8 5.4 collective-permute-start.13
  139.5 5.2 collective-permute-start.14
  142.4 96.7 %collective-permute-start.21 = (bf16[256,2048]{1,0:T(8,128)(2,1)}, bf16[256,2048]{1,0:T(8,128)(2,1)S(1)}, u32[]{:S(2)}, u32[]{:S(2)}) collective-permute-start(bf16[256,2048]{1,0:T(8,128)(2,1)} %copy-done.13), channel_id=1, source_target_pairs={{0,1},{1,0},{2,3},{3,2},{4,5},{5,4},{6,7},{7,6},{8,9},{9,8},{10,11... | collective-permute-start | bytes 3145736 | tf_op jit(solution)/shard_map/ppermute | solution.py:387
  143.2 39.9 %collective-permute-start.18 = (bf16[256,2048]{1,0:T(8,128)(2,1)}, bf16[256,2048]{1,0:T(8,128)(2,1)}, u32[]{:S(2)}, u32[]{:S(2)}) collective-permute-start(bf16[256,2048]{1,0:T(8,128)(2,1)} %copy-done.13), channel_id=1, source_target_pairs={{0,16},{16,0},{1,17},{17,1},{2,18},{18,2},{3,19},{19,3},{4,20},{20... | collective-permute-start | bytes 3145736 | tf_op jit(solution)/shard_map/ppermute | solution.py:387
  144.7 95.0 %collective-permute-start.22 = (bf16[256,2048]{1,0:T(8,128)(2,1)}, bf16[256,2048]{1,0:T(8,128)(2,1)S(1)}, u32[]{:S(2)}, u32[]{:S(2)}) collective-permute-start(bf16[256,2048]{1,0:T(8,128)(2,1)} %copy-done.12), channel_id=1, source_target_pairs={{0,1},{1,0},{2,3},{3,2},{4,5},{5,4},{6,7},{7,6},{8,9},{9,8},{10,11... | collective-permute-start | bytes 3145736 | tf_op jit(solution)/shard_map/ppermute | solution.py:387
  144.7 72.4 %collective-permute-start.19 = (bf16[256,2048]{1,0:T(8,128)(2,1)}, bf16[256,2048]{1,0:T(8,128)(2,1)}, u32[]{:S(2)}, u32[]{:S(2)}) collective-permute-start(bf16[256,2048]{1,0:T(8,128)(2,1)} %copy-done.12), channel_id=1, source_target_pairs={{0,16},{16,0},{1,17},{17,1},{2,18},{18,2},{3,19},{19,3},{4,20},{20... | collective-permute-start | bytes 3145736 | tf_op jit(solution)/shard_map/ppermute | solution.py:387
  145.6 94.2 %collective-permute-start.23 = (bf16[256,2048]{1,0:T(8,128)(2,1)}, bf16[256,2048]{1,0:T(8,128)(2,1)S(1)}, u32[]{:S(2)}, u32[]{:S(2)}) collective-permute-start(bf16[256,2048]{1,0:T(8,128)(2,1)} %copy-done.14), channel_id=1, source_target_pairs={{0,1},{1,0},{2,3},{3,2},{4,5},{5,4},{6,7},{7,6},{8,9},{9,8},{10,11... | collective-permute-start | bytes 3145736 | tf_op jit(solution)/shard_map/ppermute | solution.py:387
  150.5 32.6 %copy-start.15 = (bf16[256,2048]{1,0:T(8,128)(2,1)S(1)}, bf16[256,2048]{1,0:T(8,128)(2,1)}, u32[]{:S(2)}) copy-start(bf16[256,2048]{1,0:T(8,128)(2,1)} %copy-done.14) | copy-start | bytes 3145732
  183.1 33.9 %copy-start.9 = (bf16[2,512,512]{2,1,0:T(8,128)(2,1)S(1)}, bf16[2,512,512]{2,1,0:T(8,128)(2,1)}, u32[]{:S(2)}) copy-start(bf16[2,512,512]{2,1,0:T(8,128)(2,1)} %attend_rest.2) | copy-start | bytes 3145732
  183.1 72.8 %copy-start.11 = (bf16[4096]{0:T(1024)(128)(2,1)S(1)}, bf16[4096]{0:T(1024)(128)(2,1)}, u32[]{:S(2)}) copy-start(bf16[4096]{0:T(1024)(128)(2,1)} %param.20) | copy-start | bytes 24580
  183.1 56.0 %collective-permute-start.20 = (bf16[256,2048]{1,0:T(8,128)(2,1)S(1)}, bf16[256,2048]{1,0:T(8,128)(2,1)}, u32[]{:S(2)}, u32[]{:S(2)}) collective-permute-start(bf16[256,2048]{1,0:T(8,128)(2,1)S(1)} %copy-done.15), channel_id=1, source_target_pairs={{0,16},{16,0},{1,17},{17,1},{2,18},{18,2},{3,19},{19,3},{4,20},{20... | collective-permute-start | bytes 3145736 | tf_op jit(solution)/shard_map/ppermute | solution.py:387
  217.0 71.1 %copy-start.10 = (bf16[1,512,512]{2,1,0:T(8,128)(2,1)}, bf16[1,512,512]{2,1,0:T(8,128)(2,1)S(1)}, u32[]{:S(2)}) copy-start(bf16[1,512,512]{2,1,0:T(8,128)(2,1)S(1)} %get-tuple-element.54) | copy-start | bytes 1572868
  217.1 34.4 %collective-permute-start.15 = (bf16[512,512]{1,0:T(8,128)(2,1)S(1)}, bf16[512,512]{1,0:T(8,128)(2,1)S(1)}, u32[]{:S(2)}, u32[]{:S(2)}) collective-permute-start(bf16[512,512]{1,0:T(8,128)(2,1)S(1)} %bitcast.21), channel_id=1, source_target_pairs={{0,4},{4,0},{8,12},{12,8},{1,5},{5,1},{9,13},{13,9},{2,6},{6,2},{1... | collective-permute-start | bytes 1572872 | tf_op jit(solution)/shard_map/ppermute | solution.py:401
  239.1 49.0 %collective-permute-start.24 = (bf16[256,2048]{1,0:T(8,128)(2,1)}, bf16[256,2048]{1,0:T(8,128)(2,1)S(1)}, u32[]{:S(2)}, u32[]{:S(2)}) collective-permute-start(bf16[256,2048]{1,0:T(8,128)(2,1)} %collective-permute-done.18.refs_10_), channel_id=1, source_target_pairs={{0,1},{1,0},{2,3},{3,2},{4,5},{5,4},{6,7},{7,6},{8,9},{9,8},{10,11... | collective-permute-start | bytes 3145736 | tf_op jit(solution)/shard_map/ppermute | solution.py:387
  239.1 17.3 %copy-start.16 = (bf16[256,2048]{1,0:T(8,128)(2,1)}, bf16[256,2048]{1,0:T(8,128)(2,1)S(1)}, u32[]{:S(2)}) copy-start(bf16[256,2048]{1,0:T(8,128)(2,1)S(1)} %collective-permute-done.21.refs_13_) | copy-start | bytes 3145732
  239.1 49.0 %collective-permute-start.25 = (bf16[256,2048]{1,0:T(8,128)(2,1)}, bf16[256,2048]{1,0:T(8,128)(2,1)}, u32[]{:S(2)}, u32[]{:S(2)}) collective-permute-start(bf16[256,2048]{1,0:T(8,128)(2,1)} %collective-permute-done.19.refs_11_), channel_id=1, source_target_pairs={{0,1},{1,0},{2,3},{3,2},{4,5},{5,4},{6,7},{7,6},{8,9},{9,8},{10,11... | collective-permute-start | bytes 3145736 | tf_op jit(solution)/shard_map/ppermute | solution.py:387
  239.7 48.5 %collective-permute-start.26 = (bf16[256,2048]{1,0:T(8,128)(2,1)}, bf16[256,2048]{1,0:T(8,128)(2,1)}, u32[]{:S(2)}, u32[]{:S(2)}) collective-permute-start(bf16[256,2048]{1,0:T(8,128)(2,1)} %collective-permute-done.20.refs_12_), channel_id=1, source_target_pairs={{0,1},{1,0},{2,3},{3,2},{4,5},{5,4},{6,7},{7,6},{8,9},{9,8},{10,11... | collective-permute-start | bytes 3145736 | tf_op jit(solution)/shard_map/ppermute | solution.py:387
  239.7 27.0 %collective-permute-start.17 = (bf16[512,512]{1,0:T(8,128)(2,1)S(1)}, bf16[512,512]{1,0:T(8,128)(2,1)}, u32[]{:S(2)}, u32[]{:S(2)}) collective-permute-start(bf16[512,512]{1,0:T(8,128)(2,1)S(1)} %get-tuple-element.53), channel_id=1, source_target_pairs={{0,12},{4,8},{8,4},{12,0},{1,13},{5,9},{9,5},{13,1},{2,14},{6,10},... | collective-permute-start | bytes 1572872 | tf_op jit(solution)/shard_map/ppermute | solution.py:401
  251.4 36.6 %collective-permute-start.16 = (bf16[512,512]{1,0:T(8,128)(2,1)S(1)}, bf16[512,512]{1,0:T(8,128)(2,1)}, u32[]{:S(2)}, u32[]{:S(2)}) collective-permute-start(bf16[512,512]{1,0:T(8,128)(2,1)S(1)} %get-tuple-element.53), channel_id=1, source_target_pairs={{0,8},{4,12},{8,0},{12,4},{1,9},{5,13},{9,1},{13,5},{2,10},{6,14},... | collective-permute-start | bytes 1572872 | tf_op jit(solution)/shard_map/ppermute | solution.py:401
  (16 other events, 57.3 us)

commit v4 on v3

--- a/solution.py
+++ b/solution.py
@@ -11,11 +11,12 @@
 
 ROPE_THETA = 500000.0
 NORM_EPS = 1e-5
-ROWS_CH = 256
+ROWS_CH = 128
 F32 = jnp.float32
 BF16 = jnp.bfloat16
 HBM = pl.BlockSpec(memory_space=pl.ANY)
 VMEM = pl.BlockSpec(memory_space=pltpu.VMEM)
+IN_HBM = pl.BlockSpec(memory_space=pltpu.HBM)
 LANES = 128
 PAIR = 2 * LANES
 NT = (((1,), (1,)), ((), ()))
@@ -127,7 +128,7 @@
         out_specs=[columns(rows), fixed(by_head), fixed(by_head_t), fixed(flat), fixed(flat)],
         out_shape=[struct(s, BF16) for s in ((rows, nq * PAIR), by_head, by_head_t, flat, flat)],
         scratch_shapes=[pltpu.VMEM((rows, depth), BF16), pltpu.VMEM((rows, depth), BF16), pltpu.SemaphoreType.DMA((4,))],
-        compiler_params=params(40, dimension_semantics=("arbitrary",)),
+        compiler_params=params(56, dimension_semantics=("arbitrary",)),
         cost_estimate=cost(2 * rows * depth * (nq + 2) * PAIR, 2 * depth * rows),
         name="qkv",
     )(x, gain.reshape(1, depth), wq, wk, wv, cos_tab, sin_tab)
@@ -197,7 +198,7 @@
         values(trips * depth + u, pbufs[u])
 
 
-def prefix_kernel(q_ref, ka, va, kb, vb, acc_ref, m_ref, l_ref, kbuf, vbuf, pa, pb, sems, *, heads, c2):
+def prefix_kernel(q_ref, ka, va, kb, vb, acc_out, m_out, l_out, kbuf, vbuf, acc_ref, m_ref, l_ref, pa, pb, sems, *, heads, c2):
     fetch = Fetch(sems)
     n = ka.shape[1]
     settle(fetch.start([(ka, kbuf.at[:, tile(0, n), :]), (va, vbuf.at[:, :, tile(0, n)]), (kb, kbuf.at[:, tile(1, n), :]), (vb, vbuf.at[:, :, tile(1, n)])]))
@@ -218,6 +219,7 @@
         return pair // 2, pair % 2, (i % per) * bk
 
     attend_items(q_ref, kbuf, vbuf, acc_ref, m_ref, l_ref, (pa, pb), heads * 2 * per, item, bk, c2)
+    settle(fetch.start([(acc_ref, acc_out), (m_ref, m_out), (l_ref, l_out)]))
 
 
 def state_shapes(heads):
@@ -236,10 +238,10 @@
     return pl.pallas_call(
         functools.partial(prefix_kernel, heads=heads, c2=c2),
         in_specs=[VMEM] + [HBM] * len(flat),
-        out_specs=[VMEM] * len(shapes),
-        out_shape=shapes,
+        out_specs=[HBM] * len(shapes),
+        out_shape=[pltpu.HBM(s.shape, s.dtype) for s in shapes],
         scratch_shapes=[
-            pltpu.VMEM((2, n, LANES), BF16), pltpu.VMEM((2, LANES, n), BF16),
+            pltpu.VMEM((2, n, LANES), BF16), pltpu.VMEM((2, LANES, n), BF16), *vmem_like(shapes),
             *[pltpu.VMEM((2 * NQ, NQ), BF16)] * 2, pltpu.SemaphoreType.DMA((8,)),
         ],
         compiler_params=params(20),
@@ -253,20 +255,21 @@
     flat, refs = refs[:4 * groups], refs[4 * groups:]
     pairs = list(zip(flat[::2], flat[1::2]))
     pre, suf = pairs[:groups], pairs[groups:]
-    acc_in, m_in, l_in, o_out, q_ref, kbuf, vbuf, ksuf, vsuf, acc_ref, m_ref, l_ref, o_ref, bad_ref, sems, wa, wb, pa, pb, pc, pd = refs
+    acc_in, m_in, l_in, here_out, there_out, q_ref, kbuf, vbuf, ksuf, vsuf, acc_ref, m_ref, l_ref, acc_old, l_old, o_ref, bad_ref, sems, wa, wb, pa, pb, pc, pd = refs
     heads = PER_KV
     me = lax.axis_index(axis)
     fetch = Fetch(sems)
-    mine = group * heads * 2
+    mine = pl.ds(group * heads * 2, heads * 2)
     n_pre, n_suf = pre[0][0].shape[1], suf[0][0].shape[1]
-    first = fetch.start([(q_hbm.at[:, tile(group, heads * LANES)], q_ref)])
+    first = fetch.start([(q_hbm.at[:, tile(group, heads * LANES)], q_ref), (m_in.at[mine], m_ref)])
     for i, (kr, vr) in enumerate(pre[2:]):
         first += fetch.start([(kr.at[group], kbuf.at[0, tile(i, n_pre), :]), (vr.at[group], vbuf.at[0, :, tile(i, n_pre)])])
     second = []
     for i, (kr, vr) in enumerate(suf):
         second += fetch.start([(kr.at[group], ksuf.at[0, tile(i, n_suf), :]), (vr.at[group], vsuf.at[0, :, tile(i, n_suf)])])
-    for ref, old in ((acc_ref, acc_in), (m_ref, m_in), (l_ref, l_in)):
-        ref[...] = old[pl.ds(mine, heads * 2)]
+    third = fetch.start([(acc_in.at[mine], acc_old), (l_in.at[mine], l_old)])
+    for ref in (acc_ref, l_ref):
+        ref[...] = jnp.zeros_like(ref)
     settle(first)
     bk = 2 * NQ
     per = kbuf.shape[1] // bk
@@ -296,6 +299,7 @@
 
     attend_items(q_ref, ksuf, vsuf, acc_ref, m_ref, l_ref, (pa, pb, pc, pd), heads * last, full_item, NQ, c2)
     attend_items(q_ref, ksuf, vsuf, acc_ref, m_ref, l_ref, (pa, pb), heads * 2, diag_item, NQ, c2, diag=True)
+    settle(third)
     bad_ref[...] = jnp.zeros_like(bad_ref)
     chunk = ROWS_CH // 2
 
@@ -308,8 +312,8 @@
 
     @each(heads * 2)
     def _(i):
-        acc = acc_ref[i]
-        total = jnp.sum(l_ref[i], axis=0, keepdims=True)
+        acc = acc_ref[i] + acc_old[i]
+        total = jnp.sum(l_ref[i] + l_old[i], axis=0, keepdims=True)
         bad = jnp.where((jnp.abs(acc) < jnp.inf) & (total < jnp.inf), 0.0, 1.0)
         for j in range(NQ // LANES):
             part = bad[:, j * LANES:(j + 1) * LANES]
@@ -358,7 +362,8 @@
 
             write(i, acc_ref[i], jnp.sum(l_ref[i], axis=0, keepdims=True))
 
-    pltpu.sync_copy(o_ref, o_out)
+    side = lax.axis_index('tp') // 2
+    settle(fetch.start([(o_ref.at[side], here_out), (o_ref.at[1 - side], there_out)]))
 
 
 def attend_rest(q, pre, suf, state, c2, axis, group):
@@ -366,16 +371,16 @@
     n_pre, n_suf = 2 * pre[0][0].shape[1], groups * suf[0][0].shape[1]
     flat = [a for p in list(pre) + list(suf) for a in p]
     acc, m, total = state_shapes(PER_KV)
-    out = struct((2, rows // 2, width), BF16)
+    out = pltpu.HBM((rows // 2, width), BF16)
     return pl.pallas_call(
         functools.partial(rest_kernel, group=group, groups=groups, c2=c2, axis=axis),
-        in_specs=[HBM] * (len(flat) + 1) + [VMEM] * 3,
-        out_specs=HBM,
-        out_shape=pltpu.HBM(out.shape, out.dtype),
+        in_specs=[IN_HBM] + [HBM] * len(flat) + [IN_HBM] * 3,
+        out_specs=[HBM] * 2,
+        out_shape=[out] * 2,
         scratch_shapes=[
             pltpu.VMEM((rows, width), BF16), pltpu.VMEM((1, n_pre, LANES), BF16), pltpu.VMEM((1, LANES, n_pre), BF16),
-            pltpu.VMEM((1, n_suf, LANES), BF16), pltpu.VMEM((1, LANES, n_suf), BF16), *vmem_like([acc, m, total, out]),
-            pltpu.VMEM((8, LANES), F32), pltpu.SemaphoreType.DMA((20,)), *[pltpu.VMEM((2 * NQ, NQ), BF16)] * 2, *[pltpu.VMEM((NQ, NQ), BF16)] * 4,
+            pltpu.VMEM((1, n_suf, LANES), BF16), pltpu.VMEM((1, LANES, n_suf), BF16), *vmem_like([acc, m, total, acc, total, struct((2, rows // 2, width), BF16)]),
+            pltpu.VMEM((8, LANES), F32), pltpu.SemaphoreType.DMA((22,)), *[pltpu.VMEM((2 * NQ, NQ), BF16)] * 2, *[pltpu.VMEM((NQ, NQ), BF16)] * 4,
         ],
         compiler_params=params(20),
         cost_estimate=cost(2 * rows * width * (2 * n_pre + n_suf), 4 * q.size),
@@ -392,25 +397,25 @@
     far_pre, far_suf, wo_z, state = lax.optimization_barrier((far_pre, far_suf, wo_z, state))
     cross_pre = swap(far_pre, 'cp', groups, 1)
     cross_suf = swap(far_suf, 'cp', groups, 1)
-    wo_x = swap(wo_z, 'dp', dps, 1)
-    wo_near = swap(wo_z, 'cp', groups, 1)
+    wo = jnp.stack(wo_z)
+    wo_x, = swap((wo,), 'dp', dps, 1)
+    wo_y, = swap((wo,), 'cp', groups, 2)
     pre, suf = (own_pre, near_pre, far_pre, cross_pre), (own_suf, near_suf, far_suf, cross_suf)
-    o_first = attend_rest(q, pre, suf, state, c2, 'cp', 0)
-    side = lax.axis_index('tp') // 2
-    here, there = (lax.dynamic_index_in_dim(o_first, s, keepdims=False) for s in (side, 1 - side))
+    here, there = attend_rest(q, pre, suf, state, c2, 'cp', 0)
     o_got = tuple(lax.ppermute(a, 'tp', [(i, i ^ d) for i in range(tps)]) for d, a in ((1, here), (2, there), (3, there)))
-    o_first, q = lax.optimization_barrier((o_first, q))
+    wo, wo_x, wo_y, there, q = lax.optimization_barrier((wo, wo_x, wo_y, there, q))
+    wo_xy, = swap((wo_x,), 'cp', groups, 2)
+    near = swap((wo, wo_x, wo_y), 'cp', groups, 1)
     o_last = attend_rest(q, pre, suf, state, c2, 'cp', 1)
-    wo_x, o_last = lax.optimization_barrier((wo_x, o_last))
-    wo_cross = swap(wo_x, 'cp', groups, 1)
-    return (here,) + o_got, o_last, wo_z + wo_x + wo_near + wo_cross
+    wo_xy, o_last = lax.optimization_barrier((wo_xy, o_last))
+    return (here,) + o_got, o_last, (wo, wo_x, wo_y, wo_xy) + near + swap((wo_xy,), 'cp', groups, 1)
 
 
 MESH = pl.DeviceIdType.MESH
 DOT_N = 512
-MID_PLAN = ((), (('r2', -1), ('ha', 1), ('O', 3), ('xa', -2),), (('r4', -1),), (('xc', -2),), (('hb', 1),), (('xb', -1),), (('r1', 0), ('hc', 1), ('r3', 0),))
-END_PLAN = ((('f', -2), ('hw', 0), ('O', 3),), (), (), (), (), (), ())
-AHEAD, BEHIND = 3, 2
+MID_PLAN = ((('r3', -1),), (('xc', -3), ('r2', -1), ('hb', 1), ('ha', 1),), (('xb', -2), ('xa', -2),), (('O', 3),), (('r4', -1),), (), (('hc', 1), ('r1', 0),))
+END_PLAN = ((('hw', 0), ('f', -2),), (('O', 3),), (), (), (), (), ())
+AHEAD, BEHIND = 3, 3
 
 
 def side_of(z):
@@ -422,8 +427,8 @@
 
 
 def line_kernel(*refs, nc):
-    o_first, o_ref, x_ref, wo_ref, *refs = refs[:4], *refs[4:]
-    wo_pieces, refs = refs[:12], refs[12:]
+    o_first, o_last, x_ref, wo_ref, *refs = refs[:4], refs[4:6], *refs[6:]
+    wo_pieces, refs = refs[:8], refs[8:]
     wg_ref, wu_ref, wd_ref, gain_ref, xout_ref, land_ref = refs[:6]
     (obuf, h2, ybuf, ring, psum, act, stage, xs, xo, sstat, rstat,
      ring_sem, loc_sem, o_send, o_recv, st_send, st_recv, a1_send, a1_recv, rs_send, rs_recv, a2_send, a2_recv) = refs[6:]
@@ -431,7 +436,7 @@
     depth = wg_ref.shape[0]
     ff = wg_ref.shape[1]
     half = depth // 2
-    width = o_ref.shape[-1]
+    width = o_last[0].shape[-1]
     kz = 2 * width
     n_ct = half // DOT_N
     nd, ne = ff // PAIR, depth // DOT_N
@@ -441,7 +446,8 @@
 
     z = lax.axis_index('tp')
     dp = lax.axis_index('dp')
-    core = lax.rem(lax.axis_index('cp'), 2)
+    cp = lax.axis_index('cp')
+    core, chip = lax.rem(cp, 2), lax.div(cp, 2)
     side, q = side_of(z), colhalf_of(z)
     is_mid = q == 1
     is_end = q != 1
@@ -491,13 +497,12 @@
                         cs = tile(q * n_ct + ct, DOT_N)
                         start(wo_ref.at[:, cs], ring.at[slot, tile(ct, kz), :])
                     else:
-                        for dpx in range(2):
-                            for cx in range(2):
-                                piece = wo_pieces[(dpx + 2 * cx) * 3 + d - 1]
-                                n = piece.shape[0]
-                                j = (dp + dpx - 2 * dp * dpx) * 2 + (core + cx - 2 * core * cx)
-                                r0 = pl.multiple_of(ct * kz + j * n, n)
-                                start(piece.at[:, pl.ds(c0, DOT_N)], ring.at[slot, pl.ds(r0, n), :])
+                        for k, piece in enumerate(wo_pieces):
+                            bits = (dp, k % 2), (chip, k // 2 % 2), (core, k // 4)
+                            n = piece.shape[1]
+                            j = sum((own + x - 2 * own * x) * w for (own, x), w in zip(bits, (4, 2, 1)))
+                            r0 = pl.multiple_of(ct * kz + j * n, n)
+                            start(piece.at[d - 1, :, pl.ds(c0, DOT_N)], ring.at[slot, pl.ds(r0, n), :])
 
         @pl.when((t >= 4) & (t < 4 + nd))
         def _():
@@ -521,14 +526,14 @@
         return obuf.at[c, d, :, tile(1, width)]
 
     def o_copy(c, d):
-        return rdma(o_ref.at[side_of(peers[d]), tile(c, H), :], late(c, d), o_send.at[c, d - 1], o_recv.at[c, d - 1], peers[d])
+        return rdma(o_last[int(d > 1)].at[tile(c, H), :], late(c, d), o_send.at[c, d - 1], o_recv.at[c, d - 1], peers[d])
 
     def o_start(c):
         for d in (1, 2, 3):
             o_copy(c, d).start()
 
     def project(c, ld0):
-        own_o = pltpu.make_async_copy(o_ref.at[side, tile(c, H), :], late(c, 0), loc_sem.at[0])
+        own_o = pltpu.make_async_copy(o_last[0].at[tile(c, H), :], late(c, 0), loc_sem.at[0])
         own_x = pltpu.make_async_copy(x_ref.at[tile(c * 2 + side, H), cols_at(z)], xs, loc_sem.at[1])
         own_o.start()
         own_x.start()
@@ -778,7 +783,7 @@
 def line_block(o_first, o_last, x, w_out, pieces, w_gate, w_up, w_down, gain):
     rows, depth = x.shape
     ff = w_gate.shape[1]
-    width = o_last.shape[-1]
+    width = o_last[0].shape[-1]
     kz = 2 * width
     nc = rows // ROWS_CH
     h, half = ROWS_CH // 2, depth // 2
@@ -786,7 +791,7 @@
     sems = [pltpu.SemaphoreType.DMA((nc, n)) for n in (3, 3, 1, 1, 5, 3, 3, 5, 5, 3)]
     xout, _ = pl.pallas_call(
         functools.partial(line_kernel, nc=nc),
-        in_specs=[HBM] * (10 + len(pieces)) + [VMEM],
+        in_specs=[HBM] * (11 + len(pieces)) + [VMEM],
         out_specs=[HBM] * 2,
         out_shape=[struct(x.shape, BF16), struct((nc, 5, h, half), F32)],
         scratch_shapes=[
@@ -798,17 +803,25 @@
         compiler_params=params(60, collective_id=1, has_side_effects=True),
         cost_estimate=cost(6 * x.size * ff, 2 * x.size),
         name="line_block",
-    )(*(a.reshape(nc, h, width) for a in o_first), o_last, x, w_out, *pieces, w_gate, w_up, w_down, gain.reshape(1, depth))
+    )(*(a.reshape(nc, h, width) for a in o_first), *o_last, x, w_out, *pieces, w_gate, w_up, w_down, gain.reshape(1, depth))
     return xout
 
 
+def copy_kernel(src_ref, dst_ref):
+    dst_ref[...] = src_ref[...]
+
+
+def copied(x):
+    spec = pl.BlockSpec((LANES, x.shape[1]), lambda i: (i, 0))
+    return pl.pallas_call(copy_kernel, grid=(x.shape[0] // LANES,), in_specs=[spec], out_specs=spec, out_shape=struct(x.shape, x.dtype), name="copied")(x)
+
+
 def gather_w_out(w_out, tps):
-    z, dp, core = lax.axis_index('tp'), lax.axis_index('dp'), lax.axis_index('cp') % 2
-    n, half = w_out.shape[0] // 4, w_out.shape[1] // 2
+    z, dp, cp = (lax.axis_index(a) for a in ('tp', 'dp', 'cp'))
+    n, half = w_out.shape[0] // 8, w_out.shape[1] // 2
     q = (z + 1) // 2 % 2
-    quarter = lax.dynamic_slice_in_dim(w_out, (dp * 2 + core) * n, n, 0)
-    same = lax.dynamic_slice_in_dim(quarter, q * half, half, 1)
-    other = lax.dynamic_slice_in_dim(quarter, (1 - q) * half, half, 1)
+    part = lax.dynamic_slice_in_dim(w_out, (dp * 4 + cp) * n, n, 0)
+    same, other = (lax.dynamic_slice_in_dim(part, h * half, half, 1) for h in (q, 1 - q))
     return tuple(lax.ppermute(a, 'tp', [(i, i ^ d) for i in range(tps)]) for d, a in ((1, other), (2, other), (3, same)))
 
 
@@ -834,6 +847,7 @@
         near_suf = swap(own_suf, 'cp', groups, 1)
         o_first, o_last, wo_pieces = attend(q, own_pre, near_pre, far_pre, own_suf, near_suf, far_suf, wo_z, c2, groups, tps, dps)
         x_out = line_block(o_first, o_last, x_loc, w_out, wo_pieces, w_gate, w_up, w_down, norm_mlp)
+        x_out = copied(x_out)
         return x_out, k_flat.reshape(rows, kv_loc, head_dim), v_flat.reshape(rows, kv_loc, head_dim)
 
     row_spec = P(('dp', 'cp'), None)

time: 763 us -> 725 us (0.950)
  waiting for transfers between devices: 79.4 us -> 53.3 us
  local copies, waits for them, and re-layouts: 32.9 us -> 15.2 us
    ppermute x3, waiting for transfers between devices: 20.2 us -> 0.01 us  [gather_w_out(): lax.ppermute(a, 'tp', [(i, i ^ d) for i in range(tps)])]
    unnamed x45 -> x28, local copies, waits for them, and re-layouts: 27 us -> 7.24 us
    pallas_call x0 -> x1, Pallas kernels: none -> 8.96 us  [copied(): pl.pallas_call(copy_kernel, grid=(x.shape[0] // LANES,), in_specs=[spec],...]
    ppermute x21 -> x19, waiting for transfers between devices: 21.1 us -> 22 us  [swap(): lax.ppermute(a, axis, [(i, i ^ bit) for i in range(groups)])]
  transfers between devices with their start and end apart: 27 -> 25, of which waited for: 8 -> 6; matrix products, arithmetic and copies ran while one was open for 1% -> 2% of each run, Pallas kernels for 18% -> 19%
where the time goes in v4:
time: 725 us; the launch traced here: 723 us
  Pallas kernels  604 us (83%)
  waiting for transfers between devices  53.3 us (7%)
  starting transfers between devices  43.4 us (6%)
  local copies, waits for them, and re-layouts  15.2 us (2%)
    pallas_call x1, Pallas kernels, line_block(): pl.pallas_call(functools.partial(line_kernel, nc=nc), in_specs=[HBM] * (1...  459 us
    pallas_call x2, Pallas kernels, attend_rest(): pl.pallas_call(functools.partial(rest_kernel, group=group, groups=groups,...  63.9 us
    pallas_call x1, Pallas kernels, attend_prefix(): pl.pallas_call(functools.partial(prefix_kernel, heads=heads, c2=c2), in_s...  44.1 us
    ppermute x3, waiting for transfers between devices, attend(): lax.ppermute(a, 'tp', [(i, i ^ d) for i in range(tps)])  31.3 us
    pallas_call x1, Pallas kernels, qkv(): pl.pallas_call(functools.partial(qkv_kernel, nq=nq), grid=(nq + 2,), in_s...  28.2 us
    ppermute x3, starting transfers between devices, attend(): lax.ppermute(a, 'tp', [(i, i ^ d) for i in range(tps)])  26.5 us
    ppermute x19, waiting for transfers between devices, swap(): lax.ppermute(a, axis, [(i, i ^ bit) for i in range(groups)])  22 us
  transfers between devices with their start and end apart: 25, of which 6 were waited for; matrix products, arithmetic and copies ran while one was open for 2% of the time, Pallas kernels for 19%

profile of v4, /device:TPU:0, one launch (start us, length us, event | category | flops | bytes accessed | tf_op | source)
XLA Modules:
  0.0 723.1 jit_solution(14067656022379422275)
XLA Ops:
  0.7 2.9 fusion.6
  3.5 4.1 collective-permute-start.7
  7.6 1.6 collective-permute-start.6
  9.2 0.8 copy.16
  10.1 1.4 copy.18
  12.6 1.9 fusion
  14.5 1.3 pad_maximum_fusion.1
  15.8 28.2 %qkv.1 = (bf16[1024,1024]{1,0:T(8,128)(2,1)}, bf16[2,1024,128]{2,1,0:T(8,128)(2,1)}, bf16[2,128,1024]{2,1,0:T(8,128)(2,1)}, bf16[1024,256]{1,0:T(8,128)(2,1)}, bf16[1024,256]{1,0:T(8,128)(2,1)}) custom-call(bf16[1024,4096]{1,0:T(8,128)(2,1)} %refs_6_.1, bf16[1,4096]{1,0:T(2,128)(2,1)} %reshape.53.g_ref, bf16[4096,1024]{1,0:T(8,128)(2,1)} %wq_ref.1, ...), custom_call_target="tpu_custom_call" | custom-call | flops 12884901888 | bytes 8388608 | tf_op jit(solution)/shard_map/qkv/pallas_call | solution.py:124
  44.1 1.8 collective-permute-start.3
  46.2 1.8 collective-permute-start.4
  48.3 1.6 copy-done.3
  49.9 44.1 %attend_prefix.1 = (f32[16,128,512]{2,1,0:T(8,128)}, f32[16,1,512]{2,1,0:T(1,128)}, f32[16,8,512]{2,1,0:T(8,128)}) custom-call(bf16[1024,1024]{1,0:T(8,128)(2,1)S(1)} %copy-done.3, bf16[2,2048,128]{2,1,0:T(8,128)(2,1)S(1)} %bitcast.18, bf16[2,128,2048]{2,1,0:T(8,128)(2,1)S(1)} %bitcast.13, bf16[2,2048,128]{2,1,0:T(8,128)(2,1)} %collective-permute-done.kb.refs_3_, ...), custom_call_target="tpu_custom_call" | custom-call | flops 17179869184 | bytes 4194304 | tf_op jit(solution)/shard_map/attend_prefix/pallas_call | solution.py:238
  94.0 9.8 %collective-permute-done.4.refs_13_ = bf16[2,1024,128]{2,1,0:T(8,128)(2,1)S(1)} collective-permute-done((bf16[2,1024,128]{2,1,0:T(8,128)(2,1)}, bf16[2,1024,128]{2,1,0:T(8,128)(2,1)S(1)}, u32[]{:S(2)}, u32[]{:S(2)}) %collective-permute-start.4) | collective-permute-done | bytes 524320 | tf_op jit(solution)/shard_map/ppermute | solution.py:392
  103.9 10.3 %collective-permute-done.5.refs_14_ = bf16[2,128,1024]{2,1,0:T(8,128)(2,1)S(1)} collective-permute-done((bf16[2,128,1024]{2,1,0:T(8,128)(2,1)}, bf16[2,128,1024]{2,1,0:T(8,128)(2,1)S(1)}, u32[]{:S(2)}, u32[]{:S(2)}) %collective-permute-start.5) | collective-permute-done | bytes 524320 | tf_op jit(solution)/shard_map/ppermute | solution.py:392
  115.3 2.7 pad_maximum_fusion.refs_8_
  118.0 1.1 collective-permute-done.12.refs_12_
  119.1 1.7 collective-permute-start.19
  120.8 1.5 collective-permute-start.18
  122.4 2.2 copy-done.2
  124.6 32.0 %attend_rest.2 = (bf16[512,512]{1,0:T(8,128)(2,1)}, bf16[512,512]{1,0:T(8,128)(2,1)}) custom-call(bf16[1024,1024]{1,0:T(8,128)(2,1)S(1)} %copy-done.3, bf16[2,2048,128]{2,1,0:T(8,128)(2,1)S(1)} %bitcast.19, bf16[2,128,2048]{2,1,0:T(8,128)(2,1)S(1)} %bitcast.14, bf16[2,2048,128]{2,1,0:T(8,128)(2,1)} %collective-permute-done.kb.refs_3_, ...), custom_call_target="tpu_custom_call" | custom-call | flops 12884901888 | bytes 4194304 | tf_op jit(solution)/shard_map/attend_rest/pallas_call | solution.py:375
  157.3 1.0 collective-permute-start.20
  158.3 9.9 %collective-permute-start.15 = (bf16[512,512]{1,0:T(8,128)(2,1)}, bf16[512,512]{1,0:T(8,128)(2,1)S(1)}, u32[]{:S(2)}, u32[]{:S(2)}) collective-permute-start(bf16[512,512]{1,0:T(8,128)(2,1)} %get-tuple-element.46), channel_id=1, source_target_pairs={{0,4},{4,0},{8,12},{12,8},{1,5},{5,1},{9,13},{13,9},{2,6},{6,2},{1... | collective-permute-start | bytes 1572872 | tf_op jit(solution)/shard_map/ppermute | solution.py:405
  168.8 31.9 %attend_rest.3 = (bf16[512,512]{1,0:T(8,128)(2,1)}, bf16[512,512]{1,0:T(8,128)(2,1)}) custom-call(bf16[1024,1024]{1,0:T(8,128)(2,1)S(1)} %copy-done.3, bf16[2,2048,128]{2,1,0:T(8,128)(2,1)S(1)} %bitcast.20, bf16[2,128,2048]{2,1,0:T(8,128)(2,1)S(1)} %bitcast.15, bf16[2,2048,128]{2,1,0:T(8,128)(2,1)} %collective-permute-done.kb.refs_3_, ...), custom_call_target="tpu_custom_call" | custom-call | flops 12884901888 | bytes 4194304 | tf_op jit(solution)/shard_map/attend_rest/pallas_call | solution.py:375
  201.2 3.4 collective-permute-start.17
  204.6 12.7 %collective-permute-done.17 = bf16[512,512]{1,0:T(8,128)(2,1)S(1)} collective-permute-done((bf16[512,512]{1,0:T(8,128)(2,1)}, bf16[512,512]{1,0:T(8,128)(2,1)S(1)}, u32[]{:S(2)}, u32[]{:S(2)}) %collective-permute-start.17) | collective-permute-done | bytes 524320 | tf_op jit(solution)/shard_map/ppermute | solution.py:405
  217.3 13.3 %collective-permute-start.16 = (bf16[512,512]{1,0:T(8,128)(2,1)}, bf16[512,512]{1,0:T(8,128)(2,1)S(1)}, u32[]{:S(2)}, u32[]{:S(2)}) collective-permute-start(bf16[512,512]{1,0:T(8,128)(2,1)} %get-tuple-element.47), channel_id=1, source_target_pairs={{0,8},{4,12},{8,0},{12,4},{1,9},{5,13},{9,1},{13,5},{2,10},{6,14},... | collective-permute-start | bytes 1572872 | tf_op jit(solution)/shard_map/ppermute | solution.py:405
  231.2 2.0 reshape.59
  233.1 2.0 reshape.60
  235.1 18.6 %collective-permute-done.16 = bf16[512,512]{1,0:T(8,128)(2,1)S(1)} collective-permute-done((bf16[512,512]{1,0:T(8,128)(2,1)}, bf16[512,512]{1,0:T(8,128)(2,1)S(1)}, u32[]{:S(2)}, u32[]{:S(2)}) %collective-permute-start.16) | collective-permute-done | bytes 524320 | tf_op jit(solution)/shard_map/ppermute | solution.py:405
  253.8 0.8 copy-done.12
  255.0 459.1 %line_block.1 = (bf16[1024,4096]{1,0:T(8,128)(2,1)}, f32[8,5,64,2048]{3,2,1,0:T(8,128)}) custom-call(bf16[8,64,512]{2,1,0:T(8,128)(2,1)} %bitcast.21, bf16[8,64,512]{2,1,0:T(8,128)(2,1)} %bitcast.22, bf16[8,64,512]{2,1,0:T(8,128)(2,1)} %bitcast.24, bf16[8,64,512]{2,1,0:T(8,128)(2,1)} %bitcast.23, bf16[512,512]{1,0:T(8,128)(2,1)} %get-tuple-element.55.refs_4_, ...), custom_call_target="tpu_custom_call" | custom-call | flops 90194313216 | bytes 8388608 | tf_op jit(solution)/shard_map/line_block/pallas_call | solution.py:792
  714.1 9.0 %copied.1 = bf16[1024,4096]{1,0:T(8,128)(2,1)} custom-call(bf16[1024,4096]{1,0:T(8,128)(2,1)} %get-tuple-element.60.src_ref), custom_call_target="tpu_custom_call" | custom-call | tf_op jit(solution)/shard_map/copied/pallas_call | solution.py:816
  (62 shorter events, 6.0 us)
Async XLA Ops:
  3.5 42.3 %collective-permute-start.7 = (bf16[128,2048]{1,0:T(8,128)(2,1)}, bf16[128,2048]{1,0:T(8,128)(2,1)}, u32[]{:S(2)}, u32[]{:S(2)}) collective-permute-start(bf16[128,2048]{1,0:T(8,128)(2,1)} %get-tuple-element.64), channel_id=1, source_target_pairs={{0,8},{4,12},{8,0},{12,4},{1,9},{5,13},{9,1},{13,5},{2,10},{6,14},... | collective-permute-start | bytes 1572872 | tf_op jit(solution)/shard_map/ppermute | solution.py:825
  7.6 38.6 %collective-permute-start.6 = (bf16[128,2048]{1,0:T(8,128)(2,1)}, bf16[128,2048]{1,0:T(8,128)(2,1)}, u32[]{:S(2)}, u32[]{:S(2)}) collective-permute-start(bf16[128,2048]{1,0:T(8,128)(2,1)} %get-tuple-element.64), channel_id=1, source_target_pairs={{0,4},{4,0},{8,12},{12,8},{1,5},{5,1},{9,13},{13,9},{2,6},{6,2},{1... | collective-permute-start | bytes 1572872 | tf_op jit(solution)/shard_map/ppermute | solution.py:825
  9.2 34.9 %collective-permute-start.8 = (bf16[128,2048]{1,0:T(8,128)(2,1)}, bf16[128,2048]{1,0:T(8,128)(2,1)}, u32[]{:S(2)}, u32[]{:S(2)}) collective-permute-start(bf16[128,2048]{1,0:T(8,128)(2,1)} %get-tuple-element.63), channel_id=1, source_target_pairs={{0,12},{4,8},{8,4},{12,0},{1,13},{5,9},{9,5},{13,1},{2,14},{6,10},... | collective-permute-start | bytes 1572872 | tf_op jit(solution)/shard_map/ppermute | solution.py:825
  10.0 36.2 %collective-permute-start.1 = (bf16[2,128,2048]{2,1,0:T(8,128)(2,1)S(1)}, bf16[2,128,2048]{2,1,0:T(8,128)(2,1)S(1)}, u32[]{:S(2)}, u32[]{:S(2)}) collective-permute-start(bf16[2,128,2048]{2,1,0:T(8,128)(2,1)S(1)} %bitcast.11), channel_id=1, source_target_pairs={{0,1},{1,0},{2,3},{3,2},{4,5},{5,4},{6,7},{7,6},{8,9},{9,8},{10,11... | collective-permute-start | bytes 3145736 | tf_op jit(solution)/shard_map/ppermute | solution.py:392
  11.4 36.5 %collective-permute-start = (bf16[2,2048,128]{2,1,0:T(8,128)(2,1)S(1)}, bf16[2,2048,128]{2,1,0:T(8,128)(2,1)}, u32[]{:S(2)}, u32[]{:S(2)}) collective-permute-start(bf16[2,2048,128]{2,1,0:T(8,128)(2,1)S(1)} %bitcast.16), channel_id=1, source_target_pairs={{0,1},{1,0},{2,3},{3,2},{4,5},{5,4},{6,7},{7,6},{8,9},{9,8},{10,11... | collective-permute-start | bytes 3145736 | tf_op jit(solution)/shard_map/ppermute | solution.py:392
  44.1 70.1 %collective-permute-start.3 = (bf16[2,128,2048]{2,1,0:T(8,128)(2,1)S(1)}, bf16[2,128,2048]{2,1,0:T(8,128)(2,1)S(1)}, u32[]{:S(2)}, u32[]{:S(2)}) collective-permute-start(bf16[2,128,2048]{2,1,0:T(8,128)(2,1)S(1)} %bitcast.12), channel_id=1, source_target_pairs={{0,2},{1,3},{2,0},{3,1},{4,6},{5,7},{6,4},{7,5},{8,10},{9,11},{10,... | collective-permute-start | bytes 3145736 | tf_op jit(solution)/shard_map/ppermute | solution.py:392
  45.9 68.3 %collective-permute-start.2 = (bf16[2,2048,128]{2,1,0:T(8,128)(2,1)S(1)}, bf16[2,2048,128]{2,1,0:T(8,128)(2,1)S(1)}, u32[]{:S(2)}, u32[]{:S(2)}) collective-permute-start(bf16[2,2048,128]{2,1,0:T(8,128)(2,1)S(1)} %bitcast.17), channel_id=1, source_target_pairs={{0,2},{1,3},{2,0},{3,1},{4,6},{5,7},{6,4},{7,5},{8,10},{9,11},{10,... | collective-permute-start | bytes 3145736 | tf_op jit(solution)/shard_map/ppermute | solution.py:392
  46.2 69.0 %collective-permute-start.11 = (bf16[2,1024,128]{2,1,0:T(8,128)(2,1)}, bf16[2,1024,128]{2,1,0:T(8,128)(2,1)S(1)}, u32[]{:S(2)}, u32[]{:S(2)}) collective-permute-start(bf16[2,1024,128]{2,1,0:T(8,128)(2,1)} %get-tuple-element.34.refs_9_), channel_id=1, source_target_pairs={{0,1},{1,0},{2,3},{3,2},{4,5},{5,4},{6,7},{7,6},{8,9},{9,8},{10,11... | collective-permute-start | bytes 1572872 | tf_op jit(solution)/shard_map/ppermute | solution.py:392
  46.2 57.7 %collective-permute-start.4 = (bf16[2,1024,128]{2,1,0:T(8,128)(2,1)}, bf16[2,1024,128]{2,1,0:T(8,128)(2,1)S(1)}, u32[]{:S(2)}, u32[]{:S(2)}) collective-permute-start(bf16[2,1024,128]{2,1,0:T(8,128)(2,1)} %get-tuple-element.34.refs_9_), channel_id=1, source_target_pairs={{0,2},{1,3},{2,0},{3,1},{4,6},{5,7},{6,4},{7,5},{8,10},{9,11},{10,... | collective-permute-start | bytes 1572872 | tf_op jit(solution)/shard_map/ppermute | solution.py:392
  48.0 66.2 %collective-permute-start.5 = (bf16[2,128,1024]{2,1,0:T(8,128)(2,1)}, bf16[2,128,1024]{2,1,0:T(8,128)(2,1)S(1)}, u32[]{:S(2)}, u32[]{:S(2)}) collective-permute-start(bf16[2,128,1024]{2,1,0:T(8,128)(2,1)} %get-tuple-element.35.refs_10_), channel_id=1, source_target_pairs={{0,2},{1,3},{2,0},{3,1},{4,6},{5,7},{6,4},{7,5},{8,10},{9,11},{10,... | collective-permute-start | bytes 1572872 | tf_op jit(solution)/shard_map/ppermute | solution.py:392
  49.9 64.8 %copy-start.1 = (bf16[2,128,1024]{2,1,0:T(8,128)(2,1)S(1)}, bf16[2,128,1024]{2,1,0:T(8,128)(2,1)}, u32[]{:S(2)}) copy-start(bf16[2,128,1024]{2,1,0:T(8,128)(2,1)} %get-tuple-element.35.refs_10_) | copy-start | bytes 1572868
  94.0 28.3 %copy-start = (bf16[2,1024,128]{2,1,0:T(8,128)(2,1)S(1)}, bf16[2,1024,128]{2,1,0:T(8,128)(2,1)}, u32[]{:S(2)}) copy-start(bf16[2,1024,128]{2,1,0:T(8,128)(2,1)} %get-tuple-element.34.refs_9_) | copy-start | bytes 1572868
  94.0 28.3 %copy-start.4 = (f32[16,8,512]{2,1,0:T(8,128)S(1)}, f32[16,8,512]{2,1,0:T(8,128)}, u32[]{:S(2)}) copy-start(f32[16,8,512]{2,1,0:T(8,128)} %get-tuple-element.45.refs_19_) | copy-start | bytes 786436
  94.0 28.3 %copy-start.5 = (f32[16,1,512]{2,1,0:T(1,128)S(1)}, f32[16,1,512]{2,1,0:T(1,128)}, u32[]{:S(2)}) copy-start(f32[16,1,512]{2,1,0:T(1,128)} %get-tuple-element.44.refs_18_) | copy-start | bytes 98308
  114.2 8.1 %collective-permute-start.9 = (bf16[2,2048,128]{2,1,0:T(8,128)(2,1)S(1)}, bf16[2,2048,128]{2,1,0:T(8,128)(2,1)S(1)}, u32[]{:S(2)}, u32[]{:S(2)}) collective-permute-start(bf16[2,2048,128]{2,1,0:T(8,128)(2,1)S(1)} %collective-permute-done.2.refs_5_), channel_id=1, source_target_pairs={{0,1},{1,0},{2,3},{3,2},{4,5},{5,4},{6,7},{7,6},{8,9},{9,8},{10,11... | collective-permute-start | bytes 3145736 | tf_op jit(solution)/shard_map/ppermute | solution.py:392
  114.2 8.1 %collective-permute-start.10 = (bf16[2,128,2048]{2,1,0:T(8,128)(2,1)S(1)}, bf16[2,128,2048]{2,1,0:T(8,128)(2,1)S(1)}, u32[]{:S(2)}, u32[]{:S(2)}) collective-permute-start(bf16[2,128,2048]{2,1,0:T(8,128)(2,1)S(1)} %collective-permute-done.3.refs_6_), channel_id=1, source_target_pairs={{0,1},{1,0},{2,3},{3,2},{4,5},{5,4},{6,7},{7,6},{8,9},{9,8},{10,11... | collective-permute-start | bytes 3145736 | tf_op jit(solution)/shard_map/ppermute | solution.py:392
  114.7 4.4 collective-permute-start.12
  114.8 6.1 collective-permute-start.13
  115.2 7.1 collective-permute-start.14
  119.1 37.5 %collective-permute-start.19 = (bf16[3,128,2048]{2,1,0:T(8,128)(2,1)}, bf16[3,128,2048]{2,1,0:T(8,128)(2,1)}, u32[]{:S(2)}, u32[]{:S(2)}) collective-permute-start(bf16[3,128,2048]{2,1,0:T(8,128)(2,1)} %pad_maximum_fusion.refs_8_), channel_id=1, source_target_pairs={{0,2},{1,3},{2,0},{3,1},{4,6},{5,7},{6,4},{7,5},{8,10},{9,11},{10,... | collective-permute-start | bytes 4718600 | tf_op jit(solution)/shard_map/ppermute | solution.py:392
  120.8 36.5 %collective-permute-start.18 = (bf16[3,128,2048]{2,1,0:T(8,128)(2,1)}, bf16[3,128,2048]{2,1,0:T(8,128)(2,1)}, u32[]{:S(2)}, u32[]{:S(2)}) collective-permute-start(bf16[3,128,2048]{2,1,0:T(8,128)(2,1)} %pad_maximum_fusion.refs_8_), channel_id=1, source_target_pairs={{0,16},{16,0},{1,17},{17,1},{2,18},{18,2},{3,19},{19,3},{4,20},{20... | collective-permute-start | bytes 4718600 | tf_op jit(solution)/shard_map/ppermute | solution.py:392
  157.3 43.3 %collective-permute-start.20 = (bf16[3,128,2048]{2,1,0:T(8,128)(2,1)}, bf16[3,128,2048]{2,1,0:T(8,128)(2,1)}, u32[]{:S(2)}, u32[]{:S(2)}) collective-permute-start(bf16[3,128,2048]{2,1,0:T(8,128)(2,1)} %collective-permute-done.18.refs_9_), channel_id=1, source_target_pairs={{0,2},{1,3},{2,0},{3,1},{4,6},{5,7},{6,4},{7,5},{8,10},{9,11},{10,... | collective-permute-start | bytes 4718600 | tf_op jit(solution)/shard_map/ppermute | solution.py:392
  158.3 72.2 %copy-start.8 = (bf16[4096]{0:T(1024)(128)(2,1)S(1)}, bf16[4096]{0:T(1024)(128)(2,1)}, u32[]{:S(2)}) copy-start(bf16[4096]{0:T(1024)(128)(2,1)} %param.20) | copy-start | bytes 24580
  158.3 42.9 %collective-permute-start.15 = (bf16[512,512]{1,0:T(8,128)(2,1)}, bf16[512,512]{1,0:T(8,128)(2,1)S(1)}, u32[]{:S(2)}, u32[]{:S(2)}) collective-permute-start(bf16[512,512]{1,0:T(8,128)(2,1)} %get-tuple-element.46), channel_id=1, source_target_pairs={{0,4},{4,0},{8,12},{12,8},{1,5},{5,1},{9,13},{13,9},{2,6},{6,2},{1... | collective-permute-start | bytes 1572872 | tf_op jit(solution)/shard_map/ppermute | solution.py:405
  168.2 85.5 %collective-permute-start.22 = (bf16[3,128,2048]{2,1,0:T(8,128)(2,1)}, bf16[3,128,2048]{2,1,0:T(8,128)(2,1)}, u32[]{:S(2)}, u32[]{:S(2)}) collective-permute-start(bf16[3,128,2048]{2,1,0:T(8,128)(2,1)} %collective-permute-done.18.refs_9_), channel_id=1, source_target_pairs={{0,1},{1,0},{2,3},{3,2},{4,5},{5,4},{6,7},{7,6},{8,9},{9,8},{10,11... | collective-permute-start | bytes 4718600 | tf_op jit(solution)/shard_map/ppermute | solution.py:392
  168.2 85.5 %collective-permute-start.21 = (bf16[3,128,2048]{2,1,0:T(8,128)(2,1)}, bf16[3,128,2048]{2,1,0:T(8,128)(2,1)}, u32[]{:S(2)}, u32[]{:S(2)}) collective-permute-start(bf16[3,128,2048]{2,1,0:T(8,128)(2,1)} %pad_maximum_fusion.refs_8_), channel_id=1, source_target_pairs={{0,1},{1,0},{2,3},{3,2},{4,5},{5,4},{6,7},{7,6},{8,9},{9,8},{10,11... | collective-permute-start | bytes 4718600 | tf_op jit(solution)/shard_map/ppermute | solution.py:392
  168.7 85.0 %collective-permute-start.23 = (bf16[3,128,2048]{2,1,0:T(8,128)(2,1)}, bf16[3,128,2048]{2,1,0:T(8,128)(2,1)}, u32[]{:S(2)}, u32[]{:S(2)}) collective-permute-start(bf16[3,128,2048]{2,1,0:T(8,128)(2,1)} %collective-permute-done.19.refs_10_), channel_id=1, source_target_pairs={{0,1},{1,0},{2,3},{3,2},{4,5},{5,4},{6,7},{7,6},{8,9},{9,8},{10,11... | collective-permute-start | bytes 4718600 | tf_op jit(solution)/shard_map/ppermute | solution.py:392
  200.7 53.1 %collective-permute-start.24 = (bf16[3,128,2048]{2,1,0:T(8,128)(2,1)}, bf16[3,128,2048]{2,1,0:T(8,128)(2,1)S(1)}, u32[]{:S(2)}, u32[]{:S(2)}) collective-permute-start(bf16[3,128,2048]{2,1,0:T(8,128)(2,1)} %collective-permute-done.20.refs_11_), channel_id=1, source_target_pairs={{0,1},{1,0},{2,3},{3,2},{4,5},{5,4},{6,7},{7,6},{8,9},{9,8},{10,11... | collective-permute-start | bytes 4718600 | tf_op jit(solution)/shard_map/ppermute | solution.py:392
  201.2 29.9 %copy-start.10 = (bf16[512,512]{1,0:T(8,128)(2,1)}, bf16[512,512]{1,0:T(8,128)(2,1)S(1)}, u32[]{:S(2)}) copy-start(bf16[512,512]{1,0:T(8,128)(2,1)S(1)} %collective-permute-done.15) | copy-start | bytes 1572868
  201.2 16.0 %collective-permute-start.17 = (bf16[512,512]{1,0:T(8,128)(2,1)}, bf16[512,512]{1,0:T(8,128)(2,1)S(1)}, u32[]{:S(2)}, u32[]{:S(2)}) collective-permute-start(bf16[512,512]{1,0:T(8,128)(2,1)} %get-tuple-element.47), channel_id=1, source_target_pairs={{0,12},{4,8},{8,4},{12,0},{1,13},{5,9},{9,5},{13,1},{2,14},{6,10},... | collective-permute-start | bytes 1572872 | tf_op jit(solution)/shard_map/ppermute | solution.py:405
  217.3 36.5 %copy-start.11 = (bf16[512,512]{1,0:T(8,128)(2,1)}, bf16[512,512]{1,0:T(8,128)(2,1)S(1)}, u32[]{:S(2)}) copy-start(bf16[512,512]{1,0:T(8,128)(2,1)S(1)} %collective-permute-done.17) | copy-start | bytes 1572868
  217.3 36.4 %collective-permute-start.16 = (bf16[512,512]{1,0:T(8,128)(2,1)}, bf16[512,512]{1,0:T(8,128)(2,1)S(1)}, u32[]{:S(2)}, u32[]{:S(2)}) collective-permute-start(bf16[512,512]{1,0:T(8,128)(2,1)} %get-tuple-element.47), channel_id=1, source_target_pairs={{0,8},{4,12},{8,0},{12,4},{1,9},{5,13},{9,1},{13,5},{2,10},{6,14},... | collective-permute-start | bytes 1572872 | tf_op jit(solution)/shard_map/ppermute | solution.py:405
  (6 other events, 17.3 us)

commit v5 on v4

--- a/solution.py
+++ b/solution.py
@@ -52,7 +52,7 @@
     return jnp.concatenate([cos_tab, cos_tab], axis=1), jnp.concatenate([-sin_tab, sin_tab], axis=1)
 
 
-def qkv_kernel(x_hbm, g_ref, wq_ref, wk_ref, wv_ref, cos_ref, sin_ref, q_ref, k_ref, vt_ref, kf_ref, vf_ref, x_ref, h_ref, sems, *, nq):
+def qkv_kernel(x_hbm, g_ref, wq_ref, wk_ref, wv_ref, cos_ref, sin_ref, q_ref, kv_ref, kf_ref, vf_ref, x_ref, h_ref, sems, *, nq):
     step = pl.program_id(0)
     rows = x_ref.shape[0]
     parts, rt = sems.shape[0], 32
@@ -66,7 +66,7 @@
         for i, copy in enumerate(copies):
             copy.wait()
 
-            @pl.loop(i * n // rt, (i + 1) * n // rt)
+            @pl.loop(i * n // rt, (i + 1) * n // rt, unroll=2)
             def _(j):
                 sl = tile(j, rt)
                 xv = x_ref[sl, :].astype(F32)
@@ -95,12 +95,13 @@
     def store_k(acc, sl):
         for t, cs, part in heads_of(acc):
             kf_ref[sl, cs] = rope(part, sl)
-            k_ref[t, sl, :] = kf_ref[sl, cs]
+            kv_ref[0, t, sl, :] = kf_ref[sl, cs]
 
     def store_v(acc, sl):
         vf_ref[sl, :] = acc.astype(BF16)
         for t, _, part in heads_of(acc):
-            vt_ref[t, :, sl] = part.T.astype(BF16)
+            for b in range(mt // LANES):
+                kv_ref[1, t, pl.ds(sl.start + b * LANES, LANES), :] = part[b * LANES:(b + 1) * LANES].T.astype(BF16)
 
     pl.when(step < nq)(lambda: project(wq_ref, store_q))
     pl.when(step == nq)(lambda: project(wk_ref, store_k))
@@ -120,13 +121,13 @@
     def columns(n):
         return pl.BlockSpec((n, PAIR), lambda j: (0, jnp.minimum(j, nq - 1)))
 
-    flat, by_head, by_head_t = (rows, PAIR), (2, rows, LANES), (2, LANES, rows)
+    flat, by_head = (rows, PAIR), (2, 2, rows, LANES)
     return pl.pallas_call(
         functools.partial(qkv_kernel, nq=nq),
         grid=(nq + 2,),
         in_specs=[HBM, whole((1, depth)), columns(depth), fixed(wk.shape), fixed(wv.shape), whole(cos_tab.shape), whole(sin_tab.shape)],
-        out_specs=[columns(rows), fixed(by_head), fixed(by_head_t), fixed(flat), fixed(flat)],
-        out_shape=[struct(s, BF16) for s in ((rows, nq * PAIR), by_head, by_head_t, flat, flat)],
+        out_specs=[columns(rows), fixed(by_head), fixed(flat), fixed(flat)],
+        out_shape=[struct(s, BF16) for s in ((rows, nq * PAIR), by_head, flat, flat)],
         scratch_shapes=[pltpu.VMEM((rows, depth), BF16), pltpu.VMEM((rows, depth), BF16), pltpu.SemaphoreType.DMA((4,))],
         compiler_params=params(56, dimension_semantics=("arbitrary",)),
         cost_estimate=cost(2 * rows * depth * (nq + 2) * PAIR, 2 * depth * rows),
@@ -159,6 +160,10 @@
 
 def q_block(q_ref, head, half):
     return q_ref[tile(half, NQ), tile(head, LANES)]
+
+
+def across(blocks):
+    return jnp.concatenate([blocks[i:i + LANES] for i in range(0, blocks.shape[0], LANES)], axis=1)
 
 
 def attend_items(q_ref, kb_ref, vb_ref, acc_ref, m_ref, l_ref, pbufs, n_items, item, bk, c2, diag=False):
@@ -178,7 +183,7 @@
 
     def values(i, pb):
         head, half, start = item(i)
-        vt = vb_ref[head // PER_KV, :, pl.ds(pl.multiple_of(start, bk), bk)]
+        vt = across(vb_ref[head // PER_KV, pl.ds(pl.multiple_of(start, bk), bk), :])
         acc_ref[head * 2 + half] += jnp.dot(vt, pb[...], preferred_element_type=F32)
 
     scores(0, pbufs[0])
@@ -201,16 +206,17 @@
 def prefix_kernel(q_ref, ka, va, kb, vb, acc_out, m_out, l_out, kbuf, vbuf, acc_ref, m_ref, l_ref, pa, pb, sems, *, heads, c2):
     fetch = Fetch(sems)
     n = ka.shape[1]
-    settle(fetch.start([(ka, kbuf.at[:, tile(0, n), :]), (va, vbuf.at[:, :, tile(0, n)]), (kb, kbuf.at[:, tile(1, n), :]), (vb, vbuf.at[:, :, tile(1, n)])]))
-
-    @each(heads * 2)
-    def _(i):
-        head, half = i // 2, i % 2
-        s = lax.dot_general(kbuf[head // PER_KV, tile(0, LANES), :], q_block(q_ref, head, half), NT, preferred_element_type=F32)
-        m_ref[i] = jnp.max(s, axis=0, keepdims=True) * c2
-        for ref in (acc_ref, l_ref):
-            ref[i] = jnp.zeros(ref.shape[1:], F32)
-
+    settle(fetch.start([(ka, kbuf.at[:, tile(0, n), :]), (va, vbuf.at[:, tile(0, n), :]), (kb, kbuf.at[:, tile(1, n), :]), (vb, vbuf.at[:, tile(1, n), :])]))
+
+    @each(heads // PER_KV)
+    def _(group):
+        for j in range(2 * PER_KV):
+            i = group * 2 * PER_KV + j
+            s = lax.dot_general(kbuf[group, tile(0, LANES), :], q_block(q_ref, i // 2, j % 2), NT, preferred_element_type=F32)
+            m_ref[i] = jnp.max(s, axis=0, keepdims=True) * c2
+
+    for ref in (acc_ref, l_ref):
+        ref[...] = jnp.zeros_like(ref)
     bk = 2 * NQ
     per = kbuf.shape[1] // bk
 
@@ -241,7 +247,7 @@
         out_specs=[HBM] * len(shapes),
         out_shape=[pltpu.HBM(s.shape, s.dtype) for s in shapes],
         scratch_shapes=[
-            pltpu.VMEM((2, n, LANES), BF16), pltpu.VMEM((2, LANES, n), BF16), *vmem_like(shapes),
+            *[pltpu.VMEM((2, n, LANES), BF16)] * 2, *vmem_like(shapes),
             *[pltpu.VMEM((2 * NQ, NQ), BF16)] * 2, pltpu.SemaphoreType.DMA((8,)),
         ],
         compiler_params=params(20),
@@ -252,21 +258,20 @@
 
 def rest_kernel(*refs, group, groups, c2, axis):
     q_hbm, *refs = refs
-    flat, refs = refs[:4 * groups], refs[4 * groups:]
-    pairs = list(zip(flat[::2], flat[1::2]))
-    pre, suf = pairs[:groups], pairs[groups:]
+    flat, suf, refs = refs[:2 * groups], refs[2 * groups:3 * groups], refs[3 * groups:]
+    pre = list(zip(flat[::2], flat[1::2]))
     acc_in, m_in, l_in, here_out, there_out, q_ref, kbuf, vbuf, ksuf, vsuf, acc_ref, m_ref, l_ref, acc_old, l_old, o_ref, bad_ref, sems, wa, wb, pa, pb, pc, pd = refs
     heads = PER_KV
     me = lax.axis_index(axis)
     fetch = Fetch(sems)
     mine = pl.ds(group * heads * 2, heads * 2)
-    n_pre, n_suf = pre[0][0].shape[1], suf[0][0].shape[1]
+    n_pre, n_suf = pre[0][0].shape[1], suf[0].shape[2]
     first = fetch.start([(q_hbm.at[:, tile(group, heads * LANES)], q_ref), (m_in.at[mine], m_ref)])
     for i, (kr, vr) in enumerate(pre[2:]):
-        first += fetch.start([(kr.at[group], kbuf.at[0, tile(i, n_pre), :]), (vr.at[group], vbuf.at[0, :, tile(i, n_pre)])])
+        first += fetch.start([(kr.at[group], kbuf.at[0, tile(i, n_pre), :]), (vr.at[group], vbuf.at[0, tile(i, n_pre), :])])
     second = []
-    for i, (kr, vr) in enumerate(suf):
-        second += fetch.start([(kr.at[group], ksuf.at[0, tile(i, n_suf), :]), (vr.at[group], vsuf.at[0, :, tile(i, n_suf)])])
+    for i, kv in enumerate(suf):
+        second += fetch.start([(kv.at[j, group], buf.at[0, tile(i, n_suf), :]) for j, buf in enumerate((ksuf, vsuf))])
     third = fetch.start([(acc_in.at[mine], acc_old), (l_in.at[mine], l_old)])
     for ref in (acc_ref, l_ref):
         ref[...] = jnp.zeros_like(ref)
@@ -342,13 +347,13 @@
                 l_ref[i] = l_ref[i] * alpha + jnp.sum(e.reshape(-1, *l_ref.shape[1:]), axis=0)
                 acc_ref[i] = acc_ref[i] * alpha + jnp.dot(vt, e.astype(BF16), preferred_element_type=F32)
 
-            kpre, vpre = pa.at[:, tile(0, LANES)], pb.at[tile(0, LANES), :]
+            kpre, vpre = (p.at[:, tile(0, LANES)] for p in (pa, pb))
             for kr, vr in pre:
                 @each(n_pre // NQ)
                 def _(j):
                     pltpu.sync_copy(kr.at[group, tile(j, NQ), :], kpre)
-                    pltpu.sync_copy(vr.at[group, :, tile(j, NQ)], vpre)
-                    update(kpre[...], vpre[...], None)
+                    pltpu.sync_copy(vr.at[group, tile(j, NQ), :], vpre)
+                    update(kpre[...], across(vpre[...]), None)
 
             mine_blk = jnp.where(half == 0, me, last - me)
 
@@ -358,7 +363,7 @@
                 def _():
                     start = pl.ds(pl.multiple_of(locate(blk), NQ), NQ)
                     seen = (lax.broadcasted_iota(jnp.int32, (NQ, NQ), 0) <= lax.broadcasted_iota(jnp.int32, (NQ, NQ), 1)) | (blk < mine_blk)
-                    update(ksuf[0, start, :], vsuf[0, :, start], seen)
+                    update(ksuf[0, start, :], across(vsuf[0, start, :]), seen)
 
             write(i, acc_ref[i], jnp.sum(l_ref[i], axis=0, keepdims=True))
 
@@ -368,8 +373,8 @@
 
 def attend_rest(q, pre, suf, state, c2, axis, group):
     rows, groups, width = q.shape[0], len(suf), PER_KV * LANES
-    n_pre, n_suf = 2 * pre[0][0].shape[1], groups * suf[0][0].shape[1]
-    flat = [a for p in list(pre) + list(suf) for a in p]
+    n_pre, n_suf = 2 * pre[0][0].shape[1], groups * suf[0].shape[2]
+    flat = [a for p in pre for a in p] + list(suf)
     acc, m, total = state_shapes(PER_KV)
     out = pltpu.HBM((rows // 2, width), BF16)
     return pl.pallas_call(
@@ -378,8 +383,7 @@
         out_specs=[HBM] * 2,
         out_shape=[out] * 2,
         scratch_shapes=[
-            pltpu.VMEM((rows, width), BF16), pltpu.VMEM((1, n_pre, LANES), BF16), pltpu.VMEM((1, LANES, n_pre), BF16),
-            pltpu.VMEM((1, n_suf, LANES), BF16), pltpu.VMEM((1, LANES, n_suf), BF16), *vmem_like([acc, m, total, acc, total, struct((2, rows // 2, width), BF16)]),
+            pltpu.VMEM((rows, width), BF16), *[pltpu.VMEM((1, n, LANES), BF16) for n in (n_pre, n_pre, n_suf, n_suf)], *vmem_like([acc, m, total, acc, total, struct((2, rows // 2, width), BF16)]),
             pltpu.VMEM((8, LANES), F32), pltpu.SemaphoreType.DMA((22,)), *[pltpu.VMEM((2 * NQ, NQ), BF16)] * 2, *[pltpu.VMEM((NQ, NQ), BF16)] * 4,
         ],
         compiler_params=params(20),
@@ -396,7 +400,7 @@
     state = attend_prefix(q, (own_pre, near_pre), c2)
     far_pre, far_suf, wo_z, state = lax.optimization_barrier((far_pre, far_suf, wo_z, state))
     cross_pre = swap(far_pre, 'cp', groups, 1)
-    cross_suf = swap(far_suf, 'cp', groups, 1)
+    cross_suf, = swap((far_suf,), 'cp', groups, 1)
     wo = jnp.stack(wo_z)
     wo_x, = swap((wo,), 'dp', dps, 1)
     wo_y, = swap((wo,), 'cp', groups, 2)
@@ -413,6 +417,7 @@
 
 MESH = pl.DeviceIdType.MESH
 DOT_N = 512
+SLOTS = 6
 MID_PLAN = ((('r3', -1),), (('xc', -3), ('r2', -1), ('hb', 1), ('ha', 1),), (('xb', -2), ('xa', -2),), (('O', 3),), (('r4', -1),), (), (('hc', 1), ('r1', 0),))
 END_PLAN = ((('hw', 0), ('f', -2),), (('O', 3),), (), (), (), (), ())
 AHEAD, BEHIND = 3, 3
@@ -480,7 +485,7 @@
         return a * t + (1 - a) * ld
 
     def issue(ld):
-        slot = lax.rem(ld, 3)
+        slot = lax.rem(ld, SLOTS)
         sem = ring_sem.at[slot]
         t = load_kind(ld)
 
@@ -516,10 +521,10 @@
             start(wd_ref.at[:, cs], ring.at[slot, :ff, :])
 
     def take(ld, n_rows):
-        slot = lax.rem(ld, 3)
+        slot = lax.rem(ld, SLOTS)
         whole = ring.at[slot, :n_rows, :]
         pltpu.make_async_copy(whole, whole, ring_sem.at[slot]).wait()
-        pl.when(ld + 2 < total_loads)(lambda: issue(ld + 2))
+        pl.when(ld + SLOTS - 1 < total_loads)(lambda: issue(ld + SLOTS - 1))
         return slot
 
     def late(c, d):
@@ -732,8 +737,7 @@
     early = [pltpu.make_async_copy(src, obuf.at[:, d, :, tile(0, width)], loc_sem.at[5 + d]) for d, src in enumerate(o_first)]
     for copy in early:
         copy.start()
-    issue(jnp.int32(0))
-    issue(jnp.int32(1))
+    each(SLOTS - 1)(issue)
     for copy in early:
         copy.wait()
 
@@ -796,24 +800,15 @@
         out_shape=[struct(x.shape, BF16), struct((nc, 5, h, half), F32)],
         scratch_shapes=[
             pltpu.VMEM((nc, 4, h, kz), BF16), pltpu.VMEM((nc, ROWS_CH, depth), BF16), pltpu.VMEM((nc, h, half), F32),
-            pltpu.VMEM((3, ring_rows, DOT_N), BF16), pltpu.VMEM((2, 4, h, half), F32), pltpu.VMEM((ROWS_CH, ff), BF16),
+            pltpu.VMEM((SLOTS, ring_rows, DOT_N), BF16), pltpu.VMEM((2, 4, h, half), F32), pltpu.VMEM((ROWS_CH, ff), BF16),
             pltpu.VMEM((2, h, half), F32), pltpu.VMEM((h, half), BF16), pltpu.VMEM((nc, h, half), BF16),
-            *[pltpu.VMEM((nc, h, LANES), F32)] * 2, pltpu.SemaphoreType.DMA((3,)), pltpu.SemaphoreType.DMA((9,)), *sems,
+            *[pltpu.VMEM((nc, h, LANES), F32)] * 2, pltpu.SemaphoreType.DMA((SLOTS,)), pltpu.SemaphoreType.DMA((9,)), *sems,
         ],
         compiler_params=params(60, collective_id=1, has_side_effects=True),
         cost_estimate=cost(6 * x.size * ff, 2 * x.size),
         name="line_block",
     )(*(a.reshape(nc, h, width) for a in o_first), *o_last, x, w_out, *pieces, w_gate, w_up, w_down, gain.reshape(1, depth))
     return xout
-
-
-def copy_kernel(src_ref, dst_ref):
-    dst_ref[...] = src_ref[...]
-
-
-def copied(x):
-    spec = pl.BlockSpec((LANES, x.shape[1]), lambda i: (i, 0))
-    return pl.pallas_call(copy_kernel, grid=(x.shape[0] // LANES,), in_specs=[spec], out_specs=spec, out_shape=struct(x.shape, x.dtype), name="copied")(x)
 
 
 def gather_w_out(w_out, tps):
@@ -836,18 +831,17 @@
         c2 = head_dim ** -0.5 * math.log2(math.e)
         me = lax.axis_index('cp')
         q_pos = block_positions(me, groups, rows // 2, pre_dev * groups)
-        own_pre = (kp_loc.transpose(1, 0, 2), vp_loc.transpose(1, 2, 0))
+        vals = vp_loc.reshape(pre_dev // LANES, LANES, kv_loc, head_dim).transpose(2, 0, 3, 1)
+        own_pre = (kp_loc.transpose(1, 0, 2), vals.reshape(kv_loc, pre_dev, LANES))
         far_pre = swap(own_pre, 'cp', groups, 2)
         near_pre = swap(own_pre, 'cp', groups, 1)
         wo_z = gather_w_out(w_out, tps)
         cos_tab, sin_tab = rope_tables(q_pos, head_dim)
-        q, k_new, vt_new, k_flat, v_flat = qkv(x_loc, norm_attn, w_query, w_key, w_value, cos_tab, sin_tab)
-        own_suf = (k_new, vt_new)
-        far_suf = swap(own_suf, 'cp', groups, 2)
-        near_suf = swap(own_suf, 'cp', groups, 1)
+        q, own_suf, k_flat, v_flat = qkv(x_loc, norm_attn, w_query, w_key, w_value, cos_tab, sin_tab)
+        far_suf, = swap((own_suf,), 'cp', groups, 2)
+        near_suf, = swap((own_suf,), 'cp', groups, 1)
         o_first, o_last, wo_pieces = attend(q, own_pre, near_pre, far_pre, own_suf, near_suf, far_suf, wo_z, c2, groups, tps, dps)
         x_out = line_block(o_first, o_last, x_loc, w_out, wo_pieces, w_gate, w_up, w_down, norm_mlp)
-        x_out = copied(x_out)
         return x_out, k_flat.reshape(rows, kv_loc, head_dim), v_flat.reshape(rows, kv_loc, head_dim)
 
     row_spec = P(('dp', 'cp'), None)

time: 725 us -> 720 us (level)
  Pallas kernels: 604 us -> 586 us
  local copies, waits for them, and re-layouts: 15.2 us -> 23.2 us
    pallas_call x1 -> x0, Pallas kernels: 8.96 us -> none  [copied(): pl.pallas_call(copy_kernel, grid=(x.shape[0] // LANES,), in_specs=[spec],...]
    ppermute x19 -> x16, waiting for transfers between devices: 22 us -> 27.8 us  [swap(): lax.ppermute(a, axis, [(i, i ^ bit) for i in range(groups)])]
  transfers between devices with their start and end apart: 25 -> 22, of which waited for: 6 -> 6; matrix products, arithmetic and copies ran while one was open for 2% -> 2% of each run, Pallas kernels for 19% -> 18%
where the time goes in v5:
time: 720 us; the launch traced here: 718 us
  Pallas kernels  586 us (81%)
  waiting for transfers between devices  59.6 us (8%)
  starting transfers between devices  42.9 us (6%)
  local copies, waits for them, and re-layouts  23.2 us (3%)
    pallas_call x1, Pallas kernels, line_block(): pl.pallas_call(functools.partial(line_kernel, nc=nc), in_specs=[HBM] * (1...  459 us
    pallas_call x2, Pallas kernels, attend_rest(): pl.pallas_call(functools.partial(rest_kernel, group=group, groups=groups,...  59.5 us
    pallas_call x1, Pallas kernels, attend_prefix(): pl.pallas_call(functools.partial(prefix_kernel, heads=heads, c2=c2), in_s...  40 us
    ppermute x3, waiting for transfers between devices, attend(): lax.ppermute(a, 'tp', [(i, i ^ d) for i in range(tps)])  31.7 us
    ppermute x16, waiting for transfers between devices, swap(): lax.ppermute(a, axis, [(i, i ^ bit) for i in range(groups)])  27.8 us
    ppermute x3, starting transfers between devices, attend(): lax.ppermute(a, 'tp', [(i, i ^ d) for i in range(tps)])  27.7 us
    pallas_call x1, Pallas kernels, qkv(): pl.pallas_call(functools.partial(qkv_kernel, nq=nq), grid=(nq + 2,), in_s...  27.5 us
  transfers between devices with their start and end apart: 22, of which 6 were waited for; matrix products, arithmetic and copies ran while one was open for 2% of the time, Pallas kernels for 18%

profile of v5, /device:TPU:0, one launch (start us, length us, event | category | flops | bytes accessed | tf_op | source)
XLA Modules:
  0.0 718.2 jit_solution(5335850531414182813)
XLA Ops:
  0.7 2.9 fusion.6
  3.5 4.1 collective-permute-start.6
  7.6 1.6 collective-permute-start.5
  9.2 0.9 copy.16
  10.2 1.4 copy.18
  12.8 1.9 fusion
  14.7 1.3 pad_maximum_fusion.1
  16.0 27.5 %qkv.1 = (bf16[1024,1024]{1,0:T(8,128)(2,1)}, bf16[2,2,1024,128]{3,2,1,0:T(8,128)(2,1)}, bf16[1024,256]{1,0:T(8,128)(2,1)}, bf16[1024,256]{1,0:T(8,128)(2,1)}) custom-call(bf16[1024,4096]{1,0:T(8,128)(2,1)} %refs_6_.1, bf16[1,4096]{1,0:T(2,128)(2,1)} %reshape.59.g_ref, bf16[4096,1024]{1,0:T(8,128)(2,1)} %wq_ref.1, bf16[4096,256]{1,0:T(8,128)(2,1)} %wk_ref.1, ...), custom_call_target="tpu_custom_call" | custom-call | flops 12884901888 | bytes 8388608 | tf_op jit(solution)/shard_map/qkv/pallas_call | solution.py:125
  43.5 1.8 collective-permute-start.3
  45.6 1.8 collective-permute-start.4
  47.4 1.6 copy-done.2
  49.0 40.0 %attend_prefix.1 = (f32[16,128,512]{2,1,0:T(8,128)}, f32[16,1,512]{2,1,0:T(1,128)}, f32[16,8,512]{2,1,0:T(8,128)}) custom-call(bf16[1024,1024]{1,0:T(8,128)(2,1)S(1)} %copy-done.2, bf16[2,2048,128]{2,1,0:T(8,128)(2,1)S(1)} %bitcast.21, bf16[2,2048,128]{2,1,0:T(8,128)(2,1)S(1)} %bitcast.16, bf16[2,2048,128]{2,1,0:T(8,128)(2,1)} %collective-permute-done.kb.refs_3_, ...), custom_call_target="tpu_custom_call" | custom-call | flops 17179869184 | bytes 4194304 | tf_op jit(solution)/shard_map/attend_prefix/pallas_call | solution.py:244
  89.1 3.0 collective-permute-done.2.refs_5_
  92.1 21.5 %collective-permute-done.4.refs_11_ = bf16[2,2,1024,128]{3,2,1,0:T(8,128)(2,1)S(1)} collective-permute-done((bf16[2,2,1024,128]{3,2,1,0:T(8,128)(2,1)}, bf16[2,2,1024,128]{3,2,1,0:T(8,128)(2,1)S(1)}, u32[]{:S(2)}, u32[]{:S(2)}) %collective-permute-start.4) | collective-permute-done | bytes 1048608 | tf_op jit(solution)/shard_map/ppermute | solution.py:396
  114.1 2.7 pad_maximum_fusion.refs_8_
  116.8 1.7 collective-permute-start.16
  118.5 1.5 collective-permute-start.15
  120.1 2.2 copy-done.1
  122.2 29.8 %attend_rest.2 = (bf16[512,512]{1,0:T(8,128)(2,1)}, bf16[512,512]{1,0:T(8,128)(2,1)}) custom-call(bf16[1024,1024]{1,0:T(8,128)(2,1)S(1)} %copy-done.2, bf16[2,2048,128]{2,1,0:T(8,128)(2,1)S(1)} %bitcast.22, bf16[2,2048,128]{2,1,0:T(8,128)(2,1)S(1)} %bitcast.17, bf16[2,2048,128]{2,1,0:T(8,128)(2,1)} %collective-permute-done.kb.refs_3_, ...), custom_call_target="tpu_custom_call" | custom-call | flops 12884901888 | bytes 4194304 | tf_op jit(solution)/shard_map/attend_rest/pallas_call | solution.py:380
  152.0 1.9 collective-permute-done.16.refs_10_
  153.9 1.5 collective-permute-done.15.refs_9_
  155.7 10.7 %collective-permute-start.12 = (bf16[512,512]{1,0:T(8,128)(2,1)}, bf16[512,512]{1,0:T(8,128)(2,1)S(1)}, u32[]{:S(2)}, u32[]{:S(2)}) collective-permute-start(bf16[512,512]{1,0:T(8,128)(2,1)} %get-tuple-element.42), channel_id=1, source_target_pairs={{0,4},{4,0},{8,12},{12,8},{1,5},{5,1},{9,13},{13,9},{2,6},{6,2},{1... | collective-permute-start | bytes 1572872 | tf_op jit(solution)/shard_map/ppermute | solution.py:409
  166.9 29.7 %attend_rest.3 = (bf16[512,512]{1,0:T(8,128)(2,1)}, bf16[512,512]{1,0:T(8,128)(2,1)}) custom-call(bf16[1024,1024]{1,0:T(8,128)(2,1)S(1)} %copy-done.2, bf16[2,2048,128]{2,1,0:T(8,128)(2,1)S(1)} %bitcast.23, bf16[2,2048,128]{2,1,0:T(8,128)(2,1)S(1)} %bitcast.18, bf16[2,2048,128]{2,1,0:T(8,128)(2,1)} %collective-permute-done.kb.refs_3_, ...), custom_call_target="tpu_custom_call" | custom-call | flops 12884901888 | bytes 4194304 | tf_op jit(solution)/shard_map/attend_rest/pallas_call | solution.py:380
  197.2 3.4 collective-permute-start.14
  200.5 12.7 %collective-permute-done.14 = bf16[512,512]{1,0:T(8,128)(2,1)S(1)} collective-permute-done((bf16[512,512]{1,0:T(8,128)(2,1)}, bf16[512,512]{1,0:T(8,128)(2,1)S(1)}, u32[]{:S(2)}, u32[]{:S(2)}) %collective-permute-start.14) | collective-permute-done | bytes 524320 | tf_op jit(solution)/shard_map/ppermute | solution.py:409
  213.2 13.6 %collective-permute-start.13 = (bf16[512,512]{1,0:T(8,128)(2,1)}, bf16[512,512]{1,0:T(8,128)(2,1)S(1)}, u32[]{:S(2)}, u32[]{:S(2)}) collective-permute-start(bf16[512,512]{1,0:T(8,128)(2,1)} %get-tuple-element.43), channel_id=1, source_target_pairs={{0,8},{4,12},{8,0},{12,4},{1,9},{5,13},{9,1},{13,5},{2,10},{6,14},... | collective-permute-start | bytes 1572872 | tf_op jit(solution)/shard_map/ppermute | solution.py:409
  227.4 2.0 reshape.67
  229.4 2.0 reshape.68
  231.3 19.1 %collective-permute-done.13 = bf16[512,512]{1,0:T(8,128)(2,1)S(1)} collective-permute-done((bf16[512,512]{1,0:T(8,128)(2,1)}, bf16[512,512]{1,0:T(8,128)(2,1)S(1)}, u32[]{:S(2)}, u32[]{:S(2)}) %collective-permute-start.13) | collective-permute-done | bytes 524320 | tf_op jit(solution)/shard_map/ppermute | solution.py:409
  250.4 0.8 copy-done.11
  251.7 458.6 %line_block.1 = (bf16[1024,4096]{1,0:T(8,128)(2,1)}, f32[8,5,64,2048]{3,2,1,0:T(8,128)}) custom-call(bf16[8,64,512]{2,1,0:T(8,128)(2,1)} %bitcast.25, bf16[8,64,512]{2,1,0:T(8,128)(2,1)} %bitcast.26, bf16[8,64,512]{2,1,0:T(8,128)(2,1)} %bitcast.28, bf16[8,64,512]{2,1,0:T(8,128)(2,1)} %bitcast.27, bf16[512,512]{1,0:T(8,128)(2,1)} %get-tuple-element.51.refs_4_, ...), custom_call_target="tpu_custom_call" | custom-call | flops 90194313216 | bytes 8388608 | tf_op jit(solution)/shard_map/line_block/pallas_call | solution.py:796
  710.4 7.9 %copy.20 = bf16[1024,4096]{1,0:T(8,128)(2,1)} copy(bf16[1024,4096]{1,0:T(8,128)(2,1)} %get-tuple-element.69) | data formatting | bytes 16777216
  (54 shorter events, 4.7 us)
Async XLA Ops:
  0.6 8.6 %copy-start.5 = (bf16[2048,2,128]{2,1,0:T(2,128)(2,1)S(1)}, bf16[2048,2,128]{2,1,0:T(2,128)(2,1)}, u32[]{:S(2)}) copy-start(bf16[2048,2,128]{2,1,0:T(2,128)(2,1)} %param.14) | copy-start | bytes 3145732
  3.5 41.8 %collective-permute-start.6 = (bf16[128,2048]{1,0:T(8,128)(2,1)}, bf16[128,2048]{1,0:T(8,128)(2,1)}, u32[]{:S(2)}, u32[]{:S(2)}) collective-permute-start(bf16[128,2048]{1,0:T(8,128)(2,1)} %get-tuple-element.60), channel_id=1, source_target_pairs={{0,8},{4,12},{8,0},{12,4},{1,9},{5,13},{9,1},{13,5},{2,10},{6,14},... | collective-permute-start | bytes 1572872 | tf_op jit(solution)/shard_map/ppermute | solution.py:820
  7.6 81.5 %collective-permute-start.5 = (bf16[128,2048]{1,0:T(8,128)(2,1)}, bf16[128,2048]{1,0:T(8,128)(2,1)}, u32[]{:S(2)}, u32[]{:S(2)}) collective-permute-start(bf16[128,2048]{1,0:T(8,128)(2,1)} %get-tuple-element.60), channel_id=1, source_target_pairs={{0,4},{4,0},{8,12},{12,8},{1,5},{5,1},{9,13},{13,9},{2,6},{6,2},{1... | collective-permute-start | bytes 1572872 | tf_op jit(solution)/shard_map/ppermute | solution.py:820
  9.2 34.3 %collective-permute-start.7 = (bf16[128,2048]{1,0:T(8,128)(2,1)}, bf16[128,2048]{1,0:T(8,128)(2,1)}, u32[]{:S(2)}, u32[]{:S(2)}) collective-permute-start(bf16[128,2048]{1,0:T(8,128)(2,1)} %get-tuple-element.59), channel_id=1, source_target_pairs={{0,12},{4,8},{8,4},{12,0},{1,13},{5,9},{9,5},{13,1},{2,14},{6,10},... | collective-permute-start | bytes 1572872 | tf_op jit(solution)/shard_map/ppermute | solution.py:820
  9.2 3.0 copy-start.6
  10.1 35.5 %collective-permute-start.1 = (bf16[2,2048,128]{2,1,0:T(8,128)(2,1)S(1)}, bf16[2,2048,128]{2,1,0:T(8,128)(2,1)S(1)}, u32[]{:S(2)}, u32[]{:S(2)}) collective-permute-start(bf16[2,2048,128]{2,1,0:T(8,128)(2,1)S(1)} %bitcast.14), channel_id=1, source_target_pairs={{0,1},{1,0},{2,3},{3,2},{4,5},{5,4},{6,7},{7,6},{8,9},{9,8},{10,11... | collective-permute-start | bytes 3145736 | tf_op jit(solution)/shard_map/ppermute | solution.py:396
  11.6 34.0 %collective-permute-start = (bf16[2,2048,128]{2,1,0:T(8,128)(2,1)S(1)}, bf16[2,2048,128]{2,1,0:T(8,128)(2,1)}, u32[]{:S(2)}, u32[]{:S(2)}) collective-permute-start(bf16[2,2048,128]{2,1,0:T(8,128)(2,1)S(1)} %bitcast.19), channel_id=1, source_target_pairs={{0,1},{1,0},{2,3},{3,2},{4,5},{5,4},{6,7},{7,6},{8,9},{9,8},{10,11... | collective-permute-start | bytes 3145736 | tf_op jit(solution)/shard_map/ppermute | solution.py:396
  43.5 45.6 %collective-permute-start.3 = (bf16[2,2048,128]{2,1,0:T(8,128)(2,1)S(1)}, bf16[2,2048,128]{2,1,0:T(8,128)(2,1)S(1)}, u32[]{:S(2)}, u32[]{:S(2)}) collective-permute-start(bf16[2,2048,128]{2,1,0:T(8,128)(2,1)S(1)} %bitcast.15), channel_id=1, source_target_pairs={{0,2},{1,3},{2,0},{3,1},{4,6},{5,7},{6,4},{7,5},{8,10},{9,11},{10,... | collective-permute-start | bytes 3145736 | tf_op jit(solution)/shard_map/ppermute | solution.py:396
  45.3 46.8 %collective-permute-start.2 = (bf16[2,2048,128]{2,1,0:T(8,128)(2,1)S(1)}, bf16[2,2048,128]{2,1,0:T(8,128)(2,1)S(1)}, u32[]{:S(2)}, u32[]{:S(2)}) collective-permute-start(bf16[2,2048,128]{2,1,0:T(8,128)(2,1)S(1)} %bitcast.20), channel_id=1, source_target_pairs={{0,2},{1,3},{2,0},{3,1},{4,6},{5,7},{6,4},{7,5},{8,10},{9,11},{10,... | collective-permute-start | bytes 3145736 | tf_op jit(solution)/shard_map/ppermute | solution.py:396
  45.6 72.9 %collective-permute-start.10 = (bf16[2,2,1024,128]{3,2,1,0:T(8,128)(2,1)}, bf16[2,2,1024,128]{3,2,1,0:T(8,128)(2,1)S(1)}, u32[]{:S(2)}, u32[]{:S(2)}) collective-permute-start(bf16[2,2,1024,128]{3,2,1,0:T(8,128)(2,1)} %get-tuple-element.32.refs_9_), channel_id=1, source_target_pairs={{0,1},{1,0},{2,3},{3,2},{4,5},{5,4},{6,7},{7,6},{8,9},{9,8},{10,11... | collective-permute-start | bytes 3145736 | tf_op jit(solution)/shard_map/ppermute | solution.py:396
  45.6 68.0 %collective-permute-start.4 = (bf16[2,2,1024,128]{3,2,1,0:T(8,128)(2,1)}, bf16[2,2,1024,128]{3,2,1,0:T(8,128)(2,1)S(1)}, u32[]{:S(2)}, u32[]{:S(2)}) collective-permute-start(bf16[2,2,1024,128]{3,2,1,0:T(8,128)(2,1)} %get-tuple-element.32.refs_9_), channel_id=1, source_target_pairs={{0,2},{1,3},{2,0},{3,1},{4,6},{5,7},{6,4},{7,5},{8,10},{9,11},{10,... | collective-permute-start | bytes 3145736 | tf_op jit(solution)/shard_map/ppermute | solution.py:396
  47.4 1.6 copy-start.2
  89.0 31.0 %copy-start = (bf16[2,2,1024,128]{3,2,1,0:T(8,128)(2,1)S(1)}, bf16[2,2,1024,128]{3,2,1,0:T(8,128)(2,1)}, u32[]{:S(2)}) copy-start(bf16[2,2,1024,128]{3,2,1,0:T(8,128)(2,1)} %get-tuple-element.32.refs_9_) | copy-start | bytes 3145732
  89.1 31.0 %copy-start.3 = (f32[16,8,512]{2,1,0:T(8,128)S(1)}, f32[16,8,512]{2,1,0:T(8,128)}, u32[]{:S(2)}) copy-start(f32[16,8,512]{2,1,0:T(8,128)} %get-tuple-element.41.refs_15_) | copy-start | bytes 786436
  89.1 31.0 %copy-start.4 = (f32[16,1,512]{2,1,0:T(1,128)S(1)}, f32[16,1,512]{2,1,0:T(1,128)}, u32[]{:S(2)}) copy-start(f32[16,1,512]{2,1,0:T(1,128)} %get-tuple-element.40.refs_14_) | copy-start | bytes 98308
  113.6 6.4 collective-permute-start.8
  113.6 6.4 collective-permute-start.9
  114.1 5.9 collective-permute-start.11
  116.8 37.1 %collective-permute-start.16 = (bf16[3,128,2048]{2,1,0:T(8,128)(2,1)}, bf16[3,128,2048]{2,1,0:T(8,128)(2,1)}, u32[]{:S(2)}, u32[]{:S(2)}) collective-permute-start(bf16[3,128,2048]{2,1,0:T(8,128)(2,1)} %pad_maximum_fusion.refs_8_), channel_id=1, source_target_pairs={{0,2},{1,3},{2,0},{3,1},{4,6},{5,7},{6,4},{7,5},{8,10},{9,11},{10,... | collective-permute-start | bytes 4718600 | tf_op jit(solution)/shard_map/ppermute | solution.py:396
  118.5 36.8 %collective-permute-start.15 = (bf16[3,128,2048]{2,1,0:T(8,128)(2,1)}, bf16[3,128,2048]{2,1,0:T(8,128)(2,1)}, u32[]{:S(2)}, u32[]{:S(2)}) collective-permute-start(bf16[3,128,2048]{2,1,0:T(8,128)(2,1)} %pad_maximum_fusion.refs_8_), channel_id=1, source_target_pairs={{0,16},{16,0},{1,17},{17,1},{2,18},{18,2},{3,19},{19,3},{4,20},{20... | collective-permute-start | bytes 4718600 | tf_op jit(solution)/shard_map/ppermute | solution.py:396
  120.0 2.2 copy-start.1
  155.4 41.2 %collective-permute-start.17 = (bf16[3,128,2048]{2,1,0:T(8,128)(2,1)}, bf16[3,128,2048]{2,1,0:T(8,128)(2,1)}, u32[]{:S(2)}, u32[]{:S(2)}) collective-permute-start(bf16[3,128,2048]{2,1,0:T(8,128)(2,1)} %collective-permute-done.15.refs_9_), channel_id=1, source_target_pairs={{0,2},{1,3},{2,0},{3,1},{4,6},{5,7},{6,4},{7,5},{8,10},{9,11},{10,... | collective-permute-start | bytes 4718600 | tf_op jit(solution)/shard_map/ppermute | solution.py:396
  155.7 71.1 %copy-start.7 = (bf16[4096]{0:T(1024)(128)(2,1)S(1)}, bf16[4096]{0:T(1024)(128)(2,1)}, u32[]{:S(2)}) copy-start(bf16[4096]{0:T(1024)(128)(2,1)} %param.20) | copy-start | bytes 24580
  155.7 41.5 %collective-permute-start.12 = (bf16[512,512]{1,0:T(8,128)(2,1)}, bf16[512,512]{1,0:T(8,128)(2,1)S(1)}, u32[]{:S(2)}, u32[]{:S(2)}) collective-permute-start(bf16[512,512]{1,0:T(8,128)(2,1)} %get-tuple-element.42), channel_id=1, source_target_pairs={{0,4},{4,0},{8,12},{12,8},{1,5},{5,1},{9,13},{13,9},{2,6},{6,2},{1... | collective-permute-start | bytes 1572872 | tf_op jit(solution)/shard_map/ppermute | solution.py:409
  166.4 84.1 %collective-permute-start.19 = (bf16[3,128,2048]{2,1,0:T(8,128)(2,1)}, bf16[3,128,2048]{2,1,0:T(8,128)(2,1)}, u32[]{:S(2)}, u32[]{:S(2)}) collective-permute-start(bf16[3,128,2048]{2,1,0:T(8,128)(2,1)} %collective-permute-done.15.refs_9_), channel_id=1, source_target_pairs={{0,1},{1,0},{2,3},{3,2},{4,5},{5,4},{6,7},{7,6},{8,9},{9,8},{10,11... | collective-permute-start | bytes 4718600 | tf_op jit(solution)/shard_map/ppermute | solution.py:396
  166.4 84.0 %collective-permute-start.18 = (bf16[3,128,2048]{2,1,0:T(8,128)(2,1)}, bf16[3,128,2048]{2,1,0:T(8,128)(2,1)}, u32[]{:S(2)}, u32[]{:S(2)}) collective-permute-start(bf16[3,128,2048]{2,1,0:T(8,128)(2,1)} %pad_maximum_fusion.refs_8_), channel_id=1, source_target_pairs={{0,1},{1,0},{2,3},{3,2},{4,5},{5,4},{6,7},{7,6},{8,9},{9,8},{10,11... | collective-permute-start | bytes 4718600 | tf_op jit(solution)/shard_map/ppermute | solution.py:396
  166.9 83.5 %collective-permute-start.20 = (bf16[3,128,2048]{2,1,0:T(8,128)(2,1)}, bf16[3,128,2048]{2,1,0:T(8,128)(2,1)}, u32[]{:S(2)}, u32[]{:S(2)}) collective-permute-start(bf16[3,128,2048]{2,1,0:T(8,128)(2,1)} %collective-permute-done.16.refs_10_), channel_id=1, source_target_pairs={{0,1},{1,0},{2,3},{3,2},{4,5},{5,4},{6,7},{7,6},{8,9},{9,8},{10,11... | collective-permute-start | bytes 4718600 | tf_op jit(solution)/shard_map/ppermute | solution.py:396
  196.6 53.9 %collective-permute-start.21 = (bf16[3,128,2048]{2,1,0:T(8,128)(2,1)}, bf16[3,128,2048]{2,1,0:T(8,128)(2,1)S(1)}, u32[]{:S(2)}, u32[]{:S(2)}) collective-permute-start(bf16[3,128,2048]{2,1,0:T(8,128)(2,1)} %collective-permute-done.17.refs_11_), channel_id=1, source_target_pairs={{0,1},{1,0},{2,3},{3,2},{4,5},{5,4},{6,7},{7,6},{8,9},{9,8},{10,11... | collective-permute-start | bytes 4718600 | tf_op jit(solution)/shard_map/ppermute | solution.py:396
  197.1 30.3 %copy-start.9 = (bf16[512,512]{1,0:T(8,128)(2,1)}, bf16[512,512]{1,0:T(8,128)(2,1)S(1)}, u32[]{:S(2)}) copy-start(bf16[512,512]{1,0:T(8,128)(2,1)S(1)} %collective-permute-done.12) | copy-start | bytes 1572868
  197.2 16.0 %collective-permute-start.14 = (bf16[512,512]{1,0:T(8,128)(2,1)}, bf16[512,512]{1,0:T(8,128)(2,1)S(1)}, u32[]{:S(2)}, u32[]{:S(2)}) collective-permute-start(bf16[512,512]{1,0:T(8,128)(2,1)} %get-tuple-element.43), channel_id=1, source_target_pairs={{0,12},{4,8},{8,4},{12,0},{1,13},{5,9},{9,5},{13,1},{2,14},{6,10},... | collective-permute-start | bytes 1572872 | tf_op jit(solution)/shard_map/ppermute | solution.py:409
  213.2 37.3 %copy-start.10 = (bf16[512,512]{1,0:T(8,128)(2,1)}, bf16[512,512]{1,0:T(8,128)(2,1)S(1)}, u32[]{:S(2)}) copy-start(bf16[512,512]{1,0:T(8,128)(2,1)S(1)} %collective-permute-done.14) | copy-start | bytes 1572868
  213.2 37.2 %collective-permute-start.13 = (bf16[512,512]{1,0:T(8,128)(2,1)}, bf16[512,512]{1,0:T(8,128)(2,1)S(1)}, u32[]{:S(2)}, u32[]{:S(2)}) collective-permute-start(bf16[512,512]{1,0:T(8,128)(2,1)} %get-tuple-element.43), channel_id=1, source_target_pairs={{0,8},{4,12},{8,0},{12,4},{1,9},{5,13},{9,1},{13,5},{2,10},{6,14},... | collective-permute-start | bytes 1572872 | tf_op jit(solution)/shard_map/ppermute | solution.py:409
  (2 other events, 2.1 us)

commit v6 on v5

--- a/solution.py
+++ b/solution.py
@@ -129,7 +129,7 @@
         out_specs=[columns(rows), fixed(by_head), fixed(flat), fixed(flat)],
         out_shape=[struct(s, BF16) for s in ((rows, nq * PAIR), by_head, flat, flat)],
         scratch_shapes=[pltpu.VMEM((rows, depth), BF16), pltpu.VMEM((rows, depth), BF16), pltpu.SemaphoreType.DMA((4,))],
-        compiler_params=params(56, dimension_semantics=("arbitrary",)),
+        compiler_params=params(58, dimension_semantics=("arbitrary",)),
         cost_estimate=cost(2 * rows * depth * (nq + 2) * PAIR, 2 * depth * rows),
         name="qkv",
     )(x, gain.reshape(1, depth), wq, wk, wv, cos_tab, sin_tab)
@@ -203,10 +203,10 @@
         values(trips * depth + u, pbufs[u])
 
 
-def prefix_kernel(q_ref, ka, va, kb, vb, acc_out, m_out, l_out, kbuf, vbuf, acc_ref, m_ref, l_ref, pa, pb, sems, *, heads, c2):
+def prefix_kernel(q_hbm, ka, va, kb, vb, acc_out, m_out, l_out, q_ref, kbuf, vbuf, acc_ref, m_ref, l_ref, pa, pb, sems, *, heads, c2):
     fetch = Fetch(sems)
     n = ka.shape[1]
-    settle(fetch.start([(ka, kbuf.at[:, tile(0, n), :]), (va, vbuf.at[:, tile(0, n), :]), (kb, kbuf.at[:, tile(1, n), :]), (vb, vbuf.at[:, tile(1, n), :])]))
+    settle(fetch.start([(q_hbm, q_ref), (ka, kbuf.at[:, tile(0, n), :]), (va, vbuf.at[:, tile(0, n), :]), (kb, kbuf.at[:, tile(1, n), :]), (vb, vbuf.at[:, tile(1, n), :])]))
 
     @each(heads // PER_KV)
     def _(group):
@@ -243,14 +243,14 @@
     shapes = state_shapes(heads)
     return pl.pallas_call(
         functools.partial(prefix_kernel, heads=heads, c2=c2),
-        in_specs=[VMEM] + [HBM] * len(flat),
+        in_specs=[HBM] * (1 + len(flat)),
         out_specs=[HBM] * len(shapes),
         out_shape=[pltpu.HBM(s.shape, s.dtype) for s in shapes],
         scratch_shapes=[
-            *[pltpu.VMEM((2, n, LANES), BF16)] * 2, *vmem_like(shapes),
+            *vmem_like([q]), *[pltpu.VMEM((2, n, LANES), BF16)] * 2, *vmem_like(shapes),
             *[pltpu.VMEM((2 * NQ, NQ), BF16)] * 2, pltpu.SemaphoreType.DMA((8,)),
         ],
-        compiler_params=params(20),
+        compiler_params=params(58),
         cost_estimate=cost(4 * q.size * n, 4 * q.size),
         name="attend_prefix",
     )(q, *flat)
@@ -386,7 +386,7 @@
             pltpu.VMEM((rows, width), BF16), *[pltpu.VMEM((1, n, LANES), BF16) for n in (n_pre, n_pre, n_suf, n_suf)], *vmem_like([acc, m, total, acc, total, struct((2, rows // 2, width), BF16)]),
             pltpu.VMEM((8, LANES), F32), pltpu.SemaphoreType.DMA((22,)), *[pltpu.VMEM((2 * NQ, NQ), BF16)] * 2, *[pltpu.VMEM((NQ, NQ), BF16)] * 4,
         ],
-        compiler_params=params(20),
+        compiler_params=params(42),
         cost_estimate=cost(2 * rows * width * (2 * n_pre + n_suf), 4 * q.size),
         name="attend_rest",
     )(q, *flat, *state)
@@ -417,7 +417,7 @@
 
 MESH = pl.DeviceIdType.MESH
 DOT_N = 512
-SLOTS = 6
+SLOTS = 3
 MID_PLAN = ((('r3', -1),), (('xc', -3), ('r2', -1), ('hb', 1), ('ha', 1),), (('xb', -2), ('xa', -2),), (('O', 3),), (('r4', -1),), (), (('hc', 1), ('r1', 0),))
 END_PLAN = ((('hw', 0), ('f', -2),), (('O', 3),), (), (), (), (), ())
 AHEAD, BEHIND = 3, 3
@@ -435,7 +435,7 @@
     o_first, o_last, x_ref, wo_ref, *refs = refs[:4], refs[4:6], *refs[6:]
     wo_pieces, refs = refs[:8], refs[8:]
     wg_ref, wu_ref, wd_ref, gain_ref, xout_ref, land_ref = refs[:6]
-    (obuf, h2, ybuf, ring, psum, act, stage, xs, xo, sstat, rstat,
+    (obuf, h2, ybuf, ring, psum, act, stage, xs, sstat, rstat,
      ring_sem, loc_sem, o_send, o_recv, st_send, st_recv, a1_send, a1_recv, rs_send, rs_recv, a2_send, a2_recv) = refs[6:]
     R, H = ROWS_CH, ROWS_CH // 2
     depth = wg_ref.shape[0]
@@ -581,21 +581,20 @@
             h2[c, rows_at(z), gs] = (ybuf[c, :, cs] * inv * gain_ref[:, gs].astype(F32)).astype(BF16)
 
     class Spread:
-        def __init__(self, block, send, recv, own=None):
-            self.block, self.send, self.recv, self.own = block, send, recv, own
-
-        def copy(self, c, zz, s, r, dev, own=False):
-            src = self.own(c) if own and self.own is not None else self.block(c, zz)
-            return rdma(src, self.block(c, zz), self.send.at[c, s], self.recv.at[c, r], dev)
+        def __init__(self, block, send, recv):
+            self.block, self.send, self.recv = block, send, recv
+
+        def copy(self, c, zz, s, r, dev):
+            return rdma(self.block(c, zz), self.block(c, zz), self.send.at[c, s], self.recv.at[c, r], dev)
 
         def to_near(self, c):
-            return self.copy(c, z, 0, 0, near, own=True)
+            return self.copy(c, z, 0, 0, near)
 
         def to_outer(self, c):
-            return self.copy(c, z, 0, 0, outer, own=True)
+            return self.copy(c, z, 0, 0, outer)
 
         def to_inner(self, c):
-            return self.copy(c, z, 1, 1, inner, own=True)
+            return self.copy(c, z, 1, 1, inner)
 
         def end_to_inner(self, c):
             return self.copy(c, outer, 2, 2, inner)
@@ -633,10 +632,7 @@
 
     hidden = Spread(lambda c, zz: h2.at[c, rows_at(zz), cols_at(zz)], a1_send, a1_recv)
 
-    def out_block(c, zz):
-        return xout_ref.at[tile(c * 2 + side_of(zz), H), cols_at(zz)]
-
-    done = Spread(out_block, a2_send, a2_recv, own=lambda c: xo.at[c])
+    done = Spread(lambda c, zz: xout_ref.at[tile(c * 2 + side_of(zz), H), cols_at(zz)], a2_send, a2_recv)
 
     def gate_up(c, ld0, active, after):
         @each(nd)
@@ -714,12 +710,11 @@
             v = psum[lax.rem(c, 2), z, rs, :] + stage[0, rs, :]
             if len(ks) == 2:
                 v = v + stage[1, rs, :]
-            xo[c, rs, :] = (ybuf[c, rs, :] + v).astype(BF16)
+            r0 = pl.multiple_of((c * 2 + side) * H + rs.start, rs.size)
+            xout_ref[pl.ds(r0, rs.size), cols_at(z)] = (ybuf[c, rs, :] + v).astype(BF16)
 
         tiles(add)
         done.start(c)
-        pltpu.make_async_copy(xo.at[c], out_block(c, z), loc_sem.at[4]).start()
-        pltpu.make_async_copy(xo.at[c], out_block(c, z), loc_sem.at[4]).wait()
 
     def relay(k, c):
         pass_on(c, k, (far_end, outer, inner)[k], sums_out(c)[1][k])
@@ -796,15 +791,15 @@
     xout, _ = pl.pallas_call(
         functools.partial(line_kernel, nc=nc),
         in_specs=[HBM] * (11 + len(pieces)) + [VMEM],
-        out_specs=[HBM] * 2,
-        out_shape=[struct(x.shape, BF16), struct((nc, 5, h, half), F32)],
+        out_specs=[VMEM, HBM],
+        out_shape=[pltpu.VMEM(x.shape, BF16), struct((nc, 5, h, half), F32)],
         scratch_shapes=[
             pltpu.VMEM((nc, 4, h, kz), BF16), pltpu.VMEM((nc, ROWS_CH, depth), BF16), pltpu.VMEM((nc, h, half), F32),
             pltpu.VMEM((SLOTS, ring_rows, DOT_N), BF16), pltpu.VMEM((2, 4, h, half), F32), pltpu.VMEM((ROWS_CH, ff), BF16),
-            pltpu.VMEM((2, h, half), F32), pltpu.VMEM((h, half), BF16), pltpu.VMEM((nc, h, half), BF16),
+            pltpu.VMEM((2, h, half), F32), pltpu.VMEM((h, half), BF16),
             *[pltpu.VMEM((nc, h, LANES), F32)] * 2, pltpu.SemaphoreType.DMA((SLOTS,)), pltpu.SemaphoreType.DMA((9,)), *sems,
         ],
-        compiler_params=params(60, collective_id=1, has_side_effects=True),
+        compiler_params=params(50, collective_id=1, has_side_effects=True),
         cost_estimate=cost(6 * x.size * ff, 2 * x.size),
         name="line_block",
     )(*(a.reshape(nc, h, width) for a in o_first), *o_last, x, w_out, *pieces, w_gate, w_up, w_down, gain.reshape(1, depth))

time: 720 us -> 715 us (level)
  local copies, waits for them, and re-layouts: 23.2 us -> 14.7 us
  transfers between devices with their start and end apart: 22 -> 22, of which waited for: 6 -> 7; matrix products, arithmetic and copies ran while one was open for 2% -> 1% of each run, Pallas kernels for 18% -> 18%
where the time goes in v6:
time: 715 us; the launch traced here: 714 us
  Pallas kernels  590 us (83%)
  waiting for transfers between devices  61.1 us (9%)
  starting transfers between devices  42.4 us (6%)
  local copies, waits for them, and re-layouts  14.7 us (2%)
    pallas_call x1, Pallas kernels, line_block(): pl.pallas_call(functools.partial(line_kernel, nc=nc), in_specs=[HBM] * (1...  461 us
    pallas_call x2, Pallas kernels, attend_rest(): pl.pallas_call(functools.partial(rest_kernel, group=group, groups=groups,...  60.4 us
    pallas_call x1, Pallas kernels, attend_prefix(): pl.pallas_call(functools.partial(prefix_kernel, heads=heads, c2=c2), in_s...  41.6 us
    ppermute x3, waiting for transfers between devices, attend(): lax.ppermute(a, 'tp', [(i, i ^ d) for i in range(tps)])  34 us
    pallas_call x1, Pallas kernels, qkv(): pl.pallas_call(functools.partial(qkv_kernel, nq=nq), grid=(nq + 2,), in_s...  27.5 us
    ppermute x3, starting transfers between devices, attend(): lax.ppermute(a, 'tp', [(i, i ^ d) for i in range(tps)])  27.3 us
    ppermute x16, waiting for transfers between devices, swap(): lax.ppermute(a, axis, [(i, i ^ bit) for i in range(groups)])  27 us
  transfers between devices with their start and end apart: 22, of which 7 were waited for; matrix products, arithmetic and copies ran while one was open for 1% of the time, Pallas kernels for 18%

profile of v6, /device:TPU:0, one launch (start us, length us, event | category | flops | bytes accessed | tf_op | source)
XLA Modules:
  0.0 713.9 jit_solution(15351353532047941942)
XLA Ops:
  0.7 2.8 fusion.6
  3.5 4.1 collective-permute-start.6
  7.6 1.6 collective-permute-start.5
  9.2 0.9 copy.16
  10.2 1.7 copy.18
  12.1 0.7 reshape.59.g_ref
  12.8 1.9 fusion
  14.7 1.3 pad_maximum_fusion.1
  16.0 27.5 %qkv.1 = (bf16[1024,1024]{1,0:T(8,128)(2,1)}, bf16[2,2,1024,128]{3,2,1,0:T(8,128)(2,1)}, bf16[1024,256]{1,0:T(8,128)(2,1)}, bf16[1024,256]{1,0:T(8,128)(2,1)}) custom-call(bf16[1024,4096]{1,0:T(8,128)(2,1)} %refs_6_.1, bf16[1,4096]{1,0:T(2,128)(2,1)} %reshape.59.g_ref, bf16[4096,1024]{1,0:T(8,128)(2,1)} %wq_ref.1, bf16[4096,256]{1,0:T(8,128)(2,1)} %wk_ref.1, ...), custom_call_target="tpu_custom_call" | custom-call | flops 12884901888 | bytes 8388608 | tf_op jit(solution)/shard_map/qkv/pallas_call | solution.py:125
  43.6 1.8 collective-permute-start.3
  45.7 1.8 collective-permute-start.4
  47.5 41.6 %attend_prefix.1 = (f32[16,128,512]{2,1,0:T(8,128)}, f32[16,1,512]{2,1,0:T(1,128)}, f32[16,8,512]{2,1,0:T(8,128)}) custom-call(bf16[1024,1024]{1,0:T(8,128)(2,1)} %get-tuple-element.48.q_hbm.refs_0_, bf16[2,2048,128]{2,1,0:T(8,128)(2,1)} %bitcast.21, bf16[2,2048,128]{2,1,0:T(8,128)(2,1)} %bitcast.16, bf16[2,2048,128]{2,1,0:T(8,128)(2,1)} %collective-permute-done.kb.refs_3_, ...), custom_call_target="tpu_custom_call" | custom-call | flops 17179869184 | bytes 4194304 | tf_op jit(solution)/shard_map/attend_prefix/pallas_call | solution.py:244
  89.2 3.1 collective-permute-done.2.refs_5_
  92.3 21.7 %collective-permute-done.4.refs_11_ = bf16[2,2,1024,128]{3,2,1,0:T(8,128)(2,1)} collective-permute-done((bf16[2,2,1024,128]{3,2,1,0:T(8,128)(2,1)}, bf16[2,2,1024,128]{3,2,1,0:T(8,128)(2,1)}, u32[]{:S(2)}, u32[]{:S(2)}) %collective-permute-start.4) | collective-permute-done | bytes 1048608 | tf_op jit(solution)/shard_map/ppermute | solution.py:396
  114.5 1.5 pad_maximum_fusion.refs_8_
  116.1 1.8 collective-permute-start.16
  117.9 1.5 collective-permute-start.15
  119.9 1.0 copy-done.15
  120.9 0.9 copy-done.7
  121.8 0.8 copy-done.8
  122.6 30.3 %attend_rest.2 = (bf16[512,512]{1,0:T(8,128)(2,1)}, bf16[512,512]{1,0:T(8,128)(2,1)}) custom-call(bf16[1024,1024]{1,0:T(8,128)(2,1)} %get-tuple-element.48.q_hbm.refs_0_, bf16[2,2048,128]{2,1,0:T(8,128)(2,1)S(1)} %bitcast.22, bf16[2,2048,128]{2,1,0:T(8,128)(2,1)S(1)} %bitcast.17, bf16[2,2048,128]{2,1,0:T(8,128)(2,1)} %collective-permute-done.kb.refs_3_, ...), custom_call_target="tpu_custom_call" | custom-call | flops 12884901888 | bytes 4194304 | tf_op jit(solution)/shard_map/attend_rest/pallas_call | solution.py:380
  153.1 1.5 collective-permute-done.15.refs_9_
  154.9 10.3 %collective-permute-start.12 = (bf16[512,512]{1,0:T(8,128)(2,1)}, bf16[512,512]{1,0:T(8,128)(2,1)S(1)}, u32[]{:S(2)}, u32[]{:S(2)}) collective-permute-start(bf16[512,512]{1,0:T(8,128)(2,1)} %get-tuple-element.42), channel_id=1, source_target_pairs={{0,4},{4,0},{8,12},{12,8},{1,5},{5,1},{9,13},{13,9},{2,6},{6,2},{1... | collective-permute-start | bytes 1572872 | tf_op jit(solution)/shard_map/ppermute | solution.py:409
  165.7 30.1 %attend_rest.3 = (bf16[512,512]{1,0:T(8,128)(2,1)}, bf16[512,512]{1,0:T(8,128)(2,1)}) custom-call(bf16[1024,1024]{1,0:T(8,128)(2,1)} %get-tuple-element.48.q_hbm.refs_0_, bf16[2,2048,128]{2,1,0:T(8,128)(2,1)S(1)} %bitcast.23, bf16[2,2048,128]{2,1,0:T(8,128)(2,1)S(1)} %bitcast.18, bf16[2,2048,128]{2,1,0:T(8,128)(2,1)} %collective-permute-done.kb.refs_3_, ...), custom_call_target="tpu_custom_call" | custom-call | flops 12884901888 | bytes 4194304 | tf_op jit(solution)/shard_map/attend_rest/pallas_call | solution.py:380
  196.4 3.4 collective-permute-start.14
  199.7 12.8 %collective-permute-done.14 = bf16[512,512]{1,0:T(8,128)(2,1)} collective-permute-done((bf16[512,512]{1,0:T(8,128)(2,1)}, bf16[512,512]{1,0:T(8,128)(2,1)}, u32[]{:S(2)}, u32[]{:S(2)}) %collective-permute-start.14) | collective-permute-done | bytes 524320 | tf_op jit(solution)/shard_map/ppermute | solution.py:409
  212.5 13.6 %collective-permute-start.13 = (bf16[512,512]{1,0:T(8,128)(2,1)}, bf16[512,512]{1,0:T(8,128)(2,1)}, u32[]{:S(2)}, u32[]{:S(2)}) collective-permute-start(bf16[512,512]{1,0:T(8,128)(2,1)} %get-tuple-element.43), channel_id=1, source_target_pairs={{0,8},{4,12},{8,0},{12,4},{1,9},{5,13},{9,1},{13,5},{2,10},{6,14},... | collective-permute-start | bytes 1572872 | tf_op jit(solution)/shard_map/ppermute | solution.py:409
  226.7 0.9 reshape.67
  227.7 0.9 reshape.68
  228.6 21.3 %collective-permute-done.13 = bf16[512,512]{1,0:T(8,128)(2,1)} collective-permute-done((bf16[512,512]{1,0:T(8,128)(2,1)}, bf16[512,512]{1,0:T(8,128)(2,1)}, u32[]{:S(2)}, u32[]{:S(2)}) %collective-permute-start.13) | collective-permute-done | bytes 524320 | tf_op jit(solution)/shard_map/ppermute | solution.py:409
  249.9 460.6 %line_block.1 = (bf16[1024,4096]{1,0:T(8,128)(2,1)S(1)}, f32[8,5,64,2048]{3,2,1,0:T(8,128)}) custom-call(bf16[8,64,512]{2,1,0:T(8,128)(2,1)} %bitcast.25, bf16[8,64,512]{2,1,0:T(8,128)(2,1)} %bitcast.26, bf16[8,64,512]{2,1,0:T(8,128)(2,1)} %bitcast.7.refs_2_, bf16[8,64,512]{2,1,0:T(8,128)(2,1)} %bitcast.8.refs_3_, ...), custom_call_target="tpu_custom_call" | custom-call | flops 90194313216 | bytes 8388608 | tf_op jit(solution)/shard_map/line_block/pallas_call | solution.py:791
  710.5 3.4 copy.20
  (64 shorter events, 4.0 us)
Async XLA Ops:
  3.5 41.9 %collective-permute-start.6 = (bf16[128,2048]{1,0:T(8,128)(2,1)}, bf16[128,2048]{1,0:T(8,128)(2,1)}, u32[]{:S(2)}, u32[]{:S(2)}) collective-permute-start(bf16[128,2048]{1,0:T(8,128)(2,1)} %get-tuple-element.60), channel_id=1, source_target_pairs={{0,8},{4,12},{8,0},{12,4},{1,9},{5,13},{9,1},{13,5},{2,10},{6,14},... | collective-permute-start | bytes 1572872 | tf_op jit(solution)/shard_map/ppermute | solution.py:815
  7.6 81.6 %collective-permute-start.5 = (bf16[128,2048]{1,0:T(8,128)(2,1)}, bf16[128,2048]{1,0:T(8,128)(2,1)}, u32[]{:S(2)}, u32[]{:S(2)}) collective-permute-start(bf16[128,2048]{1,0:T(8,128)(2,1)} %get-tuple-element.60), channel_id=1, source_target_pairs={{0,4},{4,0},{8,12},{12,8},{1,5},{5,1},{9,13},{13,9},{2,6},{6,2},{1... | collective-permute-start | bytes 1572872 | tf_op jit(solution)/shard_map/ppermute | solution.py:815
  9.1 34.4 %collective-permute-start.7 = (bf16[128,2048]{1,0:T(8,128)(2,1)}, bf16[128,2048]{1,0:T(8,128)(2,1)}, u32[]{:S(2)}, u32[]{:S(2)}) collective-permute-start(bf16[128,2048]{1,0:T(8,128)(2,1)} %get-tuple-element.59), channel_id=1, source_target_pairs={{0,12},{4,8},{8,4},{12,0},{1,13},{5,9},{9,5},{13,1},{2,14},{6,10},... | collective-permute-start | bytes 1572872 | tf_op jit(solution)/shard_map/ppermute | solution.py:815
  10.1 33.5 %copy-start = (bf16[16,128,2,128]{1,3,0,2:T(8,128)(2,1)}, bf16[16,128,2,128]{1,3,0,2:T(8,128)(2,1)S(1)}, u32[]{:S(2)}) copy-start(bf16[16,128,2,128]{1,3,0,2:T(8,128)(2,1)S(1)} %copy.16) | copy-start | bytes 3145732
  10.1 35.6 %collective-permute-start.1 = (bf16[2,2048,128]{2,1,0:T(8,128)(2,1)S(1)}, bf16[2,2048,128]{2,1,0:T(8,128)(2,1)S(1)}, u32[]{:S(2)}, u32[]{:S(2)}) collective-permute-start(bf16[2,2048,128]{2,1,0:T(8,128)(2,1)S(1)} %bitcast.14), channel_id=1, source_target_pairs={{0,1},{1,0},{2,3},{3,2},{4,5},{5,4},{6,7},{7,6},{8,9},{9,8},{10,11... | collective-permute-start | bytes 3145736 | tf_op jit(solution)/shard_map/ppermute | solution.py:396
  11.8 33.6 %copy-start.2 = (bf16[2048,2,128]{2,0,1:T(8,128)(2,1)}, bf16[2048,2,128]{2,0,1:T(8,128)(2,1)S(1)}, u32[]{:S(2)}) copy-start(bf16[2048,2,128]{2,0,1:T(8,128)(2,1)S(1)} %copy.18) | copy-start | bytes 3145732
  11.9 33.9 %collective-permute-start = (bf16[2,2048,128]{2,1,0:T(8,128)(2,1)S(1)}, bf16[2,2048,128]{2,1,0:T(8,128)(2,1)}, u32[]{:S(2)}, u32[]{:S(2)}) collective-permute-start(bf16[2,2048,128]{2,1,0:T(8,128)(2,1)S(1)} %bitcast.19), channel_id=1, source_target_pairs={{0,1},{1,0},{2,3},{3,2},{4,5},{5,4},{6,7},{7,6},{8,9},{9,8},{10,11... | collective-permute-start | bytes 3145736 | tf_op jit(solution)/shard_map/ppermute | solution.py:396
  43.6 45.5 %collective-permute-start.3 = (bf16[2,2048,128]{2,1,0:T(8,128)(2,1)S(1)}, bf16[2,2048,128]{2,1,0:T(8,128)(2,1)S(1)}, u32[]{:S(2)}, u32[]{:S(2)}) collective-permute-start(bf16[2,2048,128]{2,1,0:T(8,128)(2,1)S(1)} %bitcast.15), channel_id=1, source_target_pairs={{0,2},{1,3},{2,0},{3,1},{4,6},{5,7},{6,4},{7,5},{8,10},{9,11},{10,... | collective-permute-start | bytes 3145736 | tf_op jit(solution)/shard_map/ppermute | solution.py:396
  45.4 46.9 %collective-permute-start.2 = (bf16[2,2048,128]{2,1,0:T(8,128)(2,1)S(1)}, bf16[2,2048,128]{2,1,0:T(8,128)(2,1)}, u32[]{:S(2)}, u32[]{:S(2)}) collective-permute-start(bf16[2,2048,128]{2,1,0:T(8,128)(2,1)S(1)} %bitcast.20), channel_id=1, source_target_pairs={{0,2},{1,3},{2,0},{3,1},{4,6},{5,7},{6,4},{7,5},{8,10},{9,11},{10,... | collective-permute-start | bytes 3145736 | tf_op jit(solution)/shard_map/ppermute | solution.py:396
  45.7 72.2 %collective-permute-start.10 = (bf16[2,2,1024,128]{3,2,1,0:T(8,128)(2,1)}, bf16[2,2,1024,128]{3,2,1,0:T(8,128)(2,1)}, u32[]{:S(2)}, u32[]{:S(2)}) collective-permute-start(bf16[2,2,1024,128]{3,2,1,0:T(8,128)(2,1)} %get-tuple-element.32.refs_9_), channel_id=1, source_target_pairs={{0,1},{1,0},{2,3},{3,2},{4,5},{5,4},{6,7},{7,6},{8,9},{9,8},{10,11... | collective-permute-start | bytes 3145736 | tf_op jit(solution)/shard_map/ppermute | solution.py:396
  45.7 68.3 %collective-permute-start.4 = (bf16[2,2,1024,128]{3,2,1,0:T(8,128)(2,1)}, bf16[2,2,1024,128]{3,2,1,0:T(8,128)(2,1)}, u32[]{:S(2)}, u32[]{:S(2)}) collective-permute-start(bf16[2,2,1024,128]{3,2,1,0:T(8,128)(2,1)} %get-tuple-element.32.refs_9_), channel_id=1, source_target_pairs={{0,2},{1,3},{2,0},{3,1},{4,6},{5,7},{6,4},{7,5},{8,10},{9,11},{10,... | collective-permute-start | bytes 3145736 | tf_op jit(solution)/shard_map/ppermute | solution.py:396
  47.5 73.3 %copy-start.6 = (bf16[2,2,1024,128]{3,2,1,0:T(8,128)(2,1)S(1)}, bf16[2,2,1024,128]{3,2,1,0:T(8,128)(2,1)}, u32[]{:S(2)}) copy-start(bf16[2,2,1024,128]{3,2,1,0:T(8,128)(2,1)} %get-tuple-element.32.refs_9_) | copy-start | bytes 3145732
  89.1 31.8 %copy-start.1 = (bf16[16,128,2,128]{1,3,0,2:T(8,128)(2,1)S(1)}, bf16[16,128,2,128]{1,3,0,2:T(8,128)(2,1)}, u32[]{:S(2)}) copy-start(bf16[16,128,2,128]{1,3,0,2:T(8,128)(2,1)} %copy-done) | copy-start | bytes 3145732
  89.1 31.8 %copy-start.3 = (bf16[2048,2,128]{2,0,1:T(8,128)(2,1)S(1)}, bf16[2048,2,128]{2,0,1:T(8,128)(2,1)}, u32[]{:S(2)}) copy-start(bf16[2048,2,128]{2,0,1:T(8,128)(2,1)} %copy-done.2) | copy-start | bytes 3145732
  114.0 5.4 collective-permute-start.8
  114.0 5.4 collective-permute-start.9
  114.5 5.4 collective-permute-start.11
  116.1 49.1 %copy-start.9 = (bf16[3,128,2048]{2,1,0:T(8,128)(2,1)}, bf16[3,128,2048]{2,1,0:T(8,128)(2,1)S(1)}, u32[]{:S(2)}) copy-start(bf16[3,128,2048]{2,1,0:T(8,128)(2,1)S(1)} %pad_maximum_fusion.refs_8_) | copy-start | bytes 4718596
  116.1 37.0 %collective-permute-start.16 = (bf16[3,128,2048]{2,1,0:T(8,128)(2,1)S(1)}, bf16[3,128,2048]{2,1,0:T(8,128)(2,1)}, u32[]{:S(2)}, u32[]{:S(2)}) collective-permute-start(bf16[3,128,2048]{2,1,0:T(8,128)(2,1)S(1)} %pad_maximum_fusion.refs_8_), channel_id=1, source_target_pairs={{0,2},{1,3},{2,0},{3,1},{4,6},{5,7},{6,4},{7,5},{8,10},{9,11},{10,... | collective-permute-start | bytes 4718600 | tf_op jit(solution)/shard_map/ppermute | solution.py:396
  117.9 36.6 %collective-permute-start.15 = (bf16[3,128,2048]{2,1,0:T(8,128)(2,1)S(1)}, bf16[3,128,2048]{2,1,0:T(8,128)(2,1)}, u32[]{:S(2)}, u32[]{:S(2)}) collective-permute-start(bf16[3,128,2048]{2,1,0:T(8,128)(2,1)S(1)} %pad_maximum_fusion.refs_8_), channel_id=1, source_target_pairs={{0,16},{16,0},{1,17},{17,1},{2,18},{18,2},{3,19},{19,3},{4,20},{20... | collective-permute-start | bytes 4718600 | tf_op jit(solution)/shard_map/ppermute | solution.py:396
  154.5 41.3 %collective-permute-start.17 = (bf16[3,128,2048]{2,1,0:T(8,128)(2,1)}, bf16[3,128,2048]{2,1,0:T(8,128)(2,1)}, u32[]{:S(2)}, u32[]{:S(2)}) collective-permute-start(bf16[3,128,2048]{2,1,0:T(8,128)(2,1)} %collective-permute-done.15.refs_9_), channel_id=1, source_target_pairs={{0,2},{1,3},{2,0},{3,1},{4,6},{5,7},{6,4},{7,5},{8,10},{9,11},{10,... | collective-permute-start | bytes 4718600 | tf_op jit(solution)/shard_map/ppermute | solution.py:396
  154.9 71.2 %copy-start.14 = (bf16[4096]{0:T(1024)(128)(2,1)S(1)}, bf16[4096]{0:T(1024)(128)(2,1)}, u32[]{:S(2)}) copy-start(bf16[4096]{0:T(1024)(128)(2,1)} %param.20) | copy-start | bytes 24580
  154.9 71.8 %copy-start.12 = (bf16[1024,256]{1,0:T(8,128)(2,1)S(1)}, bf16[1024,256]{1,0:T(8,128)(2,1)}, u32[]{:S(2)}) copy-start(bf16[1024,256]{1,0:T(8,128)(2,1)} %get-tuple-element.57) | copy-start | bytes 1572868
  154.9 72.8 %copy-start.11 = (bf16[1024,256]{1,0:T(8,128)(2,1)S(1)}, bf16[1024,256]{1,0:T(8,128)(2,1)}, u32[]{:S(2)}) copy-start(bf16[1024,256]{1,0:T(8,128)(2,1)} %get-tuple-element.58) | copy-start | bytes 1572868
  154.9 41.5 %collective-permute-start.12 = (bf16[512,512]{1,0:T(8,128)(2,1)}, bf16[512,512]{1,0:T(8,128)(2,1)S(1)}, u32[]{:S(2)}, u32[]{:S(2)}) collective-permute-start(bf16[512,512]{1,0:T(8,128)(2,1)} %get-tuple-element.42), channel_id=1, source_target_pairs={{0,4},{4,0},{8,12},{12,8},{1,5},{5,1},{9,13},{13,9},{2,6},{6,2},{1... | collective-permute-start | bytes 1572872 | tf_op jit(solution)/shard_map/ppermute | solution.py:409
  165.2 84.7 %collective-permute-start.19 = (bf16[3,128,2048]{2,1,0:T(8,128)(2,1)}, bf16[3,128,2048]{2,1,0:T(8,128)(2,1)}, u32[]{:S(2)}, u32[]{:S(2)}) collective-permute-start(bf16[3,128,2048]{2,1,0:T(8,128)(2,1)} %collective-permute-done.15.refs_9_), channel_id=1, source_target_pairs={{0,1},{1,0},{2,3},{3,2},{4,5},{5,4},{6,7},{7,6},{8,9},{9,8},{10,11... | collective-permute-start | bytes 4718600 | tf_op jit(solution)/shard_map/ppermute | solution.py:396
  165.2 84.7 %collective-permute-start.18 = (bf16[3,128,2048]{2,1,0:T(8,128)(2,1)S(1)}, bf16[3,128,2048]{2,1,0:T(8,128)(2,1)}, u32[]{:S(2)}, u32[]{:S(2)}) collective-permute-start(bf16[3,128,2048]{2,1,0:T(8,128)(2,1)S(1)} %pad_maximum_fusion.refs_8_), channel_id=1, source_target_pairs={{0,1},{1,0},{2,3},{3,2},{4,5},{5,4},{6,7},{7,6},{8,9},{9,8},{10,11... | collective-permute-start | bytes 4718600 | tf_op jit(solution)/shard_map/ppermute | solution.py:396
  165.7 84.2 %collective-permute-start.20 = (bf16[3,128,2048]{2,1,0:T(8,128)(2,1)}, bf16[3,128,2048]{2,1,0:T(8,128)(2,1)}, u32[]{:S(2)}, u32[]{:S(2)}) collective-permute-start(bf16[3,128,2048]{2,1,0:T(8,128)(2,1)} %collective-permute-done.16.refs_10_), channel_id=1, source_target_pairs={{0,1},{1,0},{2,3},{3,2},{4,5},{5,4},{6,7},{7,6},{8,9},{9,8},{10,11... | collective-permute-start | bytes 4718600 | tf_op jit(solution)/shard_map/ppermute | solution.py:396
  195.8 54.0 %collective-permute-start.21 = (bf16[3,128,2048]{2,1,0:T(8,128)(2,1)}, bf16[3,128,2048]{2,1,0:T(8,128)(2,1)}, u32[]{:S(2)}, u32[]{:S(2)}) collective-permute-start(bf16[3,128,2048]{2,1,0:T(8,128)(2,1)} %collective-permute-done.17.refs_11_), channel_id=1, source_target_pairs={{0,1},{1,0},{2,3},{3,2},{4,5},{5,4},{6,7},{7,6},{8,9},{9,8},{10,11... | collective-permute-start | bytes 4718600 | tf_op jit(solution)/shard_map/ppermute | solution.py:396
  196.4 53.5 %copy-start.16 = (bf16[512,512]{1,0:T(8,128)(2,1)}, bf16[512,512]{1,0:T(8,128)(2,1)S(1)}, u32[]{:S(2)}) copy-start(bf16[512,512]{1,0:T(8,128)(2,1)S(1)} %collective-permute-done.12) | copy-start | bytes 1572868
  196.4 16.1 %collective-permute-start.14 = (bf16[512,512]{1,0:T(8,128)(2,1)}, bf16[512,512]{1,0:T(8,128)(2,1)}, u32[]{:S(2)}, u32[]{:S(2)}) collective-permute-start(bf16[512,512]{1,0:T(8,128)(2,1)} %get-tuple-element.43), channel_id=1, source_target_pairs={{0,12},{4,8},{8,4},{12,0},{1,13},{5,9},{9,5},{13,1},{2,14},{6,10},... | collective-permute-start | bytes 1572872 | tf_op jit(solution)/shard_map/ppermute | solution.py:409
  212.5 37.3 %collective-permute-start.13 = (bf16[512,512]{1,0:T(8,128)(2,1)}, bf16[512,512]{1,0:T(8,128)(2,1)}, u32[]{:S(2)}, u32[]{:S(2)}) collective-permute-start(bf16[512,512]{1,0:T(8,128)(2,1)} %get-tuple-element.43), channel_id=1, source_target_pairs={{0,8},{4,12},{8,0},{12,4},{1,9},{5,13},{9,1},{13,5},{2,10},{6,14},... | collective-permute-start | bytes 1572872 | tf_op jit(solution)/shard_map/ppermute | solution.py:409
  (7 other events, 47.8 us)

commit v7 on v6

--- a/solution.py
+++ b/solution.py
@@ -76,7 +76,7 @@
     def rope(block, sl):
         return (block * cos_ref[sl, :] + pltpu.roll(block, 64, axis=1) * sin_ref[sl, :]).astype(BF16)
 
-    mt = 512
+    mt = rows
 
     def project(w_ref, store):
         @each(rows // mt)
@@ -308,22 +308,23 @@
     bad_ref[...] = jnp.zeros_like(bad_ref)
     chunk = ROWS_CH // 2
 
-    def write(i, acc, total):
-        head, half = i // 2, i % 2
+    def write(head, half, acc, total):
         out = (acc * (1.0 / total)).T.astype(BF16)
         n_p = NQ // chunk
         for p in range(n_p):
             o_ref[p % 2, tile(half * (n_p // 2) + p // 2, chunk), tile(head, LANES)] = out[p * chunk:(p + 1) * chunk]
 
-    @each(heads * 2)
-    def _(i):
-        acc = acc_ref[i] + acc_old[i]
-        total = jnp.sum(l_ref[i] + l_old[i], axis=0, keepdims=True)
-        bad = jnp.where((jnp.abs(acc) < jnp.inf) & (total < jnp.inf), 0.0, 1.0)
-        for j in range(NQ // LANES):
-            part = bad[:, j * LANES:(j + 1) * LANES]
-            bad_ref[...] = jnp.maximum(bad_ref[...], jnp.max(part.reshape(-1, *bad_ref.shape), axis=0))
-        write(i, acc, total)
+    @each(heads)
+    def _(head):
+        for half in range(2):
+            i = head * 2 + half
+            acc = acc_ref[i] + acc_old[i]
+            total = jnp.sum(l_ref[i] + l_old[i], axis=0, keepdims=True)
+            bad = jnp.where((jnp.abs(acc) < jnp.inf) & (total < jnp.inf), 0.0, 1.0)
+            for j in range(NQ // LANES):
+                part = bad[:, j * LANES:(j + 1) * LANES]
+                bad_ref[...] = jnp.maximum(bad_ref[...], jnp.max(part.reshape(-1, *bad_ref.shape), axis=0))
+            write(head, half, acc, total)
 
     @pl.when(jnp.max(bad_ref[...]) > 0.0)
     def _():
@@ -365,7 +366,7 @@
                     seen = (lax.broadcasted_iota(jnp.int32, (NQ, NQ), 0) <= lax.broadcasted_iota(jnp.int32, (NQ, NQ), 1)) | (blk < mine_blk)
                     update(ksuf[0, start, :], across(vsuf[0, start, :]), seen)
 
-            write(i, acc_ref[i], jnp.sum(l_ref[i], axis=0, keepdims=True))
+            write(head, half, acc_ref[i], jnp.sum(l_ref[i], axis=0, keepdims=True))
 
     side = lax.axis_index('tp') // 2
     settle(fetch.start([(o_ref.at[side], here_out), (o_ref.at[1 - side], there_out)]))
@@ -406,13 +407,14 @@
     wo_y, = swap((wo,), 'cp', groups, 2)
     pre, suf = (own_pre, near_pre, far_pre, cross_pre), (own_suf, near_suf, far_suf, cross_suf)
     here, there = attend_rest(q, pre, suf, state, c2, 'cp', 0)
-    o_got = tuple(lax.ppermute(a, 'tp', [(i, i ^ d) for i in range(tps)]) for d, a in ((1, here), (2, there), (3, there)))
+    o_far = tuple(lax.ppermute(there, 'tp', [(i, i ^ d) for i in range(tps)]) for d in (2, 3))
+    o_mate = swap((here,), 'tp', tps, 1)
     wo, wo_x, wo_y, there, q = lax.optimization_barrier((wo, wo_x, wo_y, there, q))
     wo_xy, = swap((wo_x,), 'cp', groups, 2)
     near = swap((wo, wo_x, wo_y), 'cp', groups, 1)
     o_last = attend_rest(q, pre, suf, state, c2, 'cp', 1)
     wo_xy, o_last = lax.optimization_barrier((wo_xy, o_last))
-    return (here,) + o_got, o_last, (wo, wo_x, wo_y, wo_xy) + near + swap((wo_xy,), 'cp', groups, 1)
+    return (here,) + o_mate + o_far, o_last, (wo, wo_x, wo_y, wo_xy) + near + swap((wo_xy,), 'cp', groups, 1)
 
 
 MESH = pl.DeviceIdType.MESH

time: 715 us -> 715 us (level)
    ppermute x16 -> x17, starting transfers between devices: 9.47 us -> 20.9 us  [swap(): lax.ppermute(a, axis, [(i, i ^ bit) for i in range(groups)])]
    ppermute x3 -> x2, starting transfers between devices: 27.3 us -> 17 us  [attend(): lax.ppermute(there, 'tp', [(i, i ^ d) for i in range(tps)])]
    ppermute x16 -> x17, waiting for transfers between devices: 27 us -> 26.3 us  [swap(): lax.ppermute(a, axis, [(i, i ^ bit) for i in range(groups)])]
    ppermute x3 -> x2, waiting for transfers between devices: 34 us -> 34 us  [attend(): lax.ppermute(there, 'tp', [(i, i ^ d) for i in range(tps)])]
  transfers between devices with their start and end apart: 22 -> 22, of which waited for: 7 -> 8; matrix products, arithmetic and copies ran while one was open for 1% -> 1% of each run, Pallas kernels for 18% -> 18%
where the time goes in v7:
time: 715 us; the launch traced here: 714 us
  Pallas kernels  588 us (82%)
  waiting for transfers between devices  61.8 us (9%)
  starting transfers between devices  43.5 us (6%)
  local copies, waits for them, and re-layouts  14.7 us (2%)
    pallas_call x1, Pallas kernels, line_block(): pl.pallas_call(functools.partial(line_kernel, nc=nc), in_specs=[HBM] * (1...  461 us
    pallas_call x2, Pallas kernels, attend_rest(): pl.pallas_call(functools.partial(rest_kernel, group=group, groups=groups,...  59.5 us
    pallas_call x1, Pallas kernels, attend_prefix(): pl.pallas_call(functools.partial(prefix_kernel, heads=heads, c2=c2), in_s...  41.7 us
    ppermute x2, waiting for transfers between devices, attend(): lax.ppermute(there, 'tp', [(i, i ^ d) for i in range(tps)])  34 us
    ppermute x17, waiting for transfers between devices, swap(): lax.ppermute(a, axis, [(i, i ^ bit) for i in range(groups)])  26.3 us
    pallas_call x1, Pallas kernels, qkv(): pl.pallas_call(functools.partial(qkv_kernel, nq=nq), grid=(nq + 2,), in_s...  26 us
    ppermute x17, starting transfers between devices, swap(): lax.ppermute(a, axis, [(i, i ^ bit) for i in range(groups)])  20.9 us
    ppermute x2, starting transfers between devices, attend(): lax.ppermute(there, 'tp', [(i, i ^ d) for i in range(tps)])  17 us
  transfers between devices with their start and end apart: 22, of which 8 were waited for; matrix products, arithmetic and copies ran while one was open for 1% of the time, Pallas kernels for 18%

profile of v7, /device:TPU:0, one launch (start us, length us, event | category | flops | bytes accessed | tf_op | source)
XLA Modules:
  0.0 713.5 jit_solution(17129419514426529720)
XLA Ops:
  0.7 2.8 fusion.6
  3.5 4.1 collective-permute-start.6
  7.6 1.6 collective-permute-start.5
  9.2 0.9 copy.16
  10.2 1.7 copy.18
  12.8 1.9 fusion
  14.7 1.3 pad_maximum_fusion.1
  16.0 26.0 %qkv.1 = (bf16[1024,1024]{1,0:T(8,128)(2,1)}, bf16[2,2,1024,128]{3,2,1,0:T(8,128)(2,1)}, bf16[1024,256]{1,0:T(8,128)(2,1)}, bf16[1024,256]{1,0:T(8,128)(2,1)}) custom-call(bf16[1024,4096]{1,0:T(8,128)(2,1)} %refs_6_.1, bf16[1,4096]{1,0:T(2,128)(2,1)} %reshape.59.g_ref, bf16[4096,1024]{1,0:T(8,128)(2,1)} %wq_ref.1, bf16[4096,256]{1,0:T(8,128)(2,1)} %wk_ref.1, ...), custom_call_target="tpu_custom_call" | custom-call | flops 12884901888 | bytes 8388608 | tf_op jit(solution)/shard_map/qkv/pallas_call | solution.py:125
  42.0 1.4 collective-permute-done.7
  43.5 1.5 collective-permute-start.3
  45.5 1.6 collective-permute-start.4
  47.1 41.7 %attend_prefix.1 = (f32[16,128,512]{2,1,0:T(8,128)}, f32[16,1,512]{2,1,0:T(1,128)}, f32[16,8,512]{2,1,0:T(8,128)}) custom-call(bf16[1024,1024]{1,0:T(8,128)(2,1)} %get-tuple-element.48.q_hbm.refs_0_, bf16[2,2048,128]{2,1,0:T(8,128)(2,1)} %bitcast.21, bf16[2,2048,128]{2,1,0:T(8,128)(2,1)} %bitcast.16, bf16[2,2048,128]{2,1,0:T(8,128)(2,1)} %collective-permute-done.kb.refs_3_, ...), custom_call_target="tpu_custom_call" | custom-call | flops 17179869184 | bytes 4194304 | tf_op jit(solution)/shard_map/attend_prefix/pallas_call | solution.py:244
  88.9 3.2 collective-permute-done.2.refs_5_
  92.1 20.5 %collective-permute-done.4.refs_11_ = bf16[2,2,1024,128]{3,2,1,0:T(8,128)(2,1)} collective-permute-done((bf16[2,2,1024,128]{3,2,1,0:T(8,128)(2,1)}, bf16[2,2,1024,128]{3,2,1,0:T(8,128)(2,1)}, u32[]{:S(2)}, u32[]{:S(2)}) %collective-permute-start.4) | collective-permute-done | bytes 1048608 | tf_op jit(solution)/shard_map/ppermute | solution.py:397
  113.1 1.5 pad_maximum_fusion.refs_8_
  114.6 1.7 collective-permute-start.16
  116.3 1.5 collective-permute-start.15
  118.4 1.0 copy-done.15
  119.4 0.9 copy-done.7
  120.4 0.8 copy-done.8
  121.1 29.8 %attend_rest.2 = (bf16[512,512]{1,0:T(8,128)(2,1)}, bf16[512,512]{1,0:T(8,128)(2,1)}) custom-call(bf16[1024,1024]{1,0:T(8,128)(2,1)} %get-tuple-element.48.q_hbm.refs_0_, bf16[2,2048,128]{2,1,0:T(8,128)(2,1)S(1)} %bitcast.22, bf16[2,2048,128]{2,1,0:T(8,128)(2,1)S(1)} %bitcast.17, bf16[2,2048,128]{2,1,0:T(8,128)(2,1)} %collective-permute-done.kb.refs_3_, ...), custom_call_target="tpu_custom_call" | custom-call | flops 12884901888 | bytes 4194304 | tf_op jit(solution)/shard_map/attend_rest/pallas_call | solution.py:381
  151.6 1.4 collective-permute-done.15.refs_9_
  153.4 11.8 %collective-permute-start.12 = (bf16[512,512]{1,0:T(8,128)(2,1)}, bf16[512,512]{1,0:T(8,128)(2,1)S(1)}, u32[]{:S(2)}, u32[]{:S(2)}) collective-permute-start(bf16[512,512]{1,0:T(8,128)(2,1)} %get-tuple-element.42), channel_id=1, source_target_pairs={{0,4},{4,0},{8,12},{12,8},{1,5},{5,1},{9,13},{13,9},{2,6},{6,2},{1... | collective-permute-start | bytes 1572872 | tf_op jit(solution)/shard_map/ppermute | solution.py:397
  165.7 29.8 %attend_rest.3 = (bf16[512,512]{1,0:T(8,128)(2,1)}, bf16[512,512]{1,0:T(8,128)(2,1)}) custom-call(bf16[1024,1024]{1,0:T(8,128)(2,1)} %get-tuple-element.48.q_hbm.refs_0_, bf16[2,2048,128]{2,1,0:T(8,128)(2,1)S(1)} %bitcast.23, bf16[2,2048,128]{2,1,0:T(8,128)(2,1)S(1)} %bitcast.18, bf16[2,2048,128]{2,1,0:T(8,128)(2,1)} %collective-permute-done.kb.refs_3_, ...), custom_call_target="tpu_custom_call" | custom-call | flops 12884901888 | bytes 4194304 | tf_op jit(solution)/shard_map/attend_rest/pallas_call | solution.py:381
  196.0 3.4 collective-permute-start.14
  199.4 12.8 %collective-permute-done.14 = bf16[512,512]{1,0:T(8,128)(2,1)} collective-permute-done((bf16[512,512]{1,0:T(8,128)(2,1)}, bf16[512,512]{1,0:T(8,128)(2,1)}, u32[]{:S(2)}, u32[]{:S(2)}) %collective-permute-start.14) | collective-permute-done | bytes 524320 | tf_op jit(solution)/shard_map/ppermute | solution.py:410
  212.2 13.6 %collective-permute-start.13 = (bf16[512,512]{1,0:T(8,128)(2,1)}, bf16[512,512]{1,0:T(8,128)(2,1)}, u32[]{:S(2)}, u32[]{:S(2)}) collective-permute-start(bf16[512,512]{1,0:T(8,128)(2,1)} %get-tuple-element.43), channel_id=1, source_target_pairs={{0,8},{4,12},{8,0},{12,4},{1,9},{5,13},{9,1},{13,5},{2,10},{6,14},... | collective-permute-start | bytes 1572872 | tf_op jit(solution)/shard_map/ppermute | solution.py:410
  226.4 0.9 reshape.67
  227.3 0.9 reshape.68
  228.2 21.3 %collective-permute-done.13 = bf16[512,512]{1,0:T(8,128)(2,1)} collective-permute-done((bf16[512,512]{1,0:T(8,128)(2,1)}, bf16[512,512]{1,0:T(8,128)(2,1)}, u32[]{:S(2)}, u32[]{:S(2)}) %collective-permute-start.13) | collective-permute-done | bytes 524320 | tf_op jit(solution)/shard_map/ppermute | solution.py:410
  249.5 460.6 %line_block.1 = (bf16[1024,4096]{1,0:T(8,128)(2,1)S(1)}, f32[8,5,64,2048]{3,2,1,0:T(8,128)}) custom-call(bf16[8,64,512]{2,1,0:T(8,128)(2,1)} %bitcast.25, bf16[8,64,512]{2,1,0:T(8,128)(2,1)} %bitcast.26, bf16[8,64,512]{2,1,0:T(8,128)(2,1)} %bitcast.7.refs_2_, bf16[8,64,512]{2,1,0:T(8,128)(2,1)} %bitcast.8.refs_3_, ...), custom_call_target="tpu_custom_call" | custom-call | flops 90194313216 | bytes 8388608 | tf_op jit(solution)/shard_map/line_block/pallas_call | solution.py:793
  710.1 3.4 copy.20
  (64 shorter events, 5.5 us)
Async XLA Ops:
  3.5 41.5 %collective-permute-start.6 = (bf16[128,2048]{1,0:T(8,128)(2,1)}, bf16[128,2048]{1,0:T(8,128)(2,1)}, u32[]{:S(2)}, u32[]{:S(2)}) collective-permute-start(bf16[128,2048]{1,0:T(8,128)(2,1)} %get-tuple-element.60), channel_id=1, source_target_pairs={{0,8},{4,12},{8,0},{12,4},{1,9},{5,13},{9,1},{13,5},{2,10},{6,14},... | collective-permute-start | bytes 1572872 | tf_op jit(solution)/shard_map/ppermute | solution.py:817
  7.6 81.3 %collective-permute-start.5 = (bf16[128,2048]{1,0:T(8,128)(2,1)}, bf16[128,2048]{1,0:T(8,128)(2,1)}, u32[]{:S(2)}, u32[]{:S(2)}) collective-permute-start(bf16[128,2048]{1,0:T(8,128)(2,1)} %get-tuple-element.60), channel_id=1, source_target_pairs={{0,4},{4,0},{8,12},{12,8},{1,5},{5,1},{9,13},{13,9},{2,6},{6,2},{1... | collective-permute-start | bytes 1572872 | tf_op jit(solution)/shard_map/ppermute | solution.py:817
  9.1 34.3 %collective-permute-start.7 = (bf16[128,2048]{1,0:T(8,128)(2,1)}, bf16[128,2048]{1,0:T(8,128)(2,1)}, u32[]{:S(2)}, u32[]{:S(2)}) collective-permute-start(bf16[128,2048]{1,0:T(8,128)(2,1)} %get-tuple-element.59), channel_id=1, source_target_pairs={{0,12},{4,8},{8,4},{12,0},{1,13},{5,9},{9,5},{13,1},{2,14},{6,10},... | collective-permute-start | bytes 1572872 | tf_op jit(solution)/shard_map/ppermute | solution.py:817
  10.1 33.4 %copy-start = (bf16[16,128,2,128]{1,3,0,2:T(8,128)(2,1)}, bf16[16,128,2,128]{1,3,0,2:T(8,128)(2,1)S(1)}, u32[]{:S(2)}) copy-start(bf16[16,128,2,128]{1,3,0,2:T(8,128)(2,1)S(1)} %copy.16) | copy-start | bytes 3145732
  10.1 35.4 %collective-permute-start.1 = (bf16[2,2048,128]{2,1,0:T(8,128)(2,1)S(1)}, bf16[2,2048,128]{2,1,0:T(8,128)(2,1)S(1)}, u32[]{:S(2)}, u32[]{:S(2)}) collective-permute-start(bf16[2,2048,128]{2,1,0:T(8,128)(2,1)S(1)} %bitcast.14), channel_id=1, source_target_pairs={{0,1},{1,0},{2,3},{3,2},{4,5},{5,4},{6,7},{7,6},{8,9},{9,8},{10,11... | collective-permute-start | bytes 3145736 | tf_op jit(solution)/shard_map/ppermute | solution.py:397
  11.8 33.2 %copy-start.2 = (bf16[2048,2,128]{2,0,1:T(8,128)(2,1)}, bf16[2048,2,128]{2,0,1:T(8,128)(2,1)S(1)}, u32[]{:S(2)}) copy-start(bf16[2048,2,128]{2,0,1:T(8,128)(2,1)S(1)} %copy.18) | copy-start | bytes 3145732
  11.9 33.7 %collective-permute-start = (bf16[2,2048,128]{2,1,0:T(8,128)(2,1)S(1)}, bf16[2,2048,128]{2,1,0:T(8,128)(2,1)}, u32[]{:S(2)}, u32[]{:S(2)}) collective-permute-start(bf16[2,2048,128]{2,1,0:T(8,128)(2,1)S(1)} %bitcast.19), channel_id=1, source_target_pairs={{0,1},{1,0},{2,3},{3,2},{4,5},{5,4},{6,7},{7,6},{8,9},{9,8},{10,11... | collective-permute-start | bytes 3145736 | tf_op jit(solution)/shard_map/ppermute | solution.py:397
  43.5 45.4 %collective-permute-start.3 = (bf16[2,2048,128]{2,1,0:T(8,128)(2,1)S(1)}, bf16[2,2048,128]{2,1,0:T(8,128)(2,1)S(1)}, u32[]{:S(2)}, u32[]{:S(2)}) collective-permute-start(bf16[2,2048,128]{2,1,0:T(8,128)(2,1)S(1)} %bitcast.15), channel_id=1, source_target_pairs={{0,2},{1,3},{2,0},{3,1},{4,6},{5,7},{6,4},{7,5},{8,10},{9,11},{10,... | collective-permute-start | bytes 3145736 | tf_op jit(solution)/shard_map/ppermute | solution.py:397
  45.0 47.1 %collective-permute-start.2 = (bf16[2,2048,128]{2,1,0:T(8,128)(2,1)S(1)}, bf16[2,2048,128]{2,1,0:T(8,128)(2,1)}, u32[]{:S(2)}, u32[]{:S(2)}) collective-permute-start(bf16[2,2048,128]{2,1,0:T(8,128)(2,1)S(1)} %bitcast.20), channel_id=1, source_target_pairs={{0,2},{1,3},{2,0},{3,1},{4,6},{5,7},{6,4},{7,5},{8,10},{9,11},{10,... | collective-permute-start | bytes 3145736 | tf_op jit(solution)/shard_map/ppermute | solution.py:397
  45.5 70.8 %collective-permute-start.10 = (bf16[2,2,1024,128]{3,2,1,0:T(8,128)(2,1)}, bf16[2,2,1024,128]{3,2,1,0:T(8,128)(2,1)}, u32[]{:S(2)}, u32[]{:S(2)}) collective-permute-start(bf16[2,2,1024,128]{3,2,1,0:T(8,128)(2,1)} %get-tuple-element.32.refs_9_), channel_id=1, source_target_pairs={{0,1},{1,0},{2,3},{3,2},{4,5},{5,4},{6,7},{7,6},{8,9},{9,8},{10,11... | collective-permute-start | bytes 3145736 | tf_op jit(solution)/shard_map/ppermute | solution.py:397
  45.5 67.0 %collective-permute-start.4 = (bf16[2,2,1024,128]{3,2,1,0:T(8,128)(2,1)}, bf16[2,2,1024,128]{3,2,1,0:T(8,128)(2,1)}, u32[]{:S(2)}, u32[]{:S(2)}) collective-permute-start(bf16[2,2,1024,128]{3,2,1,0:T(8,128)(2,1)} %get-tuple-element.32.refs_9_), channel_id=1, source_target_pairs={{0,2},{1,3},{2,0},{3,1},{4,6},{5,7},{6,4},{7,5},{8,10},{9,11},{10,... | collective-permute-start | bytes 3145736 | tf_op jit(solution)/shard_map/ppermute | solution.py:397
  47.1 72.3 %copy-start.6 = (bf16[2,2,1024,128]{3,2,1,0:T(8,128)(2,1)S(1)}, bf16[2,2,1024,128]{3,2,1,0:T(8,128)(2,1)}, u32[]{:S(2)}) copy-start(bf16[2,2,1024,128]{3,2,1,0:T(8,128)(2,1)} %get-tuple-element.32.refs_9_) | copy-start | bytes 3145732
  88.9 30.5 %copy-start.1 = (bf16[16,128,2,128]{1,3,0,2:T(8,128)(2,1)S(1)}, bf16[16,128,2,128]{1,3,0,2:T(8,128)(2,1)}, u32[]{:S(2)}) copy-start(bf16[16,128,2,128]{1,3,0,2:T(8,128)(2,1)} %copy-done) | copy-start | bytes 3145732
  88.9 30.5 %copy-start.3 = (bf16[2048,2,128]{2,0,1:T(8,128)(2,1)S(1)}, bf16[2048,2,128]{2,0,1:T(8,128)(2,1)}, u32[]{:S(2)}) copy-start(bf16[2048,2,128]{2,0,1:T(8,128)(2,1)} %copy-done.2) | copy-start | bytes 3145732
  112.6 5.3 collective-permute-start.8
  112.6 5.3 collective-permute-start.9
  113.1 5.4 collective-permute-start.11
  114.6 50.5 %copy-start.9 = (bf16[3,128,2048]{2,1,0:T(8,128)(2,1)}, bf16[3,128,2048]{2,1,0:T(8,128)(2,1)S(1)}, u32[]{:S(2)}) copy-start(bf16[3,128,2048]{2,1,0:T(8,128)(2,1)S(1)} %pad_maximum_fusion.refs_8_) | copy-start | bytes 4718596
  114.6 37.0 %collective-permute-start.16 = (bf16[3,128,2048]{2,1,0:T(8,128)(2,1)S(1)}, bf16[3,128,2048]{2,1,0:T(8,128)(2,1)}, u32[]{:S(2)}, u32[]{:S(2)}) collective-permute-start(bf16[3,128,2048]{2,1,0:T(8,128)(2,1)S(1)} %pad_maximum_fusion.refs_8_), channel_id=1, source_target_pairs={{0,2},{1,3},{2,0},{3,1},{4,6},{5,7},{6,4},{7,5},{8,10},{9,11},{10,... | collective-permute-start | bytes 4718600 | tf_op jit(solution)/shard_map/ppermute | solution.py:397
  116.3 36.6 %collective-permute-start.15 = (bf16[3,128,2048]{2,1,0:T(8,128)(2,1)S(1)}, bf16[3,128,2048]{2,1,0:T(8,128)(2,1)}, u32[]{:S(2)}, u32[]{:S(2)}) collective-permute-start(bf16[3,128,2048]{2,1,0:T(8,128)(2,1)S(1)} %pad_maximum_fusion.refs_8_), channel_id=1, source_target_pairs={{0,16},{16,0},{1,17},{17,1},{2,18},{18,2},{3,19},{19,3},{4,20},{20... | collective-permute-start | bytes 4718600 | tf_op jit(solution)/shard_map/ppermute | solution.py:397
  153.0 42.5 %collective-permute-start.17 = (bf16[3,128,2048]{2,1,0:T(8,128)(2,1)}, bf16[3,128,2048]{2,1,0:T(8,128)(2,1)}, u32[]{:S(2)}, u32[]{:S(2)}) collective-permute-start(bf16[3,128,2048]{2,1,0:T(8,128)(2,1)} %collective-permute-done.15.refs_9_), channel_id=1, source_target_pairs={{0,2},{1,3},{2,0},{3,1},{4,6},{5,7},{6,4},{7,5},{8,10},{9,11},{10,... | collective-permute-start | bytes 4718600 | tf_op jit(solution)/shard_map/ppermute | solution.py:397
  153.4 72.4 %copy-start.14 = (bf16[4096]{0:T(1024)(128)(2,1)S(1)}, bf16[4096]{0:T(1024)(128)(2,1)}, u32[]{:S(2)}) copy-start(bf16[4096]{0:T(1024)(128)(2,1)} %param.20) | copy-start | bytes 24580
  153.4 73.0 %copy-start.12 = (bf16[1024,256]{1,0:T(8,128)(2,1)S(1)}, bf16[1024,256]{1,0:T(8,128)(2,1)}, u32[]{:S(2)}) copy-start(bf16[1024,256]{1,0:T(8,128)(2,1)} %get-tuple-element.57) | copy-start | bytes 1572868
  153.4 74.0 %copy-start.11 = (bf16[1024,256]{1,0:T(8,128)(2,1)S(1)}, bf16[1024,256]{1,0:T(8,128)(2,1)}, u32[]{:S(2)}) copy-start(bf16[1024,256]{1,0:T(8,128)(2,1)} %get-tuple-element.58) | copy-start | bytes 1572868
  153.4 42.7 %collective-permute-start.12 = (bf16[512,512]{1,0:T(8,128)(2,1)}, bf16[512,512]{1,0:T(8,128)(2,1)S(1)}, u32[]{:S(2)}, u32[]{:S(2)}) collective-permute-start(bf16[512,512]{1,0:T(8,128)(2,1)} %get-tuple-element.42), channel_id=1, source_target_pairs={{0,4},{4,0},{8,12},{12,8},{1,5},{5,1},{9,13},{13,9},{2,6},{6,2},{1... | collective-permute-start | bytes 1572872 | tf_op jit(solution)/shard_map/ppermute | solution.py:397
  165.2 84.3 %collective-permute-start.19 = (bf16[3,128,2048]{2,1,0:T(8,128)(2,1)}, bf16[3,128,2048]{2,1,0:T(8,128)(2,1)}, u32[]{:S(2)}, u32[]{:S(2)}) collective-permute-start(bf16[3,128,2048]{2,1,0:T(8,128)(2,1)} %collective-permute-done.15.refs_9_), channel_id=1, source_target_pairs={{0,1},{1,0},{2,3},{3,2},{4,5},{5,4},{6,7},{7,6},{8,9},{9,8},{10,11... | collective-permute-start | bytes 4718600 | tf_op jit(solution)/shard_map/ppermute | solution.py:397
  165.2 84.3 %collective-permute-start.18 = (bf16[3,128,2048]{2,1,0:T(8,128)(2,1)S(1)}, bf16[3,128,2048]{2,1,0:T(8,128)(2,1)}, u32[]{:S(2)}, u32[]{:S(2)}) collective-permute-start(bf16[3,128,2048]{2,1,0:T(8,128)(2,1)S(1)} %pad_maximum_fusion.refs_8_), channel_id=1, source_target_pairs={{0,1},{1,0},{2,3},{3,2},{4,5},{5,4},{6,7},{7,6},{8,9},{9,8},{10,11... | collective-permute-start | bytes 4718600 | tf_op jit(solution)/shard_map/ppermute | solution.py:397
  165.7 83.8 %collective-permute-start.20 = (bf16[3,128,2048]{2,1,0:T(8,128)(2,1)}, bf16[3,128,2048]{2,1,0:T(8,128)(2,1)}, u32[]{:S(2)}, u32[]{:S(2)}) collective-permute-start(bf16[3,128,2048]{2,1,0:T(8,128)(2,1)} %collective-permute-done.16.refs_10_), channel_id=1, source_target_pairs={{0,1},{1,0},{2,3},{3,2},{4,5},{5,4},{6,7},{7,6},{8,9},{9,8},{10,11... | collective-permute-start | bytes 4718600 | tf_op jit(solution)/shard_map/ppermute | solution.py:397
  195.5 54.0 %collective-permute-start.21 = (bf16[3,128,2048]{2,1,0:T(8,128)(2,1)}, bf16[3,128,2048]{2,1,0:T(8,128)(2,1)}, u32[]{:S(2)}, u32[]{:S(2)}) collective-permute-start(bf16[3,128,2048]{2,1,0:T(8,128)(2,1)} %collective-permute-done.17.refs_11_), channel_id=1, source_target_pairs={{0,1},{1,0},{2,3},{3,2},{4,5},{5,4},{6,7},{7,6},{8,9},{9,8},{10,11... | collective-permute-start | bytes 4718600 | tf_op jit(solution)/shard_map/ppermute | solution.py:397
  196.0 53.5 %copy-start.16 = (bf16[512,512]{1,0:T(8,128)(2,1)}, bf16[512,512]{1,0:T(8,128)(2,1)S(1)}, u32[]{:S(2)}) copy-start(bf16[512,512]{1,0:T(8,128)(2,1)S(1)} %collective-permute-done.12) | copy-start | bytes 1572868
  196.0 16.1 %collective-permute-start.14 = (bf16[512,512]{1,0:T(8,128)(2,1)}, bf16[512,512]{1,0:T(8,128)(2,1)}, u32[]{:S(2)}, u32[]{:S(2)}) collective-permute-start(bf16[512,512]{1,0:T(8,128)(2,1)} %get-tuple-element.43), channel_id=1, source_target_pairs={{0,12},{4,8},{8,4},{12,0},{1,13},{5,9},{9,5},{13,1},{2,14},{6,10},... | collective-permute-start | bytes 1572872 | tf_op jit(solution)/shard_map/ppermute | solution.py:410
  212.2 37.3 %collective-permute-start.13 = (bf16[512,512]{1,0:T(8,128)(2,1)}, bf16[512,512]{1,0:T(8,128)(2,1)}, u32[]{:S(2)}, u32[]{:S(2)}) collective-permute-start(bf16[512,512]{1,0:T(8,128)(2,1)} %get-tuple-element.43), channel_id=1, source_target_pairs={{0,8},{4,12},{8,0},{12,4},{1,9},{5,13},{9,1},{13,5},{2,10},{6,14},... | collective-permute-start | bytes 1572872 | tf_op jit(solution)/shard_map/ppermute | solution.py:410
  (7 other events, 46.3 us)

commit v8 on v7

--- a/solution.py
+++ b/solution.py
@@ -206,7 +206,7 @@
 def prefix_kernel(q_hbm, ka, va, kb, vb, acc_out, m_out, l_out, q_ref, kbuf, vbuf, acc_ref, m_ref, l_ref, pa, pb, sems, *, heads, c2):
     fetch = Fetch(sems)
     n = ka.shape[1]
-    settle(fetch.start([(q_hbm, q_ref), (ka, kbuf.at[:, tile(0, n), :]), (va, vbuf.at[:, tile(0, n), :]), (kb, kbuf.at[:, tile(1, n), :]), (vb, vbuf.at[:, tile(1, n), :])]))
+    settle(fetch.start([(q_hbm, q_ref), (ka, kbuf.at[:, tile(0, n), :]), (va, vbuf.at[:, tile(0, n), :]), (kb.at[0], kbuf.at[0, tile(1, n), :]), (vb.at[0], vbuf.at[0, tile(1, n), :])]))
 
     @each(heads // PER_KV)
     def _(group):
@@ -218,13 +218,16 @@
     for ref in (acc_ref, l_ref):
         ref[...] = jnp.zeros_like(ref)
     bk = 2 * NQ
-    per = kbuf.shape[1] // bk
+    per = n // bk
+    pairs = 2 * PER_KV
+    whole = pairs * 2 * per
 
     def item(i):
-        pair = i // per
-        return pair // 2, pair % 2, (i % per) * bk
-
-    attend_items(q_ref, kbuf, vbuf, acc_ref, m_ref, l_ref, (pa, pb), heads * 2 * per, item, bk, c2)
+        j = jnp.maximum(i - whole, 0)
+        pair = jnp.where(i < whole, i // (2 * per), pairs + j // per)
+        return pair // 2, pair % 2, jnp.where(i < whole, i % (2 * per), j % per) * bk
+
+    attend_items(q_ref, kbuf, vbuf, acc_ref, m_ref, l_ref, (pa, pb), whole + pairs * per, item, bk, c2)
     settle(fetch.start([(acc_ref, acc_out), (m_ref, m_out), (l_ref, l_out)]))
 
 
@@ -267,7 +270,7 @@
     mine = pl.ds(group * heads * 2, heads * 2)
     n_pre, n_suf = pre[0][0].shape[1], suf[0].shape[2]
     first = fetch.start([(q_hbm.at[:, tile(group, heads * LANES)], q_ref), (m_in.at[mine], m_ref)])
-    for i, (kr, vr) in enumerate(pre[2:]):
+    for i, (kr, vr) in enumerate(pre[2 - group:]):
         first += fetch.start([(kr.at[group], kbuf.at[0, tile(i, n_pre), :]), (vr.at[group], vbuf.at[0, tile(i, n_pre), :])])
     second = []
     for i, kv in enumerate(suf):
@@ -374,7 +377,7 @@
 
 def attend_rest(q, pre, suf, state, c2, axis, group):
     rows, groups, width = q.shape[0], len(suf), PER_KV * LANES
-    n_pre, n_suf = 2 * pre[0][0].shape[1], groups * suf[0].shape[2]
+    n_pre, n_suf = (2 + group) * pre[0][0].shape[1], groups * suf[0].shape[2]
     flat = [a for p in pre for a in p] + list(suf)
     acc, m, total = state_shapes(PER_KV)
     out = pltpu.HBM((rows // 2, width), BF16)

time: 715 us -> 717 us (level)
    pallas_call x1, Pallas kernels: 41.7 us -> 32.6 us  [attend_prefix(): pl.pallas_call(functools.partial(prefix_kernel, heads=heads, c2=c2), in_s...]
    pallas_call x2, Pallas kernels: 59.5 us -> 68 us  [attend_rest(): pl.pallas_call(functools.partial(rest_kernel, group=group, groups=groups,...]
  transfers between devices with their start and end apart: 22 -> 22, of which waited for: 8 -> 6; matrix products, arithmetic and copies ran while one was open for 1% -> 1% of each run, Pallas kernels for 18% -> 18%
where the time goes in v8:
time: 717 us; the launch traced here: 716 us
  Pallas kernels  584 us (81%)
  waiting for transfers between devices  68.6 us (10%)
  starting transfers between devices  42.9 us (6%)
  local copies, waits for them, and re-layouts  14.7 us (2%)
    pallas_call x1, Pallas kernels, line_block(): pl.pallas_call(functools.partial(line_kernel, nc=nc), in_specs=[HBM] * (1...  458 us
    pallas_call x2, Pallas kernels, attend_rest(): pl.pallas_call(functools.partial(rest_kernel, group=group, groups=groups,...  68 us
    ppermute x2, waiting for transfers between devices, attend(): lax.ppermute(there, 'tp', [(i, i ^ d) for i in range(tps)])  33.7 us
    ppermute x17, waiting for transfers between devices, swap(): lax.ppermute(a, axis, [(i, i ^ bit) for i in range(groups)])  33.4 us
    pallas_call x1, Pallas kernels, attend_prefix(): pl.pallas_call(functools.partial(prefix_kernel, heads=heads, c2=c2), in_s...  32.6 us
    pallas_call x1, Pallas kernels, qkv(): pl.pallas_call(functools.partial(qkv_kernel, nq=nq), grid=(nq + 2,), in_s...  26 us
    ppermute x17, starting transfers between devices, swap(): lax.ppermute(a, axis, [(i, i ^ bit) for i in range(groups)])  21.9 us
    ppermute x2, starting transfers between devices, attend(): lax.ppermute(there, 'tp', [(i, i ^ d) for i in range(tps)])  15.4 us
  transfers between devices with their start and end apart: 22, of which 6 were waited for; matrix products, arithmetic and copies ran while one was open for 1% of the time, Pallas kernels for 18%

profile of v8, /device:TPU:0, one launch (start us, length us, event | category | flops | bytes accessed | tf_op | source)
XLA Modules:
  0.0 716.0 jit_solution(17787709194908718378)
XLA Ops:
  0.7 2.8 fusion.6
  3.5 4.1 collective-permute-start.6
  7.6 1.6 collective-permute-start.5
  9.2 0.9 copy.16
  10.2 1.7 copy.18
  12.8 1.9 fusion
  14.7 1.3 pad_maximum_fusion.1
  16.0 26.0 %qkv.1 = (bf16[1024,1024]{1,0:T(8,128)(2,1)}, bf16[2,2,1024,128]{3,2,1,0:T(8,128)(2,1)}, bf16[1024,256]{1,0:T(8,128)(2,1)}, bf16[1024,256]{1,0:T(8,128)(2,1)}) custom-call(bf16[1024,4096]{1,0:T(8,128)(2,1)} %refs_6_.1, bf16[1,4096]{1,0:T(2,128)(2,1)} %reshape.59.g_ref, bf16[4096,1024]{1,0:T(8,128)(2,1)} %wq_ref.1, bf16[4096,256]{1,0:T(8,128)(2,1)} %wk_ref.1, ...), custom_call_target="tpu_custom_call" | custom-call | flops 12884901888 | bytes 8388608 | tf_op jit(solution)/shard_map/qkv/pallas_call | solution.py:125
  42.0 1.4 collective-permute-done.7
  43.5 1.5 collective-permute-start.3
  45.5 1.6 collective-permute-start.4
  47.1 32.6 %attend_prefix.1 = (f32[16,128,512]{2,1,0:T(8,128)}, f32[16,1,512]{2,1,0:T(1,128)}, f32[16,8,512]{2,1,0:T(8,128)}) custom-call(bf16[1024,1024]{1,0:T(8,128)(2,1)} %get-tuple-element.48.q_hbm.refs_0_, bf16[2,2048,128]{2,1,0:T(8,128)(2,1)} %bitcast.21, bf16[2,2048,128]{2,1,0:T(8,128)(2,1)} %bitcast.16, bf16[2,2048,128]{2,1,0:T(8,128)(2,1)} %collective-permute-done.kb.refs_3_, ...), custom_call_target="tpu_custom_call" | custom-call | flops 17179869184 | bytes 4194304 | tf_op jit(solution)/shard_map/attend_prefix/pallas_call | solution.py:247
  79.8 12.3 %collective-permute-done.2.refs_5_ = bf16[2,2048,128]{2,1,0:T(8,128)(2,1)} collective-permute-done((bf16[2,2048,128]{2,1,0:T(8,128)(2,1)S(1)}, bf16[2,2048,128]{2,1,0:T(8,128)(2,1)}, u32[]{:S(2)}, u32[]{:S(2)}) %collective-permute-start.2) | collective-permute-done | bytes 1048608 | tf_op jit(solution)/shard_map/ppermute | solution.py:400
  92.1 20.5 %collective-permute-done.4.refs_11_ = bf16[2,2,1024,128]{3,2,1,0:T(8,128)(2,1)} collective-permute-done((bf16[2,2,1024,128]{3,2,1,0:T(8,128)(2,1)}, bf16[2,2,1024,128]{3,2,1,0:T(8,128)(2,1)}, u32[]{:S(2)}, u32[]{:S(2)}) %collective-permute-start.4) | collective-permute-done | bytes 1048608 | tf_op jit(solution)/shard_map/ppermute | solution.py:400
  113.1 1.5 pad_maximum_fusion.refs_8_
  114.6 1.7 collective-permute-start.16
  116.3 1.5 collective-permute-start.15
  118.4 1.0 copy-done.15
  119.4 0.9 copy-done.7
  120.4 0.8 copy-done.8
  121.1 29.8 %attend_rest.2 = (bf16[512,512]{1,0:T(8,128)(2,1)}, bf16[512,512]{1,0:T(8,128)(2,1)}) custom-call(bf16[1024,1024]{1,0:T(8,128)(2,1)} %get-tuple-element.48.q_hbm.refs_0_, bf16[2,2048,128]{2,1,0:T(8,128)(2,1)S(1)} %bitcast.22, bf16[2,2048,128]{2,1,0:T(8,128)(2,1)S(1)} %bitcast.17, bf16[2,2048,128]{2,1,0:T(8,128)(2,1)} %collective-permute-done.kb.refs_3_, ...), custom_call_target="tpu_custom_call" | custom-call | flops 12884901888 | bytes 4194304 | tf_op jit(solution)/shard_map/attend_rest/pallas_call | solution.py:384
  150.9 11.9 %collective-permute-start.12 = (bf16[512,512]{1,0:T(8,128)(2,1)}, bf16[512,512]{1,0:T(8,128)(2,1)S(1)}, u32[]{:S(2)}, u32[]{:S(2)}) collective-permute-start(bf16[512,512]{1,0:T(8,128)(2,1)} %get-tuple-element.42), channel_id=1, source_target_pairs={{0,4},{4,0},{8,12},{12,8},{1,5},{5,1},{9,13},{13,9},{2,6},{6,2},{1... | collective-permute-start | bytes 1572872 | tf_op jit(solution)/shard_map/ppermute | solution.py:400
  162.9 1.6 collective-permute-start.17
  165.0 38.2 %attend_rest.3 = (bf16[512,512]{1,0:T(8,128)(2,1)}, bf16[512,512]{1,0:T(8,128)(2,1)}) custom-call(bf16[1024,1024]{1,0:T(8,128)(2,1)} %get-tuple-element.48.q_hbm.refs_0_, bf16[2,2048,128]{2,1,0:T(8,128)(2,1)S(1)} %bitcast.23, bf16[2,2048,128]{2,1,0:T(8,128)(2,1)S(1)} %bitcast.18, bf16[2,2048,128]{2,1,0:T(8,128)(2,1)} %collective-permute-done.kb.refs_3_, ...), custom_call_target="tpu_custom_call" | custom-call | flops 17179869184 | bytes 4194304 | tf_op jit(solution)/shard_map/attend_rest/pallas_call | solution.py:384
  203.4 3.4 collective-permute-start.14
  206.8 13.0 %collective-permute-done.14 = bf16[512,512]{1,0:T(8,128)(2,1)} collective-permute-done((bf16[512,512]{1,0:T(8,128)(2,1)}, bf16[512,512]{1,0:T(8,128)(2,1)}, u32[]{:S(2)}, u32[]{:S(2)}) %collective-permute-start.14) | collective-permute-done | bytes 524320 | tf_op jit(solution)/shard_map/ppermute | solution.py:413
  219.8 12.0 %collective-permute-start.13 = (bf16[512,512]{1,0:T(8,128)(2,1)}, bf16[512,512]{1,0:T(8,128)(2,1)}, u32[]{:S(2)}, u32[]{:S(2)}) collective-permute-start(bf16[512,512]{1,0:T(8,128)(2,1)} %get-tuple-element.43), channel_id=1, source_target_pairs={{0,8},{4,12},{8,0},{12,4},{1,9},{5,13},{9,1},{13,5},{2,10},{6,14},... | collective-permute-start | bytes 1572872 | tf_op jit(solution)/shard_map/ppermute | solution.py:413
  232.4 0.9 reshape.67
  233.4 0.9 reshape.68
  234.3 20.7 %collective-permute-done.13 = bf16[512,512]{1,0:T(8,128)(2,1)} collective-permute-done((bf16[512,512]{1,0:T(8,128)(2,1)}, bf16[512,512]{1,0:T(8,128)(2,1)}, u32[]{:S(2)}, u32[]{:S(2)}) %collective-permute-start.13) | collective-permute-done | bytes 524320 | tf_op jit(solution)/shard_map/ppermute | solution.py:413
  255.0 457.6 %line_block.1 = (bf16[1024,4096]{1,0:T(8,128)(2,1)S(1)}, f32[8,5,64,2048]{3,2,1,0:T(8,128)}) custom-call(bf16[8,64,512]{2,1,0:T(8,128)(2,1)} %bitcast.25, bf16[8,64,512]{2,1,0:T(8,128)(2,1)} %bitcast.26, bf16[8,64,512]{2,1,0:T(8,128)(2,1)} %bitcast.7.refs_2_, bf16[8,64,512]{2,1,0:T(8,128)(2,1)} %bitcast.8.refs_3_, ...), custom_call_target="tpu_custom_call" | custom-call | flops 90194313216 | bytes 8388608 | tf_op jit(solution)/shard_map/line_block/pallas_call | solution.py:796
  712.6 3.4 copy.20
  (64 shorter events, 4.2 us)
Async XLA Ops:
  3.5 41.5 %collective-permute-start.6 = (bf16[128,2048]{1,0:T(8,128)(2,1)}, bf16[128,2048]{1,0:T(8,128)(2,1)}, u32[]{:S(2)}, u32[]{:S(2)}) collective-permute-start(bf16[128,2048]{1,0:T(8,128)(2,1)} %get-tuple-element.60), channel_id=1, source_target_pairs={{0,8},{4,12},{8,0},{12,4},{1,9},{5,13},{9,1},{13,5},{2,10},{6,14},... | collective-permute-start | bytes 1572872 | tf_op jit(solution)/shard_map/ppermute | solution.py:820
  7.6 72.2 %collective-permute-start.5 = (bf16[128,2048]{1,0:T(8,128)(2,1)}, bf16[128,2048]{1,0:T(8,128)(2,1)}, u32[]{:S(2)}, u32[]{:S(2)}) collective-permute-start(bf16[128,2048]{1,0:T(8,128)(2,1)} %get-tuple-element.60), channel_id=1, source_target_pairs={{0,4},{4,0},{8,12},{12,8},{1,5},{5,1},{9,13},{13,9},{2,6},{6,2},{1... | collective-permute-start | bytes 1572872 | tf_op jit(solution)/shard_map/ppermute | solution.py:820
  9.1 34.3 %collective-permute-start.7 = (bf16[128,2048]{1,0:T(8,128)(2,1)}, bf16[128,2048]{1,0:T(8,128)(2,1)}, u32[]{:S(2)}, u32[]{:S(2)}) collective-permute-start(bf16[128,2048]{1,0:T(8,128)(2,1)} %get-tuple-element.59), channel_id=1, source_target_pairs={{0,12},{4,8},{8,4},{12,0},{1,13},{5,9},{9,5},{13,1},{2,14},{6,10},... | collective-permute-start | bytes 1572872 | tf_op jit(solution)/shard_map/ppermute | solution.py:820
  10.1 33.4 %copy-start = (bf16[16,128,2,128]{1,3,0,2:T(8,128)(2,1)}, bf16[16,128,2,128]{1,3,0,2:T(8,128)(2,1)S(1)}, u32[]{:S(2)}) copy-start(bf16[16,128,2,128]{1,3,0,2:T(8,128)(2,1)S(1)} %copy.16) | copy-start | bytes 3145732
  10.1 35.4 %collective-permute-start.1 = (bf16[2,2048,128]{2,1,0:T(8,128)(2,1)S(1)}, bf16[2,2048,128]{2,1,0:T(8,128)(2,1)S(1)}, u32[]{:S(2)}, u32[]{:S(2)}) collective-permute-start(bf16[2,2048,128]{2,1,0:T(8,128)(2,1)S(1)} %bitcast.14), channel_id=1, source_target_pairs={{0,1},{1,0},{2,3},{3,2},{4,5},{5,4},{6,7},{7,6},{8,9},{9,8},{10,11... | collective-permute-start | bytes 3145736 | tf_op jit(solution)/shard_map/ppermute | solution.py:400
  11.9 33.7 %collective-permute-start = (bf16[2,2048,128]{2,1,0:T(8,128)(2,1)S(1)}, bf16[2,2048,128]{2,1,0:T(8,128)(2,1)}, u32[]{:S(2)}, u32[]{:S(2)}) collective-permute-start(bf16[2,2048,128]{2,1,0:T(8,128)(2,1)S(1)} %bitcast.19), channel_id=1, source_target_pairs={{0,1},{1,0},{2,3},{3,2},{4,5},{5,4},{6,7},{7,6},{8,9},{9,8},{10,11... | collective-permute-start | bytes 3145736 | tf_op jit(solution)/shard_map/ppermute | solution.py:400
  43.5 36.3 %collective-permute-start.3 = (bf16[2,2048,128]{2,1,0:T(8,128)(2,1)S(1)}, bf16[2,2048,128]{2,1,0:T(8,128)(2,1)S(1)}, u32[]{:S(2)}, u32[]{:S(2)}) collective-permute-start(bf16[2,2048,128]{2,1,0:T(8,128)(2,1)S(1)} %bitcast.15), channel_id=1, source_target_pairs={{0,2},{1,3},{2,0},{3,1},{4,6},{5,7},{6,4},{7,5},{8,10},{9,11},{10,... | collective-permute-start | bytes 3145736 | tf_op jit(solution)/shard_map/ppermute | solution.py:400
  45.0 47.1 %collective-permute-start.2 = (bf16[2,2048,128]{2,1,0:T(8,128)(2,1)S(1)}, bf16[2,2048,128]{2,1,0:T(8,128)(2,1)}, u32[]{:S(2)}, u32[]{:S(2)}) collective-permute-start(bf16[2,2048,128]{2,1,0:T(8,128)(2,1)S(1)} %bitcast.20), channel_id=1, source_target_pairs={{0,2},{1,3},{2,0},{3,1},{4,6},{5,7},{6,4},{7,5},{8,10},{9,11},{10,... | collective-permute-start | bytes 3145736 | tf_op jit(solution)/shard_map/ppermute | solution.py:400
  45.5 70.8 %collective-permute-start.10 = (bf16[2,2,1024,128]{3,2,1,0:T(8,128)(2,1)}, bf16[2,2,1024,128]{3,2,1,0:T(8,128)(2,1)}, u32[]{:S(2)}, u32[]{:S(2)}) collective-permute-start(bf16[2,2,1024,128]{3,2,1,0:T(8,128)(2,1)} %get-tuple-element.32.refs_9_), channel_id=1, source_target_pairs={{0,1},{1,0},{2,3},{3,2},{4,5},{5,4},{6,7},{7,6},{8,9},{9,8},{10,11... | collective-permute-start | bytes 3145736 | tf_op jit(solution)/shard_map/ppermute | solution.py:400
  45.5 67.0 %collective-permute-start.4 = (bf16[2,2,1024,128]{3,2,1,0:T(8,128)(2,1)}, bf16[2,2,1024,128]{3,2,1,0:T(8,128)(2,1)}, u32[]{:S(2)}, u32[]{:S(2)}) collective-permute-start(bf16[2,2,1024,128]{3,2,1,0:T(8,128)(2,1)} %get-tuple-element.32.refs_9_), channel_id=1, source_target_pairs={{0,2},{1,3},{2,0},{3,1},{4,6},{5,7},{6,4},{7,5},{8,10},{9,11},{10,... | collective-permute-start | bytes 3145736 | tf_op jit(solution)/shard_map/ppermute | solution.py:400
  47.1 72.3 %copy-start.6 = (bf16[2,2,1024,128]{3,2,1,0:T(8,128)(2,1)S(1)}, bf16[2,2,1024,128]{3,2,1,0:T(8,128)(2,1)}, u32[]{:S(2)}) copy-start(bf16[2,2,1024,128]{3,2,1,0:T(8,128)(2,1)} %get-tuple-element.32.refs_9_) | copy-start | bytes 3145732
  79.8 39.7 %copy-start.1 = (bf16[16,128,2,128]{1,3,0,2:T(8,128)(2,1)S(1)}, bf16[16,128,2,128]{1,3,0,2:T(8,128)(2,1)}, u32[]{:S(2)}) copy-start(bf16[16,128,2,128]{1,3,0,2:T(8,128)(2,1)} %copy-done) | copy-start | bytes 3145732
  79.8 39.6 %copy-start.3 = (bf16[2048,2,128]{2,0,1:T(8,128)(2,1)S(1)}, bf16[2048,2,128]{2,0,1:T(8,128)(2,1)}, u32[]{:S(2)}) copy-start(bf16[2048,2,128]{2,0,1:T(8,128)(2,1)} %copy-done.2) | copy-start | bytes 3145732
  79.8 39.6 %copy-start.5 = (bf16[2,2048,128]{2,1,0:T(8,128)(2,1)S(1)}, bf16[2,2048,128]{2,1,0:T(8,128)(2,1)}, u32[]{:S(2)}) copy-start(bf16[2,2048,128]{2,1,0:T(8,128)(2,1)} %copy-done.4) | copy-start | bytes 3145732
  112.6 5.3 collective-permute-start.8
  112.6 5.3 collective-permute-start.9
  113.1 5.4 collective-permute-start.11
  114.6 49.9 %copy-start.9 = (bf16[3,128,2048]{2,1,0:T(8,128)(2,1)}, bf16[3,128,2048]{2,1,0:T(8,128)(2,1)S(1)}, u32[]{:S(2)}) copy-start(bf16[3,128,2048]{2,1,0:T(8,128)(2,1)S(1)} %pad_maximum_fusion.refs_8_) | copy-start | bytes 4718596
  114.6 48.1 %collective-permute-start.16 = (bf16[3,128,2048]{2,1,0:T(8,128)(2,1)S(1)}, bf16[3,128,2048]{2,1,0:T(8,128)(2,1)}, u32[]{:S(2)}, u32[]{:S(2)}) collective-permute-start(bf16[3,128,2048]{2,1,0:T(8,128)(2,1)S(1)} %pad_maximum_fusion.refs_8_), channel_id=1, source_target_pairs={{0,2},{1,3},{2,0},{3,1},{4,6},{5,7},{6,4},{7,5},{8,10},{9,11},{10,... | collective-permute-start | bytes 4718600 | tf_op jit(solution)/shard_map/ppermute | solution.py:400
  116.3 46.4 %collective-permute-start.15 = (bf16[3,128,2048]{2,1,0:T(8,128)(2,1)S(1)}, bf16[3,128,2048]{2,1,0:T(8,128)(2,1)}, u32[]{:S(2)}, u32[]{:S(2)}) collective-permute-start(bf16[3,128,2048]{2,1,0:T(8,128)(2,1)S(1)} %pad_maximum_fusion.refs_8_), channel_id=1, source_target_pairs={{0,16},{16,0},{1,17},{17,1},{2,18},{18,2},{3,19},{19,3},{4,20},{20... | collective-permute-start | bytes 4718600 | tf_op jit(solution)/shard_map/ppermute | solution.py:400
  150.9 52.5 %collective-permute-start.12 = (bf16[512,512]{1,0:T(8,128)(2,1)}, bf16[512,512]{1,0:T(8,128)(2,1)S(1)}, u32[]{:S(2)}, u32[]{:S(2)}) collective-permute-start(bf16[512,512]{1,0:T(8,128)(2,1)} %get-tuple-element.42), channel_id=1, source_target_pairs={{0,4},{4,0},{8,12},{12,8},{1,5},{5,1},{9,13},{13,9},{2,6},{6,2},{1... | collective-permute-start | bytes 1572872 | tf_op jit(solution)/shard_map/ppermute | solution.py:400
  162.8 69.1 %copy-start.14 = (bf16[4096]{0:T(1024)(128)(2,1)S(1)}, bf16[4096]{0:T(1024)(128)(2,1)}, u32[]{:S(2)}) copy-start(bf16[4096]{0:T(1024)(128)(2,1)} %param.20) | copy-start | bytes 24580
  162.8 69.7 %copy-start.12 = (bf16[1024,256]{1,0:T(8,128)(2,1)S(1)}, bf16[1024,256]{1,0:T(8,128)(2,1)}, u32[]{:S(2)}) copy-start(bf16[1024,256]{1,0:T(8,128)(2,1)} %get-tuple-element.57) | copy-start | bytes 1572868
  162.8 70.6 %copy-start.11 = (bf16[1024,256]{1,0:T(8,128)(2,1)S(1)}, bf16[1024,256]{1,0:T(8,128)(2,1)}, u32[]{:S(2)}) copy-start(bf16[1024,256]{1,0:T(8,128)(2,1)} %get-tuple-element.58) | copy-start | bytes 1572868
  162.8 92.2 %collective-permute-start.19 = (bf16[3,128,2048]{2,1,0:T(8,128)(2,1)}, bf16[3,128,2048]{2,1,0:T(8,128)(2,1)}, u32[]{:S(2)}, u32[]{:S(2)}) collective-permute-start(bf16[3,128,2048]{2,1,0:T(8,128)(2,1)} %collective-permute-done.15.refs_9_), channel_id=1, source_target_pairs={{0,1},{1,0},{2,3},{3,2},{4,5},{5,4},{6,7},{7,6},{8,9},{9,8},{10,11... | collective-permute-start | bytes 4718600 | tf_op jit(solution)/shard_map/ppermute | solution.py:400
  162.9 40.3 %collective-permute-start.17 = (bf16[3,128,2048]{2,1,0:T(8,128)(2,1)}, bf16[3,128,2048]{2,1,0:T(8,128)(2,1)}, u32[]{:S(2)}, u32[]{:S(2)}) collective-permute-start(bf16[3,128,2048]{2,1,0:T(8,128)(2,1)} %collective-permute-done.15.refs_9_), channel_id=1, source_target_pairs={{0,2},{1,3},{2,0},{3,1},{4,6},{5,7},{6,4},{7,5},{8,10},{9,11},{10,... | collective-permute-start | bytes 4718600 | tf_op jit(solution)/shard_map/ppermute | solution.py:400
  164.5 90.5 %collective-permute-start.18 = (bf16[3,128,2048]{2,1,0:T(8,128)(2,1)S(1)}, bf16[3,128,2048]{2,1,0:T(8,128)(2,1)}, u32[]{:S(2)}, u32[]{:S(2)}) collective-permute-start(bf16[3,128,2048]{2,1,0:T(8,128)(2,1)S(1)} %pad_maximum_fusion.refs_8_), channel_id=1, source_target_pairs={{0,1},{1,0},{2,3},{3,2},{4,5},{5,4},{6,7},{7,6},{8,9},{9,8},{10,11... | collective-permute-start | bytes 4718600 | tf_op jit(solution)/shard_map/ppermute | solution.py:400
  164.6 90.3 %collective-permute-start.20 = (bf16[3,128,2048]{2,1,0:T(8,128)(2,1)}, bf16[3,128,2048]{2,1,0:T(8,128)(2,1)}, u32[]{:S(2)}, u32[]{:S(2)}) collective-permute-start(bf16[3,128,2048]{2,1,0:T(8,128)(2,1)} %collective-permute-done.16.refs_10_), channel_id=1, source_target_pairs={{0,1},{1,0},{2,3},{3,2},{4,5},{5,4},{6,7},{7,6},{8,9},{9,8},{10,11... | collective-permute-start | bytes 4718600 | tf_op jit(solution)/shard_map/ppermute | solution.py:400
  203.2 51.8 %collective-permute-start.21 = (bf16[3,128,2048]{2,1,0:T(8,128)(2,1)}, bf16[3,128,2048]{2,1,0:T(8,128)(2,1)}, u32[]{:S(2)}, u32[]{:S(2)}) collective-permute-start(bf16[3,128,2048]{2,1,0:T(8,128)(2,1)} %collective-permute-done.17.refs_11_), channel_id=1, source_target_pairs={{0,1},{1,0},{2,3},{3,2},{4,5},{5,4},{6,7},{7,6},{8,9},{9,8},{10,11... | collective-permute-start | bytes 4718600 | tf_op jit(solution)/shard_map/ppermute | solution.py:400
  203.4 51.6 %copy-start.16 = (bf16[512,512]{1,0:T(8,128)(2,1)}, bf16[512,512]{1,0:T(8,128)(2,1)S(1)}, u32[]{:S(2)}) copy-start(bf16[512,512]{1,0:T(8,128)(2,1)S(1)} %collective-permute-done.12) | copy-start | bytes 1572868
  203.4 16.4 %collective-permute-start.14 = (bf16[512,512]{1,0:T(8,128)(2,1)}, bf16[512,512]{1,0:T(8,128)(2,1)}, u32[]{:S(2)}, u32[]{:S(2)}) collective-permute-start(bf16[512,512]{1,0:T(8,128)(2,1)} %get-tuple-element.43), channel_id=1, source_target_pairs={{0,12},{4,8},{8,4},{12,0},{1,13},{5,9},{9,5},{13,1},{2,14},{6,10},... | collective-permute-start | bytes 1572872 | tf_op jit(solution)/shard_map/ppermute | solution.py:413
  219.8 35.1 %collective-permute-start.13 = (bf16[512,512]{1,0:T(8,128)(2,1)}, bf16[512,512]{1,0:T(8,128)(2,1)}, u32[]{:S(2)}, u32[]{:S(2)}) collective-permute-start(bf16[512,512]{1,0:T(8,128)(2,1)} %get-tuple-element.43), channel_id=1, source_target_pairs={{0,8},{4,12},{8,0},{12,4},{1,9},{5,13},{9,1},{13,5},{2,10},{6,14},... | collective-permute-start | bytes 1572872 | tf_op jit(solution)/shard_map/ppermute | solution.py:413
  (7 other events, 49.0 us)
